TPU v7x, 256 devices: a whole 4x4x8 slice. The times are simulated.
256 devices in a mesh: dp: 16 (over x, z_lo), ctx: 16 (over z_hi, y, core).
Axes of the slice: x: 4, y: 4, z: 8 (z_hi: 2, z_lo: 4; z = z_hi * 4 + z_lo), core: 2. Of those that a mesh axis runs over, the one named last changes fastest.
Arguments:
- stream: bfloat16 [16, 2048, 4096], P('dp', 'ctx'), may hold values from -6 to 6
- queries: bfloat16 [16, 2048, 2048], P('dp', 'ctx'), may hold values from -150 to 150
- keys: bfloat16 [16, 2048, 512], P('dp', 'ctx'), may hold values from -6 to 6
- values: bfloat16 [16, 2048, 512], P('dp', 'ctx'), may hold values from -6 to 6
- clip_lengths: int32 [16], P('dp'), may hold values from 1024 to 2048, as said below
- mod_shift: float32 [16, 4096], P('dp'), may hold values from -3 to 3
- mod_scale: float32 [16, 4096], P('dp'), may hold values from -0.5 to 0.5
- out_weight: bfloat16 [2048, 4096], P('ctx', 'dp'), may hold values from -4 to 4
- final_weight: bfloat16 [4096, 128], replicated, may hold values from -0.09375 to 0.09375
- noisy_latents: bfloat16 [16, 2048, 128], P('dp', 'ctx'), may hold values from -6 to 6
- timestep: int32 [16], P('dp'), may hold values from 100 to 599
- crop_map: int32 [16, 256], P('dp'), may hold values from 0 to 2047, as said below
- embed_weight: bfloat16 [128, 1408], replicated, may hold values from -0.5 to 0.5
- pre_gain: float32 [1408], replicated, may hold values from 0.1 to 1.9
- up_weight: bfloat16 [1408, 6144], P(None, 'ctx'), may hold values from -0.15625 to 0.15625
- down_weight: bfloat16 [6144, 1408], P('ctx'), may hold values from -0.21875 to 0.21875
- post_gain: float32 [1408], replicated, may hold values from 0.1 to 1.9
- head_weight: float32 [1408], replicated, may hold values from -4 to 4
Outputs:
- reward: float32 [16], P('dp')
- grad_stream: bfloat16 [16, 2048, 4096], P('dp', 'ctx')
- grad_queries: bfloat16 [16, 2048, 2048], P('dp', 'ctx')
Inputs may be any that keep to these rules, and one draw needn't show every extreme that they name: `clip_lengths`: each clip's length lies between 1024 and 2048; in every draw some clip has length exactly 2048. `crop_map`: every crop token of clip b points below clip_lengths[b].
All inputs are finite; a program needn't handle non-finite values.
Results may differ from a plain program's by a relative error of at most 0.04.
Values may be sent and summed in bfloat16 or wider, within the bound.
No kernel may reach another device: no remote copies, remote signals or barrier semaphores. Data moves between devices by JAX's collectives and lax.ppermute only.
A program may use at most 128 MiB of HBM per device.

v0:
```python
import math

import jax
import jax.numpy as jnp
from jax import lax
from jax.sharding import PartitionSpec as P

HEADS = 16
KV_HEADS = 4
HEAD = 128
PATCH = 128


MASKED = -1e30
LOSS_SCALE = 16.0
EPSILON = 1e-06


def sent_together(arrays, axis, dim, along):
    ends, at = ([], 0)
    for a in arrays[:-1]:
        at += a.shape[along]
        ends.append(at)
    both = jnp.concatenate(arrays, axis=along)
    return tuple(jnp.split(lax.all_gather(both, axis, axis=dim, tiled=True), ends, axis=along))


def laid_out(pieces, dim):
    shape = list(pieces.shape[1:])
    shape[dim] *= pieces.shape[0]
    return jnp.moveaxis(pieces, 0, dim).reshape(shape)


def copy_for_each(value, axis):
    copies = jnp.broadcast_to(value, (lax.axis_size(axis), *value.shape))
    return lax.all_to_all(copies, axis, split_axis=0, concat_axis=0, tiled=True)


def gather_directly(value, axis, dim):
    return laid_out(copy_for_each(value, axis), dim)


def in_blocks(value, dim, size):
    before, after = (value.shape[:dim], value.shape[dim + 1 :])
    return jnp.moveaxis(value.reshape(*before, size, -1, *after), dim, 0)


def sum_at_owner(value, axis, dim):
    pieces = in_blocks(value, dim, lax.axis_size(axis))
    arrived = lax.all_to_all(pieces, axis, split_axis=0, concat_axis=0, tiled=True)
    return arrived.astype(jnp.float32).sum(axis=0)


def taken_together(value, axis):
    everything = copy_for_each(value, axis)
    return jnp.sum(everything, axis=0)


def plan(noise_step):
    phase = (noise_step.astype(jnp.float32) / 1000.0 + 0.008) / 1.008 * (math.pi / 2.0)
    signal_root = jnp.cos(phase)
    return (signal_root, jnp.sqrt(1.0 - signal_root * signal_root))


def gelu_slope(hidden, upstream):
    return jax.vjp(lambda argument: jax.nn.gelu(argument, approximate=True), hidden)[1](upstream)[0]


def keep_state(current):
    return current


def sweep(folder, initial, whole_pair, tokens):
    all_rows = whole_pair[0].shape[0]
    block_rows = math.gcd(all_rows, max(tokens, 512))

    def sweep_advance(step_index, running):
        offset = step_index * block_rows
        pieces = tuple(
            (lax.dynamic_slice_in_dim(member, offset, block_rows, 0) for member in whole_pair)
        )
        return folder(running, pieces, offset)

    return lax.fori_loop(0, all_rows // block_rows, sweep_advance, initial)


def per_device(
    stream,
    queries,
    keys,
    values,
    clip_lengths,
    mod_shift,
    mod_scale,
    out_weight,
    final_weight,
    noisy_latents,
    timestep,
    crop_map,
    embed_weight,
    pre_gain,
    up_weight,
    down_weight,
    post_gain,
    head_weight,
):
    tokens = queries.shape[1]
    per_group = HEADS // KV_HEADS
    clip_length = clip_lengths[0]
    query_heads = queries[0].reshape(tokens, KV_HEADS, per_group, HEAD)

    def key_scores(key_piece, offset):
        row_count = key_piece.shape[0]
        scores = jnp.einsum(
            "tkgd,skd->kgts",
            query_heads,
            key_piece.reshape(row_count, KV_HEADS, HEAD),
            preferred_element_type=jnp.float32,
        ) / math.sqrt(HEAD)
        is_live = offset + jnp.arange(row_count, dtype=jnp.int32) < clip_length
        return jnp.where(is_live, scores, MASKED)

    def forward_fold(running, pieces, offset):
        key_piece, value_piece = pieces

        def forward_advance(current):
            highest, denominator, numerator = current
            row_count = key_piece.shape[0]
            scores = key_scores(key_piece, offset)
            new_highest = jnp.maximum(highest, jnp.max(scores, axis=-1))
            factor = jnp.exp(highest - new_highest)
            weights_rows = jnp.exp(scores - new_highest[..., None])
            blended = jnp.einsum(
                "kgts,skd->kgtd",
                weights_rows.astype(jnp.bfloat16),
                value_piece.reshape(row_count, KV_HEADS, HEAD),
                preferred_element_type=jnp.float32,
            )
            return (
                new_highest,
                denominator * factor + jnp.sum(weights_rows, axis=-1),
                numerator * factor[..., None] + blended,
            )

        return lax.cond(offset < clip_length, forward_advance, keep_state, running)

    shape_heads = (KV_HEADS, per_group, tokens)
    start_state = (
        jnp.full(shape_heads, -jnp.inf, jnp.float32),
        jnp.zeros(shape_heads, jnp.float32),
        jnp.zeros(shape_heads + (HEAD,), jnp.float32),
    )
    whole_pair = sent_together((keys[0], values[0]), "ctx", 0, 1)
    highest, denominator, numerator = sweep(forward_fold, start_state, whole_pair, tokens)
    attended = (
        jnp.transpose(numerator / denominator[..., None], (2, 0, 1, 3))
        .reshape(tokens, HEADS * HEAD)
        .astype(jnp.bfloat16)
    )
    log_total = highest + jnp.log(denominator)
    column_full = gather_directly(out_weight, "dp", 1)
    full_weight = lax.all_gather(column_full, "ctx", axis=0, tiled=True)
    residual = stream[0].astype(jnp.float32) + jnp.dot(
        attended, full_weight, preferred_element_type=jnp.float32
    )
    centred = residual - jnp.mean(residual, axis=-1, keepdims=True)
    inverse = lax.rsqrt(jnp.mean(centred * centred, axis=-1, keepdims=True) + EPSILON)
    unit_rows = centred * inverse
    gain_rows = 1.0 + mod_scale[0]
    modulated = (unit_rows * gain_rows + mod_shift[0]).astype(jnp.bfloat16)
    predicted = jnp.dot(modulated, final_weight, preferred_element_type=jnp.float32)
    signal_root, noise_root = plan(timestep[0])
    denoised = (
        (noisy_latents[0].astype(jnp.float32) - noise_root * predicted) / signal_root
    ).astype(jnp.bfloat16)
    gathered = gather_directly(denoised, "ctx", 0)
    crop_rows = crop_map[0]
    crop_tokens = jnp.take(gathered, crop_rows, axis=0)
    embedded = jnp.dot(crop_tokens, embed_weight, preferred_element_type=jnp.float32)
    first_root = jnp.sqrt(jnp.mean(embedded * embedded, axis=-1, keepdims=True) + EPSILON)
    first_unit = embedded / first_root
    normed = (first_unit * pre_gain).astype(jnp.bfloat16)
    hidden = jnp.dot(normed, up_weight, preferred_element_type=jnp.float32)
    active = jax.nn.gelu(hidden, approximate=True).astype(jnp.bfloat16)
    row_total = embedded.shape[0]
    head_slope = -(LOSS_SCALE / row_total) * head_weight * post_gain
    share = row_total // lax.axis_size("ctx")
    first_row = lax.axis_index("ctx") * share
    own_embedded = lax.dynamic_slice_in_dim(embedded, first_row, share, 0)
    own_root = lax.dynamic_slice_in_dim(first_root, first_row, share, 0)
    own_unit = lax.dynamic_slice_in_dim(first_unit, first_row, share, 0)
    summed = own_embedded + sum_at_owner(
        jnp.dot(active, down_weight, preferred_element_type=jnp.float32).astype(jnp.bfloat16),
        "ctx",
        0,
    )
    second_root = jnp.sqrt(jnp.mean(summed * summed, axis=-1, keepdims=True) + EPSILON)
    second_unit = summed / second_root
    reward = taken_together(jnp.sum(second_unit * post_gain * head_weight) / row_total, "ctx")
    summed_slope = (
        head_slope - second_unit * jnp.mean(head_slope * second_unit, axis=-1, keepdims=True)
    ) / second_root
    slope_all = lax.all_gather(summed_slope.astype(jnp.bfloat16), "ctx", axis=0, tiled=True)
    active_slope = jnp.einsum(
        "rw,hw->rh", slope_all, down_weight, preferred_element_type=jnp.float32
    )
    hidden_slope = gelu_slope(hidden, active_slope).astype(jnp.bfloat16)
    normed_slope = (
        sum_at_owner(
            jnp.einsum(
                "rh,wh->rw", hidden_slope, up_weight, preferred_element_type=jnp.float32
            ).astype(jnp.bfloat16),
            "ctx",
            0,
        )
        * pre_gain
    )
    embed_slope = (
        summed_slope
        + (normed_slope - own_unit * jnp.mean(normed_slope * own_unit, axis=-1, keepdims=True))
        / own_root
    )
    token_slope = jnp.einsum(
        "rw,pw->rp",
        embed_slope.astype(jnp.bfloat16),
        embed_weight,
        preferred_element_type=jnp.float32,
    )
    own_crops = lax.dynamic_slice_in_dim(crop_rows, first_row, share, 0)
    latent_part = jnp.zeros((gathered.shape[0], PATCH), jnp.float32).at[own_crops].add(token_slope)
    latent_slope = sum_at_owner(latent_part.astype(jnp.bfloat16), "ctx", 0)
    noise_slope = (-(noise_root / signal_root) * latent_slope).astype(jnp.bfloat16)
    modulated_slope = (
        jnp.einsum("tp,dp->td", noise_slope, final_weight, preferred_element_type=jnp.float32)
        * gain_rows
    )
    residual_slope = (
        modulated_slope
        - jnp.mean(modulated_slope, axis=-1, keepdims=True)
        - unit_rows * jnp.mean(modulated_slope * unit_rows, axis=-1, keepdims=True)
    ) * inverse
    grad_stream = residual_slope.astype(jnp.bfloat16)
    attended_slope = jnp.einsum(
        "td,hd->th", grad_stream, full_weight, preferred_element_type=jnp.float32
    ).astype(jnp.bfloat16)
    slope_heads = attended_slope.reshape(tokens, KV_HEADS, per_group, HEAD)
    row_delta = jnp.transpose(
        jnp.sum(
            slope_heads.astype(jnp.float32)
            * attended.reshape(tokens, KV_HEADS, per_group, HEAD).astype(jnp.float32),
            axis=-1,
        ),
        (1, 2, 0),
    )

    def backward_fold(running, pieces, offset):
        key_piece, value_piece = pieces

        def backward_advance(current):
            row_count = key_piece.shape[0]
            scores = key_scores(key_piece, offset)
            weights_rows = jnp.exp(scores - log_total[..., None])
            slopes = jnp.einsum(
                "tkgd,skd->kgts",
                slope_heads,
                value_piece.reshape(row_count, KV_HEADS, HEAD),
                preferred_element_type=jnp.float32,
            )
            score_slope = (weights_rows * (slopes - row_delta[..., None])).astype(jnp.bfloat16)
            return current + jnp.einsum(
                "kgts,skd->kgtd",
                score_slope,
                key_piece.reshape(row_count, KV_HEADS, HEAD),
                preferred_element_type=jnp.float32,
            )

        return lax.cond(offset < clip_length, backward_advance, keep_state, running)

    start_grad = jnp.zeros(shape_heads + (HEAD,), jnp.float32)
    query_slope = sweep(backward_fold, start_grad, whole_pair, tokens)
    grad_queries = (
        jnp.transpose(query_slope, (2, 0, 1, 3)).reshape(tokens, HEADS * HEAD) / math.sqrt(HEAD)
    ).astype(jnp.bfloat16)
    return (jnp.reshape(reward, (1,)), grad_stream[None], grad_queries[None])


def solution(mesh):
    return jax.shard_map(
        per_device,
        mesh=mesh,
        in_specs=(
            P("dp", "ctx", None),
            P("dp", "ctx", None),
            P("dp", "ctx", None),
            P("dp", "ctx", None),
            P("dp"),
            P("dp", None),
            P("dp", None),
            P("ctx", "dp"),
            P(),
            P("dp", "ctx", None),
            P("dp"),
            P("dp", None),
            P(),
            P(),
            P(None, "ctx"),
            P("ctx", None),
            P(),
            P(),
        ),
        out_specs=(P("dp"), P("dp", "ctx", None), P("dp", "ctx", None)),
        check_vma=False,
    )
```

profile of v0, /device:TPU:69, one launch (start us, length us, event | category | flops | bytes accessed | tf_op | source)
XLA Modules:
  0.0 509.4 jit_solution(1205504490812721230)
XLA Ops:
  11.3 36.4 %all_to_all.31 = bf16[16,128,256]{1,2,0:T(8,128)(2,1)} all-to-all(bf16[16,128,256]{1,2,0:T(8,128)(2,1)S(1)} %broadcast_in_dim.83), channel_id=1, replica_groups=mesh['dp'=16,'ctx'=16] {'dp'}, dimensions={0} | all-to-all | bytes 2097152 | tf_op jit(solution)/shard_map/all_to_all | solution.py:36
  49.1 42.8 %all-gather.3.cloned.1.call-done = bf16[2048,1024]{0,1:T(8,128)(2,1)} async-done(((bf16[128,1024]{0,1:T(8,128)(2,1)}), bf16[2048,1024]{0,1:T(8,128)(2,1)}) %all-gather.3.cloned.1.call-update) | async-done | bytes 4194320 | tf_op jit(solution)/shard_map/all_gather | solution.py:25
  91.9 4.8 fusion.76
  96.8 26.2 %while.33 = (s32[]{:T(128)}, f32[4,4,128]{2,1,0:T(4,128)S(1)}, f32[4,4,128]{2,1,0:T(4,128)S(1)}, f32[4,4,128,128]{3,2,1,0:T(8,128)S(1)}, s32[]{:T(128)}, /*index...) while((s32[]{:T(128)}, f32[4,4,128]{2,1,0:T(4,128)S(1)}, ...), condition=%wide.region_5.6_spmd, body=%wide.region_0.5_spmd.sunk | while | flops 548934656 | bytes 18483492 | solution.py:84
  97.5 5.8 %conditional.4 = ((f32[4,4,128]{2,1,0:T(4,128)S(1)}, f32[4,4,128]{2,1,0:T(4,128)S(1)}, f32[4,4,128,128]{3,2,1,0:T(8,128)S(1)})) conditional(s32[]{:T(128)} %convert_element_type.197, (f32[4,4,128]{2,1,0:T(4,128)S(1)}, f32[4,4,128]{2,1,0:T(4,128)S(1)}, f32[4,4,128,128]{3,2,1,0:T(8,128)S(1)}) %tuple.116, (s32[]{:T(128)}, s32[]{:T(128)}, ...), branch_computations={%region_1.0_spmd, %region_2.4_spmd} | conditional | flops 548934656 | bytes 18483278 | solution.py:145
  104.0 6.0 %conditional.4 = ((f32[4,4,128]{2,1,0:T(4,128)S(1)}, f32[4,4,128]{2,1,0:T(4,128)S(1)}, f32[4,4,128,128]{3,2,1,0:T(8,128)S(1)})) conditional(s32[]{:T(128)} %convert_element_type.197, (f32[4,4,128]{2,1,0:T(4,128)S(1)}, f32[4,4,128]{2,1,0:T(4,128)S(1)}, f32[4,4,128,128]{3,2,1,0:T(8,128)S(1)}) %tuple.116, (s32[]{:T(128)}, s32[]{:T(128)}, ...), branch_computations={%region_1.0_spmd, %region_2.4_spmd} | conditional | flops 548934656 | bytes 18483278 | solution.py:145
  110.6 5.8 %conditional.4 = ((f32[4,4,128]{2,1,0:T(4,128)S(1)}, f32[4,4,128]{2,1,0:T(4,128)S(1)}, f32[4,4,128,128]{3,2,1,0:T(8,128)S(1)})) conditional(s32[]{:T(128)} %convert_element_type.197, (f32[4,4,128]{2,1,0:T(4,128)S(1)}, f32[4,4,128]{2,1,0:T(4,128)S(1)}, f32[4,4,128,128]{3,2,1,0:T(8,128)S(1)}) %tuple.116, (s32[]{:T(128)}, s32[]{:T(128)}, ...), branch_computations={%region_1.0_spmd, %region_2.4_spmd} | conditional | flops 548934656 | bytes 18483278 | solution.py:145
  117.1 5.9 %conditional.4 = ((f32[4,4,128]{2,1,0:T(4,128)S(1)}, f32[4,4,128]{2,1,0:T(4,128)S(1)}, f32[4,4,128,128]{3,2,1,0:T(8,128)S(1)})) conditional(s32[]{:T(128)} %convert_element_type.197, (f32[4,4,128]{2,1,0:T(4,128)S(1)}, f32[4,4,128]{2,1,0:T(4,128)S(1)}, f32[4,4,128,128]{3,2,1,0:T(8,128)S(1)}) %tuple.116, (s32[]{:T(128)}, s32[]{:T(128)}, ...), branch_computations={%region_1.0_spmd, %region_2.4_spmd} | conditional | flops 548934656 | bytes 18483278 | solution.py:145
  125.7 149.0 %all-gather.5.cloned.1.call-done = bf16[2048,4096]{0,1:T(8,128)(2,1)} async-done(((bf16[128,4096]{0,1:T(8,128)(2,1)}), bf16[2048,4096]{0,1:T(8,128)(2,1)}) %all-gather.5.cloned.1.call-update) | async-done | bytes 16777232 | tf_op jit(solution)/shard_map/all_gather | solution.py:162
  274.7 12.9 %fusion.77 = (f32[128]{0:T(128)S(1)}, f32[128,4096]{1,0:T(8,128)}) fusion(bf16[128,2048]{0,1:T(8,128)(2,1)S(1)} %bitcast.133, bf16[2048,4096]{0,1:T(8,128)(2,1)} %all-gather.5.cloned.1.call-done, bf16[1,128,4096]{2,1,0:T(8,128)(2,1)} %param.26), kind=kOutput, calls=%fused_computation.138 | convolution fusion | flops 2149056512 | bytes 20447744 | tf_op jit(solution)/shard_map/dot_general | solution.py:163
  292.6 5.9 %all-to-all-start.1 = ((bf16[16,128,128]{2,1,0:T(8,128)(2,1)}), bf16[16,128,128]{2,1,0:T(8,128)(2,1)S(1)}, u32[]{:S(2)}, u32[]{:S(2)}) async-start(bf16[16,128,128]{2,1,0:T(8,128)(2,1)} %broadcast_in_dim.84), calls=%async_computation.1 | async-start | bytes 1048576 | tf_op jit(solution)/shard_map/all_to_all | solution.py:36
  298.5 19.1 %all-to-all-done.1 = bf16[16,128,128]{2,1,0:T(8,128)(2,1)S(1)} async-done(((bf16[16,128,128]{2,1,0:T(8,128)(2,1)}), bf16[16,128,128]{2,1,0:T(8,128)(2,1)S(1)}, u32[]{:S(2)}, u32[]{:S(2)}) %all-to-all-start.1) | async-done | bytes 524320 | tf_op jit(solution)/shard_map/all_to_all | solution.py:36
  327.3 20.7 %all-to-all-done.2 = bf16[16,16,1408]{2,1,0:T(8,128)(2,1)S(1)} async-done(((bf16[16,16,1408]{2,1,0:T(8,128)(2,1)}), bf16[16,16,1408]{2,1,0:T(8,128)(2,1)S(1)}, u32[]{:S(2)}, u32[]{:S(2)}) %all-to-all-start.2) | async-done | bytes 720928 | tf_op jit(solution)/shard_map/all_to_all | solution.py:50
  350.8 27.4 %all_gather.11 = bf16[256,1408]{1,0:T(8,128)(2,1)S(1)} all-gather(bf16[16,1408]{1,0:T(8,128)(2,1)S(1)} %fusion.74), channel_id=1, replica_groups=mesh['dp'=16,'ctx'=16] {'ctx'}, dimensions={0}, use_global_device_ids=true | all-gather | bytes 765952 | tf_op jit(solution)/shard_map/all_gather | solution.py:203
  381.7 7.0 %all-to-all-start.4 = ((bf16[16,16,1408]{2,1,0:T(8,128)(2,1)}), bf16[16,16,1408]{2,1,0:T(8,128)(2,1)S(1)}, u32[]{:S(2)}, u32[]{:S(2)}) async-start(bf16[16,16,1408]{2,1,0:T(8,128)(2,1)} %bitcast.33), calls=%async_computation.4 | async-start | bytes 1441792 | tf_op jit(solution)/shard_map/all_to_all | solution.py:50
  389.5 18.9 %all-to-all-done.4 = bf16[16,16,1408]{2,1,0:T(8,128)(2,1)S(1)} async-done(((bf16[16,16,1408]{2,1,0:T(8,128)(2,1)}), bf16[16,16,1408]{2,1,0:T(8,128)(2,1)S(1)}, u32[]{:S(2)}, u32[]{:S(2)}) %all-to-all-start.4) | async-done | bytes 720928 | tf_op jit(solution)/shard_map/all_to_all | solution.py:50
  416.7 5.4 %all-to-all-done.3 = f32[16,1,1]{2,1,0:T(1,128)S(1)} async-done(((f32[16,1,1]{2,1,0:T(1,128)}), f32[16,1,1]{2,1,0:T(1,128)S(1)}, u32[]{:S(2)}, u32[]{:S(2)}) %all-to-all-start.3) | async-done | bytes 96 | tf_op jit(solution)/shard_map/all_to_all | solution.py:36
  427.1 17.3 %all-to-all-done.5 = bf16[16,128,128]{2,1,0:T(8,128)(2,1)S(1)} async-done(((bf16[16,128,128]{2,1,0:T(8,128)(2,1)}), bf16[16,128,128]{2,1,0:T(8,128)(2,1)S(1)}, u32[]{:S(2)}, u32[]{:S(2)}) %all-to-all-start.5) | async-done | bytes 524320 | tf_op jit(solution)/shard_map/all_to_all | solution.py:50
  448.0 9.3 %convolution_convert_fusion.2 = bf16[128,2048]{1,0:T(8,128)(2,1)} fusion(bf16[128,4096]{1,0:T(8,128)(2,1)S(1)} %multiply_convert_fusion, bf16[2048,4096]{0,1:T(8,128)(2,1)} %all-gather.5.cloned.1.call-done), kind=kOutput, calls=%fused_computation.37 | convolution fusion | flops 2147745792 | bytes 18350080 | tf_op jit(solution)/shard_map/td,hd->th/dot_general | solution.py:243
  461.1 39.7 %while.34 = (s32[]{:T(128)}, f32[4,4,128,128]{3,2,1,0:T(8,128)S(1)}, s32[]{:T(128)}, bf16[2048,512]{0,1:T(8,128)(2,1)}, bf16[128,4,4,128]{3,0,2,1:T(8,128)(2,1)S...) while((s32[]{:T(128)}, ...), condition=%wide.region_24.25_spmd, body=%wide.region_21.24_spmd.sunk | while | flops 811860992 | bytes 15222021 | solution.py:84
  461.8 9.2 %conditional.5 = (f32[4,4,128,128]{3,2,1,0:T(8,128)S(1)}) conditional(s32[]{:T(128)} %convert_element_type.198, f32[4,4,128,128]{3,2,1,0:T(8,128)S(1)} %get-tuple-element.839, (s32[]{:T(128)}, s32[]{:T(128)}, bf16[2048,512]{0,1:T(8,128)(2,1)}, bf16[128,4,4,128]{3,0,2,1:T(8,128)(2,1)S(1)}, f32[4,4,128]{2,1,0:T(4,128)S(1)}, ...), branch_computations={%region_22.22_spmd, %region_23.23_spmd} | conditional | flops 811860992 | bytes 15221814 | solution.py:277
  471.7 9.3 %conditional.5 = (f32[4,4,128,128]{3,2,1,0:T(8,128)S(1)}) conditional(s32[]{:T(128)} %convert_element_type.198, f32[4,4,128,128]{3,2,1,0:T(8,128)S(1)} %get-tuple-element.839, (s32[]{:T(128)}, s32[]{:T(128)}, bf16[2048,512]{0,1:T(8,128)(2,1)}, bf16[128,4,4,128]{3,0,2,1:T(8,128)(2,1)S(1)}, f32[4,4,128]{2,1,0:T(4,128)S(1)}, ...), branch_computations={%region_22.22_spmd, %region_23.23_spmd} | conditional | flops 811860992 | bytes 15221814 | solution.py:277
  481.6 9.3 %conditional.5 = (f32[4,4,128,128]{3,2,1,0:T(8,128)S(1)}) conditional(s32[]{:T(128)} %convert_element_type.198, f32[4,4,128,128]{3,2,1,0:T(8,128)S(1)} %get-tuple-element.839, (s32[]{:T(128)}, s32[]{:T(128)}, bf16[2048,512]{0,1:T(8,128)(2,1)}, bf16[128,4,4,128]{3,0,2,1:T(8,128)(2,1)S(1)}, f32[4,4,128]{2,1,0:T(4,128)S(1)}, ...), branch_computations={%region_22.22_spmd, %region_23.23_spmd} | conditional | flops 811860992 | bytes 15221814 | solution.py:277
  491.6 9.3 %conditional.5 = (f32[4,4,128,128]{3,2,1,0:T(8,128)S(1)}) conditional(s32[]{:T(128)} %convert_element_type.198, f32[4,4,128,128]{3,2,1,0:T(8,128)S(1)} %get-tuple-element.839, (s32[]{:T(128)}, s32[]{:T(128)}, bf16[2048,512]{0,1:T(8,128)(2,1)}, bf16[128,4,4,128]{3,0,2,1:T(8,128)(2,1)S(1)}, f32[4,4,128]{2,1,0:T(4,128)S(1)}, ...), branch_computations={%region_22.22_spmd, %region_23.23_spmd} | conditional | flops 811860992 | bytes 15221814 | solution.py:277
  (153 shorter events, 111.0 us)
Async XLA Ops:
  7.2 314.0 %copy-start = (bf16[384,1408]{1,0:T(8,128)(2,1)S(1)}, bf16[384,1408]{1,0:T(8,128)(2,1)}, u32[]{:S(2)}) copy-start(bf16[384,1408]{1,0:T(8,128)(2,1)} %param.41) | copy-start | bytes 3244036
  7.2 84.8 %all-gather.3.cloned.1.call-start = ((), (), s32[]{:S(2)}) async-start(), calls=%async_computation.6 | async-start | bytes 4456448 | tf_op jit(solution)/shard_map/all_gather | solution.py:25
  10.1 264.6 %all-gather.5.cloned.1.call-start = ((), (), s32[]{:S(2)}) async-start(), calls=%async_computation.7 | async-start | bytes 17825792 | tf_op jit(solution)/shard_map/all_gather | solution.py:162
  11.1 36.6 %copy-start.9 = (bf16[1,128,2048]{2,1,0:T(8,128)(2,1)S(1)}, bf16[1,128,2048]{2,1,0:T(8,128)(2,1)}, u32[]{:S(2)}) copy-start(bf16[1,128,2048]{2,1,0:T(8,128)(2,1)} %param.27) | copy-start | bytes 1572868
  47.7 1.4 copy-start.16
  274.7 15.0 %copy-start.18 = (bf16[1,128,128]{2,1,0:T(8,128)(2,1)S(1)}, bf16[1,128,128]{2,1,0:T(8,128)(2,1)}, u32[]{:S(2)}) copy-start(bf16[1,128,128]{2,1,0:T(8,128)(2,1)} %param.35) | copy-start | bytes 98308
  274.7 15.0 %copy-start.19 = (f32[1,4096]{1,0:T(1,128)S(1)}, f32[1,4096]{1,0:T(1,128)}, u32[]{:S(2)}) copy-start(f32[1,4096]{1,0:T(1,128)} %param.31) | copy-start | bytes 49156
  287.6 2.2 copy-start.2
  289.8 8.6 %copy-start.17 = (s32[1,256]{1,0:T(1,128)S(1)}, s32[1,256]{1,0:T(1,128)}, u32[]{:S(2)}) copy-start(s32[1,256]{1,0:T(1,128)} %param.37) | copy-start | bytes 3076
  292.6 25.0 %all-to-all-start.1 = ((bf16[16,128,128]{2,1,0:T(8,128)(2,1)}), bf16[16,128,128]{2,1,0:T(8,128)(2,1)S(1)}, u32[]{:S(2)}, u32[]{:S(2)}) async-start(bf16[16,128,128]{2,1,0:T(8,128)(2,1)} %broadcast_in_dim.84), calls=%async_computation.1 | async-start | bytes 1048576 | tf_op jit(solution)/shard_map/all_to_all | solution.py:36
  318.5 1.8 copy-start.8
  318.5 1.8 copy-start.13
  320.3 2.3 copy-start.5
  321.2 1.4 copy-start.11
  321.2 6.1 %copy-start.14 = (f32[1408]{0:T(1024)S(1)}, f32[1408]{0:T(1024)}, u32[]{:S(2)}) copy-start(f32[1408]{0:T(1024)} %param.42) | copy-start | bytes 16900
  321.2 6.1 %copy-start.15 = (f32[1408]{0:T(1024)S(1)}, f32[1408]{0:T(1024)}, u32[]{:S(2)}) copy-start(f32[1408]{0:T(1024)} %param.43) | copy-start | bytes 16900
  322.6 25.4 %all-to-all-start.2 = ((bf16[16,16,1408]{2,1,0:T(8,128)(2,1)}), bf16[16,16,1408]{2,1,0:T(8,128)(2,1)S(1)}, u32[]{:S(2)}, u32[]{:S(2)}) async-start(bf16[16,16,1408]{2,1,0:T(8,128)(2,1)} %bitcast.139), calls=%async_computation.2 | async-start | bytes 1441792 | tf_op jit(solution)/shard_map/all_to_all | solution.py:50
  381.7 32.2 %copy-start.12 = (bf16[128,1408]{1,0:T(8,128)(2,1)S(1)}, bf16[128,1408]{1,0:T(8,128)(2,1)}, u32[]{:S(2)}) copy-start(bf16[128,1408]{1,0:T(8,128)(2,1)} %param.38) | copy-start | bytes 1081348
  381.7 26.7 %all-to-all-start.4 = ((bf16[16,16,1408]{2,1,0:T(8,128)(2,1)}), bf16[16,16,1408]{2,1,0:T(8,128)(2,1)S(1)}, u32[]{:S(2)}, u32[]{:S(2)}) async-start(bf16[16,16,1408]{2,1,0:T(8,128)(2,1)} %bitcast.33), calls=%async_computation.4 | async-start | bytes 1441792 | tf_op jit(solution)/shard_map/all_to_all | solution.py:50
  409.0 13.1 %all-to-all-start.3 = ((f32[16,1,1]{2,1,0:T(1,128)}), f32[16,1,1]{2,1,0:T(1,128)S(1)}, u32[]{:S(2)}, u32[]{:S(2)}) async-start(f32[16,1,1]{2,1,0:T(1,128)} %broadcast_in_dim.86), calls=%async_computation.3 | async-start | bytes 16384 | tf_op jit(solution)/shard_map/all_to_all | solution.py:36
  422.1 22.3 %all-to-all-start.5 = ((bf16[16,128,128]{2,1,0:T(8,128)(2,1)}), bf16[16,128,128]{2,1,0:T(8,128)(2,1)S(1)}, u32[]{:S(2)}, u32[]{:S(2)}) async-start(bf16[16,128,128]{2,1,0:T(8,128)(2,1)} %bitcast.34), calls=%async_computation.5 | async-start | bytes 1048576 | tf_op jit(solution)/shard_map/all_to_all | solution.py:50
  444.5 2.8 copy-start.3
  448.0 9.3 %copy-start.6 = (bf16[128,4096]{1,0:T(8,128)(2,1)}, bf16[128,4096]{1,0:T(8,128)(2,1)S(1)}, u32[]{:S(2)}) copy-start(bf16[128,4096]{1,0:T(8,128)(2,1)S(1)} %multiply_convert_fusion) | copy-start | bytes 3145732
  500.8 1.8 copy-start.1
  (3 other events, 3.1 us)
Sparse Core Ops, SparseCore 0:
  11.1 80.7 all-gather.2
  94.5 180.1 all-gather.4
where the time goes:
time: 511 us; the launch traced here: 509 us
  waiting for transfers between devices  273 us (53%)
  matrix products  75.6 us (15%)
  blocking collectives  63.8 us (12%)
  local copies, waits for them, and re-layouts  29.7 us (6%)
  starting transfers between devices  25.7 us (5%)
  other arithmetic  19.7 us (4%)
  between operations  15.9 us (3%)
  loops' own time  5.78 us (1%)
    all_gather x1, waiting for transfers between devices, per_device(): full_weight = lax.all_gather(column_full, 'ctx', axis=0, tiled=True)  149 us
    all_to_all x3, waiting for transfers between devices, sum_at_owner(): lax.all_to_all(pieces, axis, split_axis=0, concat_axis=0, tiled=True)  56.9 us
    all_gather x1, waiting for transfers between devices, sent_together(): lax.all_gather(both, axis, axis=dim, tiled=True)  42.8 us
    all_to_all x1, blocking collectives, copy_for_each(): return lax.all_to_all(copies, axis, split_axis=0, concat_axis=0, tiled=True)  36.4 us
    all_gather x1, blocking collectives, per_device(): lax.all_gather(summed_slope.astype(jnp.bfloat16), 'ctx', axis=0, tiled=True)  27.4 us
    all_to_all x2, waiting for transfers between devices, copy_for_each(): return lax.all_to_all(copies, axis, split_axis=0, concat_axis=0, tiled=True)  24.5 us
    dot_general x4, matrix products, backward_advance(): jnp.einsum('kgts,skd->kgtd', score_slope, key_piece.reshape(row_count, KV...  18.3 us
    all_to_all x3, starting transfers between devices, sum_at_owner(): lax.all_to_all(pieces, axis, split_axis=0, concat_axis=0, tiled=True)  16 us
  transfers between devices with their start and end apart: 7, of which 7 were waited for; matrix products, arithmetic and copies ran while one was open for 7% of the time, Pallas kernels for 0%

commit v1 on v0

v1 whole, which is shorter than its diff:
```python
import math

import jax
import jax.numpy as jnp
from jax import lax
from jax.sharding import Mesh, PartitionSpec as P

HEADS = 16
KV_HEADS = 4
HEAD = 128
PATCH = 128
CHIPS = 8

MASKED = -1e30
LOSS_SCALE = 16.0
EPSILON = 1e-06

F32 = jnp.float32
BF16 = jnp.bfloat16
CHIP = ("zh", "y")


def dot(a, b, dims):
    return lax.dot_general(a, b, (dims, ((), ())), preferred_element_type=F32)


def mm(a, b):
    return dot(a, b, ((1,), (0,)))


def mt(a, b):
    return dot(a, b, ((1,), (1,)))


def exchange(pieces, axis):
    return lax.all_to_all(pieces, axis, split_axis=0, concat_axis=0, tiled=True)


def copies(value, axis):
    size = lax.axis_size(axis)
    return exchange(jnp.broadcast_to(value, (size, *value.shape)), axis)


def swap(value, axis="core"):
    return lax.ppermute(value, axis, [(0, 1), (1, 0)])


def ring_blocks(value, axis):
    size = lax.axis_size(axis)
    blocks = [value]
    for step in range(1, size):
        blocks.append(lax.ppermute(value, axis, [((i + step) % size, i) for i in range(size)]))
    return blocks


def in_order(blocks, axis):
    size = len(blocks)
    if size == 1:
        return jnp.stack(blocks)
    twice = jnp.stack(blocks + blocks)
    start = lax.rem(size - lax.axis_index(axis), size)
    return lax.dynamic_slice_in_dim(twice, start, size, 0)


def plan(noise_step):
    phase = (noise_step.astype(F32) / 1000.0 + 0.008) / 1.008 * (math.pi / 2.0)
    signal_root = jnp.cos(phase)
    return (signal_root, jnp.sqrt(1.0 - signal_root * signal_root))


def gelu_slope(hidden, upstream):
    return jax.vjp(lambda argument: jax.nn.gelu(argument, approximate=True), hidden)[1](upstream)[0]


def split3(value):
    first = value.astype(BF16)
    rest = value - first.astype(F32)
    second = rest.astype(BF16)
    third = (rest - second.astype(F32)).astype(BF16)
    return first, second, third


def per_device(
    stream,
    queries,
    keys,
    values,
    clip_lengths,
    mod_shift,
    mod_scale,
    out_weight,
    final_weight,
    noisy_latents,
    timestep,
    crop_map,
    embed_weight,
    pre_gain,
    up_weight,
    down_weight,
    post_gain,
    head_weight,
):
    tokens = queries.shape[1]
    width = stream.shape[2]
    crop = crop_map[0]
    rows = crop.shape[0]
    half = rows // 2
    share = half // CHIPS
    core = lax.axis_index("core")
    zh = lax.axis_index("zh")
    y = lax.axis_index("y")
    chip = zh * 4 + y
    is_first = core == 0

    by_zl = in_order(ring_blocks(out_weight, "zl"), "zl")
    by_dp = in_order(ring_blocks(by_zl, "x"), "x")
    own_weight = jnp.transpose(by_dp.reshape(-1, *out_weight.shape), (1, 0, 2)).reshape(
        out_weight.shape[0], width
    )
    chip_weight = jnp.concatenate([own_weight, swap(own_weight)], axis=0)
    chip_stream = jnp.concatenate([stream[0], swap(stream[0])], axis=0)
    chip_noisy = jnp.concatenate([noisy_latents[0], swap(noisy_latents[0])], axis=0)
    up_pair = jnp.concatenate([up_weight, swap(up_weight)], axis=1)
    down_pair = jnp.concatenate([down_weight, swap(down_weight)], axis=0)

    query_pairs = queries[0].reshape(tokens, CHIPS, 2, HEAD)
    query_pairs = jnp.where(is_first, query_pairs, query_pairs[:, :, ::-1])
    query_pairs = jnp.transpose(query_pairs.reshape(tokens, CHIPS, 2 * HEAD), (1, 0, 2))

    def for_chips(side):
        heads = jnp.transpose(side.reshape(tokens, KV_HEADS, HEAD), (1, 0, 2))
        return jnp.repeat(heads, CHIPS // KV_HEADS, axis=0)

    sent = jnp.concatenate([query_pairs, for_chips(keys[0]), for_chips(values[0])], axis=2)
    mine = exchange(sent, CHIP).reshape(CHIPS * tokens, 4 * HEAD)
    other = swap(mine[:, HEAD:])
    query_side = jnp.concatenate([mine[:, :HEAD], other[:, :HEAD]], axis=0)
    key_side = jnp.concatenate([mine[:, 2 * HEAD : 3 * HEAD], other[:, HEAD : 2 * HEAD]], axis=0)
    value_side = jnp.concatenate([mine[:, 3 * HEAD :], other[:, 2 * HEAD :]], axis=0)

    place = jnp.arange(2 * CHIPS * tokens, dtype=jnp.int32)
    place_core = jnp.where(place < CHIPS * tokens, core, 1 - core)
    place_rest = place % (CHIPS * tokens)
    token_at = (place_rest // tokens) * (2 * tokens) + place_core * tokens + place_rest % tokens
    crop_core = (crop // tokens) % 2
    crop_at = (
        jnp.where(crop_core == core, 0, CHIPS * tokens)
        + (crop // (2 * tokens)) * tokens
        + crop % tokens
    )
    query_rows = jnp.take(query_side, crop_at, axis=0, mode="clip")

    scores = mt(query_rows, key_side) * (1.0 / math.sqrt(HEAD))
    scores = jnp.where(token_at < clip_lengths[0], scores, MASKED)
    highest = jnp.max(scores, axis=-1, keepdims=True)
    weights = jnp.exp(scores - highest)
    denominator = jnp.sum(weights, axis=-1, keepdims=True)
    weights = weights.astype(BF16)
    attended = (mm(weights, value_side) / denominator).astype(BF16)

    kept = lax.dynamic_slice_in_dim(attended, core * half, half, 0)
    given = lax.dynamic_slice_in_dim(attended, (1 - core) * half, half, 0)
    attended_pair = jnp.concatenate([kept, swap(given)], axis=1)
    crop_half = lax.dynamic_slice_in_dim(crop, core * half, half, 0)
    pair_place = jnp.arange(2 * tokens, dtype=jnp.int32)
    pair_token = chip * (2 * tokens) + jnp.where(
        pair_place < tokens, core * tokens + pair_place, (1 - core) * tokens + pair_place - tokens
    )
    pick = (crop_half[:, None] == pair_token[None, :]).astype(BF16)
    partial = mm(attended_pair, chip_weight) + mm(pick, chip_stream)
    partial = jnp.concatenate([partial, mm(pick, chip_noisy)], axis=1).astype(BF16)
    arrived = exchange(partial.reshape(CHIPS, share, width + PATCH), CHIP)
    arrived = arrived.astype(F32).sum(axis=0)
    residual = arrived[:, :width]
    noisy = arrived[:, width:]

    centred = residual - jnp.mean(residual, axis=-1, keepdims=True)
    inverse = lax.rsqrt(jnp.mean(centred * centred, axis=-1, keepdims=True) + EPSILON)
    unit_rows = centred * inverse
    gain_rows = 1.0 + mod_scale[0]
    modulated = (unit_rows * gain_rows + mod_shift[0]).astype(BF16)
    predicted = mm(modulated, final_weight)
    signal_root, noise_root = plan(timestep[0])
    denoised = ((noisy - noise_root * predicted) / signal_root).astype(BF16)
    crop_tokens = copies(denoised, CHIP).reshape(half, PATCH)

    inverse_parts = jnp.concatenate(
        list(split3(inverse)) + [jnp.zeros((share, 125), BF16)], axis=1
    )
    unit_own = jnp.concatenate([unit_rows.astype(BF16), inverse_parts], axis=1)
    unit_pair = jnp.concatenate([unit_own, swap(unit_own, "zh")], axis=0)
    unit_half = jnp.concatenate(ring_blocks(unit_pair, "y"), axis=0)
    unit_all = jnp.concatenate([unit_half, swap(unit_half)], axis=0)
    spot = jnp.arange(rows, dtype=jnp.int32)
    spot_rest = spot % half
    spot_y = (y + spot_rest // (2 * share)) % 4
    spot_zh = jnp.where((spot_rest // share) % 2 == 0, zh, 1 - zh)
    spot_row = (
        jnp.where(spot < half, core, 1 - core) * half
        + (spot_zh * 4 + spot_y) * share
        + spot_rest % share
    )

    embedded = mm(crop_tokens, embed_weight)
    first_root = jnp.sqrt(jnp.mean(embedded * embedded, axis=-1, keepdims=True) + EPSILON)
    first_unit = embedded / first_root
    normed = (first_unit * pre_gain).astype(BF16)
    hidden = mm(normed, up_pair)
    active = jax.nn.gelu(hidden, approximate=True).astype(BF16)
    head_slope = -(LOSS_SCALE / rows) * head_weight * post_gain
    added = exchange(mm(active, down_pair).astype(BF16).reshape(CHIPS, share, -1), CHIP)
    summed = lax.dynamic_slice_in_dim(embedded, chip * share, share, 0) + added.astype(F32).sum(
        axis=0
    )
    second_root = jnp.sqrt(jnp.mean(summed * summed, axis=-1, keepdims=True) + EPSILON)
    second_unit = summed / second_root
    reward_part = jnp.sum(second_unit * post_gain * head_weight) / rows
    summed_slope = (
        head_slope - second_unit * jnp.mean(head_slope * second_unit, axis=-1, keepdims=True)
    ) / second_root
    slope_half = copies(summed_slope.astype(BF16), CHIP).reshape(half, -1)
    active_slope = mt(slope_half, down_pair)
    hidden_slope32 = gelu_slope(hidden, active_slope)
    hidden_slope = hidden_slope32.astype(BF16)
    gained_embed = (embed_weight.astype(F32) * pre_gain).astype(BF16)
    hidden_embed = mm(gained_embed, up_pair).astype(BF16)
    along = jnp.sum(hidden_slope32 * hidden, axis=-1, keepdims=True) / embedded.shape[1]
    unit_embed = mt(first_unit.astype(BF16), embed_weight)
    part = (mt(hidden_slope, hidden_embed) - along * unit_embed) / first_root
    reward_lanes = jnp.concatenate(
        [jnp.broadcast_to(piece.reshape(1, 1), (16, PATCH)) for piece in split3(reward_part)], axis=0
    )
    parts = copies(jnp.concatenate([part.astype(BF16), reward_lanes], axis=0), CHIP)
    parts = parts.astype(F32).sum(axis=0)
    token_half = parts[:half] + mt(slope_half, embed_weight)
    reward_half = parts[half : half + 8] + parts[half + 16 : half + 24] + parts[half + 32 : half + 40]
    both = jnp.concatenate([token_half, reward_half], axis=0)
    back = swap(both)
    reward = (both + back)[half, 0]
    token_slope = jnp.concatenate(
        [
            jnp.where(is_first, token_half, back[:half]),
            jnp.where(is_first, back[:half], token_half),
        ],
        axis=0,
    )
    same = crop[:, None] == crop[None, :]
    latent_slope = mm(same.astype(BF16), token_slope.astype(BF16))
    noise_slope = (-(noise_root / signal_root) * latent_slope).astype(BF16)

    gained = final_weight.astype(F32) * gain_rows[:, None]
    gained16 = gained.astype(BF16)
    weight_latent = mm(own_weight, gained16)
    weight_sum = jnp.sum(own_weight.astype(F32), axis=1)
    units = unit_all[:, :width]
    by_spot = jnp.concatenate(
        [
            mt(units, own_weight),
            mm(units, gained16) / width,
            unit_all[:, width:].astype(F32),
        ],
        axis=1,
    )
    canon = jnp.take(by_spot, jnp.zeros((rows,), jnp.int32).at[spot_row].set(spot), axis=0, mode="clip")
    unit_weight = canon[:, :HEAD]
    unit_latent = canon[:, HEAD : HEAD + PATCH]
    row_inverse = jnp.sum(canon[:, HEAD + PATCH :], axis=-1, keepdims=True)
    noise32 = noise_slope.astype(F32)
    row_mean = jnp.sum(noise32 * jnp.mean(gained, axis=0), axis=-1, keepdims=True)
    row_along = jnp.sum(noise32 * unit_latent, axis=-1, keepdims=True)
    attended_slope = (
        (mt(noise_slope, weight_latent.astype(BF16)) - row_mean * weight_sum - row_along * unit_weight)
        * row_inverse
    ).astype(BF16)
    row_delta = jnp.sum(attended_slope.astype(F32) * attended.astype(F32), axis=-1, keepdims=True)
    slopes = mt(attended_slope, value_side)
    score_slope = (weights.astype(F32) * ((slopes - row_delta) / denominator)).astype(BF16)
    query_slope = (mm(score_slope, key_side) * (1.0 / math.sqrt(HEAD))).astype(BF16)

    earlier = same & (jnp.arange(rows)[None, :] < jnp.arange(rows)[:, None])
    first_seen = jnp.logical_not(jnp.any(earlier, axis=1))
    label = jnp.where(first_seen, crop, -1)
    query_other = swap(query_slope)
    query_pair = jnp.concatenate(
        [
            jnp.where(is_first, query_slope, query_other),
            jnp.where(is_first, query_other, query_slope),
        ],
        axis=1,
    )
    spread = (token_at[: CHIPS * tokens, None] == label[None, :]).astype(BF16)
    spread_rows = mm(spread, query_pair).astype(BF16)
    home = exchange(spread_rows.reshape(CHIPS, tokens, 2 * HEAD), CHIP)
    grad_queries = jnp.transpose(home, (1, 0, 2)).reshape(tokens, HEADS * HEAD)

    own_token = (chip * 2 + core) * tokens + jnp.arange(tokens, dtype=jnp.int32)
    spot_label = jnp.sum(
        jnp.where(spot_row[:, None] == jnp.arange(rows, dtype=jnp.int32)[None, :], label[None, :], 0),
        axis=1,
    )
    own_spots = (own_token[:, None] == spot_label[None, :]).astype(BF16)
    own_units = mm(own_spots, unit_all)
    own_inverse = jnp.sum(own_units[:, width:], axis=-1, keepdims=True)
    own_units = own_units[:, :width]
    own_rows = (own_token[:, None] == label[None, :]).astype(BF16)
    own_noise = mm(own_rows, noise_slope).astype(BF16)
    modulated_slope = mt(own_noise, final_weight) * gain_rows
    grad_stream = (
        (
            modulated_slope
            - jnp.mean(modulated_slope, axis=-1, keepdims=True)
            - own_units * jnp.mean(modulated_slope * own_units, axis=-1, keepdims=True)
        )
        * own_inverse
    ).astype(BF16)
    return (jnp.reshape(reward, (1,)), grad_stream[None], grad_queries[None])


DP = ("x", "zl")
CTX = ("zh", "y", "core")


def solution(mesh):
    across = mesh.shape["dp"]
    near = min(4, across)
    fine = Mesh(
        mesh.devices.reshape(across // near, near, 2, 4, 2), ("x", "zl", "zh", "y", "core")
    )
    return jax.shard_map(
        per_device,
        mesh=fine,
        in_specs=(
            P(DP, CTX, None),
            P(DP, CTX, None),
            P(DP, CTX, None),
            P(DP, CTX, None),
            P(DP),
            P(DP, None),
            P(DP, None),
            P(CTX, DP),
            P(),
            P(DP, CTX, None),
            P(DP),
            P(DP, None),
            P(),
            P(),
            P(None, CTX),
            P(CTX, None),
            P(),
            P(),
        ),
        out_specs=(P(DP), P(DP, CTX, None), P(DP, CTX, None)),
        check_vma=False,
    )
```

time: 511 us -> 252 us (0.49)
  the two profiles are of different devices: /device:TPU:69 before, /device:TPU:32 now
where the time goes in v1:
time: 252 us; the launch traced here: 250 us
  starting transfers between devices  69.4 us (28%)
  waiting for transfers between devices  68.9 us (27%)
  local copies, waits for them, and re-layouts  48.2 us (19%)
  matrix products  37.2 us (15%)
  other arithmetic  19.9 us (8%)
  between operations  6.19 us (2%)
    all_to_all x7, starting transfers between devices, exchange(): return lax.all_to_all(pieces, axis, split_axis=0, concat_axis=0, tiled=True)  46 us
    all_to_all x7, waiting for transfers between devices, exchange(): return lax.all_to_all(pieces, axis, split_axis=0, concat_axis=0, tiled=True)  41.7 us
    dot_general x21, matrix products, dot(): return lax.dot_general(a, b, (dims, ((), ())), preferred_element_type=F32)  37.2 us
    ppermute x9, waiting for transfers between devices, ring_blocks(): lax.ppermute(value, axis, [((i + step) % size, i) for i in range(size)])  27.1 us
    unnamed x132, local copies, waits for them, and re-layouts  16.3 us
    ppermute x9, starting transfers between devices, ring_blocks(): lax.ppermute(value, axis, [((i + step) % size, i) for i in range(size)])  14.7 us
    ppermute x11, starting transfers between devices, swap(): return lax.ppermute(value, axis, [(0, 1), (1, 0)])  8.69 us
  transfers between devices with their start and end apart: 27, of which 8 were waited for; matrix products, arithmetic and copies ran while one was open for 34% of the time, Pallas kernels for 0%

profile of v1, /device:TPU:32, one launch (start us, length us, event | category | flops | bytes accessed | tf_op | source)
XLA Modules:
  0.0 249.8 jit_solution(13998783542247472940)
XLA Ops:
  4.1 2.8 %collective-permute-start.4 = (bf16[128,256]{1,0:T(8,128)(2,1)}, bf16[128,256]{1,0:T(8,128)(2,1)S(1)}, u32[]{:S(2)}, u32[]{:S(2)}) collective-permute-start(bf16[128,256]{1,0:T(8,128)(2,1)} %param.25), channel_id=1, source_target_pairs={{48,0},{0,16},{16,32},{32,48},{49,1},{1,17},{17,33},{33,49},{50,2}... | collective-permute-start | bytes 196616 | tf_op jit(solution)/shard_map/ppermute | solution.py:52
  8.3 2.7 %rev.3 = bf16[128,8,2,128]{3,2,1,0:T(2,128)(2,1)S(1)} reverse(bf16[128,8,2,128]{3,2,1,0:T(2,128)(2,1)S(1)} %reshape_squeeze.12), dimensions={2} | reverse | bytes 1048576 | tf_op jit(solution)/shard_map/rev | solution.py:127
  13.3 8.4 %all-to-all-start = ((bf16[8,128,512]{2,1,0:T(8,128)(2,1)}), bf16[8,128,512]{2,1,0:T(8,128)(2,1)S(1)}, u32[]{:S(2)}, u32[]{:S(2)}) async-start(bf16[8,128,512]{2,1,0:T(8,128)(2,1)} %pad_maximum_fusion.1), calls=%async_computation | async-start | bytes 2097152 | tf_op jit(solution)/shard_map/all_to_all | solution.py:36
  29.2 2.8 %collective-permute-start.5 = (bf16[4,128,256]{2,1,0:T(8,128)(2,1)S(1)}, bf16[4,128,256]{2,1,0:T(8,128)(2,1)S(1)}, u32[]{:S(2)}, u32[]{:S(2)}) collective-permute-start(bf16[4,128,256]{2,1,0:T(8,128)(2,1)S(1)} %get-tuple-element.11), channel_id=1, source_target_pairs={{64,0},{128,64},{192,128},{0,192},{65,1},{129,65},{193,129},{1,193... | collective-permute-start | bytes 786440 | tf_op jit(solution)/shard_map/ppermute | solution.py:52
  33.0 10.5 %collective-permute-done.5 = bf16[4,128,256]{2,1,0:T(8,128)(2,1)S(1)} collective-permute-done((bf16[4,128,256]{2,1,0:T(8,128)(2,1)S(1)}, bf16[4,128,256]{2,1,0:T(8,128)(2,1)S(1)}, u32[]{:S(2)}, u32[]{:S(2)}) %collective-permute-start.5) | collective-permute-done | bytes 262176 | tf_op jit(solution)/shard_map/ppermute | solution.py:52
  44.9 7.9 %collective-permute-done.7 = bf16[4,128,256]{2,1,0:T(8,128)(2,1)S(1)} collective-permute-done((bf16[4,128,256]{2,1,0:T(8,128)(2,1)S(1)}, bf16[4,128,256]{2,1,0:T(8,128)(2,1)S(1)}, u32[]{:S(2)}, u32[]{:S(2)}) %collective-permute-start.7) | collective-permute-done | bytes 262176 | tf_op jit(solution)/shard_map/ppermute | solution.py:52
  74.7 9.6 %all-to-all-start.1 = ((bf16[8,16,4224]{2,1,0:T(8,128)(2,1)}), bf16[8,16,4224]{2,1,0:T(8,128)(2,1)S(1)}, u32[]{:S(2)}, u32[]{:S(2)}) async-start(bf16[8,16,4224]{2,1,0:T(8,128)(2,1)} %pad_maximum_fusion), calls=%async_computation.1 | async-start | bytes 2162688 | tf_op jit(solution)/shard_map/all_to_all | solution.py:36
  95.8 18.8 %all-to-all-done.1 = bf16[8,16,4224]{2,1,0:T(8,128)(2,1)S(1)} async-done(((bf16[8,16,4224]{2,1,0:T(8,128)(2,1)}), bf16[8,16,4224]{2,1,0:T(8,128)(2,1)S(1)}, u32[]{:S(2)}, u32[]{:S(2)}) %all-to-all-start.1) | async-done | bytes 1081376 | tf_op jit(solution)/shard_map/all_to_all | solution.py:36
  116.3 4.1 %all-to-all-start.2 = ((bf16[8,16,128]{2,1,0:T(8,128)(2,1)}), bf16[8,16,128]{2,1,0:T(8,128)(2,1)S(1)}, u32[]{:S(2)}, u32[]{:S(2)}) async-start(bf16[8,16,128]{2,1,0:T(8,128)(2,1)} %broadcast_in_dim.145), calls=%async_computation.2 | async-start | bytes 65536 | tf_op jit(solution)/shard_map/all_to_all | solution.py:36
  120.8 6.0 %collective-permute-start.14 = (bf16[16,4224]{1,0:T(8,128)(2,1)S(1)}, bf16[16,4224]{1,0:T(8,128)(2,1)S(1)}, u32[]{:S(2)}, u32[]{:S(2)}) collective-permute-start(bf16[16,4224]{1,0:T(8,128)(2,1)S(1)} %concatenate.85), channel_id=1, source_target_pairs={{0,8},{8,0},{1,9},{9,1},{2,10},{10,2},{3,11},{11,3},{4,12},{12,4},... | collective-permute-start | bytes 405512 | tf_op jit(solution)/shard_map/ppermute | solution.py:45
  127.5 4.4 %all-to-all-done.2 = bf16[8,16,128]{2,1,0:T(8,128)(2,1)S(1)} async-done(((bf16[8,16,128]{2,1,0:T(8,128)(2,1)}), bf16[8,16,128]{2,1,0:T(8,128)(2,1)S(1)}, u32[]{:S(2)}, u32[]{:S(2)}) %all-to-all-start.2) | async-done | bytes 32800 | tf_op jit(solution)/shard_map/all_to_all | solution.py:36
  134.7 3.1 %convolution_convert_fusion = bf16[128,1408]{1,0:T(8,128)(2,1)} fusion(bf16[768,1408]{1,0:T(8,128)(2,1)} %constant_dynamic-update-slice_fusion.2, f32[128,768]{1,0:T(8,128)S(1)} %fusion.53), kind=kOutput, calls=%fused_computation.12 | convolution fusion | flops 277889024 | bytes 2916352 | tf_op jit(solution)/shard_map/dot_general | solution.py:24
  137.8 3.6 %all-to-all-start.3 = ((bf16[8,16,1408]{2,1,0:T(8,128)(2,1)}), bf16[8,16,1408]{2,1,0:T(8,128)(2,1)S(1)}, u32[]{:S(2)}, u32[]{:S(2)}) async-start(bf16[8,16,1408]{2,1,0:T(8,128)(2,1)} %bitcast.31), calls=%async_computation.3 | async-start | bytes 720896 | tf_op jit(solution)/shard_map/all_to_all | solution.py:36
  142.1 3.1 %collective-permute-start.15 = (bf16[32,4224]{1,0:T(8,128)(2,1)}, bf16[32,4224]{1,0:T(8,128)(2,1)S(1)}, u32[]{:S(2)}, u32[]{:S(2)}) collective-permute-start(bf16[32,4224]{1,0:T(8,128)(2,1)} %pad_maximum_fusion.11), channel_id=1, source_target_pairs={{2,0},{4,2},{6,4},{0,6},{3,1},{5,3},{7,5},{1,7},{10,8},{12,10},{14... | collective-permute-start | bytes 811016 | tf_op jit(solution)/shard_map/ppermute | solution.py:52
  147.7 8.7 %collective-permute-done.15 = bf16[32,4224]{1,0:T(8,128)(2,1)S(1)} collective-permute-done((bf16[32,4224]{1,0:T(8,128)(2,1)}, bf16[32,4224]{1,0:T(8,128)(2,1)S(1)}, u32[]{:S(2)}, u32[]{:S(2)}) %collective-permute-start.15) | collective-permute-done | bytes 270368 | tf_op jit(solution)/shard_map/ppermute | solution.py:52
  160.9 8.7 %all-to-all-start.4 = ((bf16[8,16,1408]{2,1,0:T(8,128)(2,1)}), bf16[8,16,1408]{2,1,0:T(8,128)(2,1)S(1)}, u32[]{:S(2)}, u32[]{:S(2)}) async-start(bf16[8,16,1408]{2,1,0:T(8,128)(2,1)} %broadcast_in_dim.146), calls=%async_computation.4 | async-start | bytes 720896 | tf_op jit(solution)/shard_map/all_to_all | solution.py:36
  175.6 5.5 %all-to-all-done.4 = bf16[8,16,1408]{2,1,0:T(8,128)(2,1)S(1)} async-done(((bf16[8,16,1408]{2,1,0:T(8,128)(2,1)}), bf16[8,16,1408]{2,1,0:T(8,128)(2,1)S(1)}, u32[]{:S(2)}, u32[]{:S(2)}) %all-to-all-start.4) | async-done | bytes 360480 | tf_op jit(solution)/shard_map/all_to_all | solution.py:36
  181.1 3.3 %multiply_reduce_fusion.2 = (f32[128]{0:T(128)S(1)}, f32[128,768]{1,0:T(8,128)}) fusion(f32[128,768]{1,0:T(8,128)} %copy-done.13, bf16[128,1408]{1,0:T(8,128)(2,1)S(1)} %bitcast.124, bf16[768,1408]{1,0:T(8,128)(2,1)} %constant_dynamic-update-slice_fusion.2), kind=kOutput, calls=%fused_computation.88 | convolution fusion | flops 278888320 | bytes 3310080 | tf_op jit(solution)/shard_map/dot_general | solution.py:24
  188.7 4.1 %all-to-all-start.5 = ((bf16[8,176,128]{2,1,0:T(8,128)(2,1)}), bf16[8,176,128]{2,1,0:T(8,128)(2,1)}, u32[]{:S(2)}, u32[]{:S(2)}) async-start(bf16[8,176,128]{2,1,0:T(8,128)(2,1)} %broadcast_in_dim.150), calls=%async_computation.5 | async-start | bytes 720896 | tf_op jit(solution)/shard_map/all_to_all | solution.py:36
  211.8 3.2 %fusion.147 = (f32[128]{0:T(128)}, f32[128]{0:T(128)}, f32[128,4096]{1,0:T(8,128)}) fusion(f32[128,4224]{1,0:T(8,128)S(1)} %fusion.78, f32[4096]{0:T(1024)S(1)} %bitcast.133, bf16[4096,128]{1,0:T(8,128)(2,1)S(1)} %copy-done, bf16[256,128]{0,1:T(8,128)(2,1)S(1)} %get-tuple-element.48, s32[256]{0:T(256)} %bitcast.140, s32[128]{0:T(128)} %iota_add_fusion), kind=kOutput, calls=%fused_computation.323 | convolution fusion | flops 144752384 | bytes 5327360 | tf_op jit(solution)/shard_map/dot_general | solution.py:24
  215.0 3.8 %multiply_reduce_fusion.4 = (f32[256]{0:T(256)}, bf16[256,128]{0,1:T(8,128)(2,1)}) fusion(bf16[256,128]{0,1:T(8,128)(2,1)S(1)} %copy-done.15, f32[256]{0:T(256)} %get-tuple-element.20, f32[256,128]{0,1:T(8,128)} %copy.69, f32[256]{0:T(256)} %get-tuple-element.8, f32[128]{0:T(128)} %convert_reduce_fusion.1, f32[256]{0:T(256)} %get-tuple-element.7, ...), kind=kOutput, calls=%fused_computation.130 | convolution fusion | flops 144523008 | bytes 2445824 | tf_op jit(solution)/shard_map/dot_general | solution.py:24
  225.9 7.5 %all-to-all-start.6 = ((bf16[8,128,256]{2,1,0:T(8,128)(2,1)}), bf16[8,128,256]{2,1,0:T(8,128)(2,1)S(1)}, u32[]{:S(2)}, u32[]{:S(2)}) async-start(bf16[8,128,256]{2,1,0:T(8,128)(2,1)} %bitcast.39), calls=%async_computation.6 | async-start | bytes 1048576 | tf_op jit(solution)/shard_map/all_to_all | solution.py:36
  233.4 3.0 %fusion.38 = bf16[1,128,4096]{2,1,0:T(8,128)(2,1)} fusion(f32[128,4224]{1,0:T(8,128)S(1)} %fusion.78, f32[128,4096]{1,0:T(8,128)} %get-tuple-element.47, f32[128]{0:T(128)S(1)} %copy-done.39, f32[128]{0:T(128)S(1)} %broadcast_multiply_fusion.1, f32[128]{0:T(128)S(1)} %broadcast_multiply_fusion.2), kind=kLoop, calls=%fused_computation.62 | loop fusion | flops 2621440 | bytes 5244416 | tf_op jit(solution)/shard_map/broadcast_in_dim | solution.py:316
  236.4 10.9 %all-to-all-done.6 = bf16[8,128,256]{2,1,0:T(8,128)(2,1)S(1)} async-done(((bf16[8,128,256]{2,1,0:T(8,128)(2,1)}), bf16[8,128,256]{2,1,0:T(8,128)(2,1)S(1)}, u32[]{:S(2)}, u32[]{:S(2)}) %all-to-all-start.6) | async-done | bytes 524320 | tf_op jit(solution)/shard_map/all_to_all | solution.py:36
  (281 shorter events, 97.1 us)
Async XLA Ops:
  0.6 27.1 %collective-permute-start.2 = (bf16[128,256]{1,0:T(8,128)(2,1)}, bf16[128,256]{1,0:T(8,128)(2,1)S(1)}, u32[]{:S(2)}, u32[]{:S(2)}) collective-permute-start(bf16[128,256]{1,0:T(8,128)(2,1)} %param.25), channel_id=1, source_target_pairs={{16,0},{32,16},{48,32},{0,48},{17,1},{33,17},{49,33},{1,49},{18,2}... | collective-permute-start | bytes 196616 | tf_op jit(solution)/shard_map/ppermute | solution.py:52
  2.5 25.4 %collective-permute-start.3 = (bf16[128,256]{1,0:T(8,128)(2,1)}, bf16[128,256]{1,0:T(8,128)(2,1)S(1)}, u32[]{:S(2)}, u32[]{:S(2)}) collective-permute-start(bf16[128,256]{1,0:T(8,128)(2,1)} %param.25), channel_id=1, source_target_pairs={{32,0},{48,16},{0,32},{16,48},{33,1},{49,17},{1,33},{17,49},{34,2}... | collective-permute-start | bytes 196616 | tf_op jit(solution)/shard_map/ppermute | solution.py:52
  4.1 24.3 %collective-permute-start.4 = (bf16[128,256]{1,0:T(8,128)(2,1)}, bf16[128,256]{1,0:T(8,128)(2,1)S(1)}, u32[]{:S(2)}, u32[]{:S(2)}) collective-permute-start(bf16[128,256]{1,0:T(8,128)(2,1)} %param.25), channel_id=1, source_target_pairs={{48,0},{0,16},{16,32},{32,48},{49,1},{1,17},{17,33},{33,49},{50,2}... | collective-permute-start | bytes 196616 | tf_op jit(solution)/shard_map/ppermute | solution.py:52
  13.3 41.7 %all-to-all-start = ((bf16[8,128,512]{2,1,0:T(8,128)(2,1)}), bf16[8,128,512]{2,1,0:T(8,128)(2,1)S(1)}, u32[]{:S(2)}, u32[]{:S(2)}) async-start(bf16[8,128,512]{2,1,0:T(8,128)(2,1)} %pad_maximum_fusion.1), calls=%async_computation | async-start | bytes 2097152 | tf_op jit(solution)/shard_map/all_to_all | solution.py:36
  21.7 47.8 %collective-permute-start.9 = (bf16[128,4096]{1,0:T(8,128)(2,1)}, bf16[128,4096]{1,0:T(8,128)(2,1)}, u32[]{:S(2)}, u32[]{:S(2)}) collective-permute-start(bf16[128,4096]{1,0:T(8,128)(2,1)} %bitcast.23), channel_id=1, source_target_pairs={{0,1},{1,0},{2,3},{3,2},{4,5},{5,4},{6,7},{7,6},{8,9},{9,8},{10,11... | collective-permute-start | bytes 3145736 | tf_op jit(solution)/shard_map/ppermute | solution.py:45
  21.8 10.2 %collective-permute-start.10 = (bf16[128,128]{1,0:T(8,128)(2,1)S(1)}, bf16[128,128]{1,0:T(8,128)(2,1)S(1)}, u32[]{:S(2)}, u32[]{:S(2)}) collective-permute-start(bf16[128,128]{1,0:T(8,128)(2,1)S(1)} %bitcast.145), channel_id=1, source_target_pairs={{0,1},{1,0},{2,3},{3,2},{4,5},{5,4},{6,7},{7,6},{8,9},{9,8},{10,11... | collective-permute-start | bytes 98312 | tf_op jit(solution)/shard_map/ppermute | solution.py:45
  27.7 62.9 %collective-permute-start.11 = (bf16[1408,384]{1,0:T(8,128)(2,1)}, bf16[1408,384]{1,0:T(8,128)(2,1)}, u32[]{:S(2)}, u32[]{:S(2)}) collective-permute-start(bf16[1408,384]{1,0:T(8,128)(2,1)} %param.32), channel_id=1, source_target_pairs={{0,1},{1,0},{2,3},{3,2},{4,5},{5,4},{6,7},{7,6},{8,9},{9,8},{10,11... | collective-permute-start | bytes 3244040 | tf_op jit(solution)/shard_map/ppermute | solution.py:45
  27.9 64.2 %collective-permute-start.12 = (bf16[384,1408]{1,0:T(8,128)(2,1)}, bf16[384,1408]{1,0:T(8,128)(2,1)}, u32[]{:S(2)}, u32[]{:S(2)}) collective-permute-start(bf16[384,1408]{1,0:T(8,128)(2,1)} %param.33), channel_id=1, source_target_pairs={{0,1},{1,0},{2,3},{3,2},{4,5},{5,4},{6,7},{7,6},{8,9},{9,8},{10,11... | collective-permute-start | bytes 3244040 | tf_op jit(solution)/shard_map/ppermute | solution.py:45
  29.2 14.2 %collective-permute-start.5 = (bf16[4,128,256]{2,1,0:T(8,128)(2,1)S(1)}, bf16[4,128,256]{2,1,0:T(8,128)(2,1)S(1)}, u32[]{:S(2)}, u32[]{:S(2)}) collective-permute-start(bf16[4,128,256]{2,1,0:T(8,128)(2,1)S(1)} %get-tuple-element.11), channel_id=1, source_target_pairs={{64,0},{128,64},{192,128},{0,192},{65,1},{129,65},{193,129},{1,193... | collective-permute-start | bytes 786440 | tf_op jit(solution)/shard_map/ppermute | solution.py:52
  32.0 12.2 %collective-permute-start.6 = (bf16[4,128,256]{2,1,0:T(8,128)(2,1)S(1)}, bf16[4,128,256]{2,1,0:T(8,128)(2,1)S(1)}, u32[]{:S(2)}, u32[]{:S(2)}) collective-permute-start(bf16[4,128,256]{2,1,0:T(8,128)(2,1)S(1)} %get-tuple-element.11), channel_id=1, source_target_pairs={{128,0},{192,64},{0,128},{64,192},{129,1},{193,65},{1,129},{65,193... | collective-permute-start | bytes 786440 | tf_op jit(solution)/shard_map/ppermute | solution.py:52
  43.5 9.4 %collective-permute-start.7 = (bf16[4,128,256]{2,1,0:T(8,128)(2,1)S(1)}, bf16[4,128,256]{2,1,0:T(8,128)(2,1)S(1)}, u32[]{:S(2)}, u32[]{:S(2)}) collective-permute-start(bf16[4,128,256]{2,1,0:T(8,128)(2,1)S(1)} %get-tuple-element.11), channel_id=1, source_target_pairs={{192,0},{0,64},{64,128},{128,192},{193,1},{1,65},{65,129},{129,193... | collective-permute-start | bytes 786440 | tf_op jit(solution)/shard_map/ppermute | solution.py:52
  56.1 7.0 %collective-permute-start = (bf16[1024,384]{1,0:T(8,128)(2,1)}, bf16[1024,384]{1,0:T(8,128)(2,1)}, u32[]{:S(2)}, u32[]{:S(2)}) collective-permute-start(bf16[1024,384]{1,0:T(8,128)(2,1)} %slice.98), channel_id=1, source_target_pairs={{0,1},{1,0},{2,3},{3,2},{4,5},{5,4},{6,7},{7,6},{8,9},{9,8},{10,11... | collective-permute-start | bytes 2359304 | tf_op jit(solution)/shard_map/ppermute | solution.py:45
  61.5 10.1 %collective-permute-start.8 = (bf16[128,4096]{0,1:T(8,128)(2,1)S(1)}, bf16[128,4096]{0,1:T(8,128)(2,1)}, u32[]{:S(2)}, u32[]{:S(2)}) collective-permute-start(bf16[128,4096]{0,1:T(8,128)(2,1)S(1)} %bitcast.112), channel_id=1, source_target_pairs={{0,1},{1,0},{2,3},{3,2},{4,5},{5,4},{6,7},{7,6},{8,9},{9,8},{10,11... | collective-permute-start | bytes 3145736 | tf_op jit(solution)/shard_map/ppermute | solution.py:45
  74.7 39.9 %all-to-all-start.1 = ((bf16[8,16,4224]{2,1,0:T(8,128)(2,1)}), bf16[8,16,4224]{2,1,0:T(8,128)(2,1)S(1)}, u32[]{:S(2)}, u32[]{:S(2)}) async-start(bf16[8,16,4224]{2,1,0:T(8,128)(2,1)} %pad_maximum_fusion), calls=%async_computation.1 | async-start | bytes 2162688 | tf_op jit(solution)/shard_map/all_to_all | solution.py:36
  116.3 15.6 %all-to-all-start.2 = ((bf16[8,16,128]{2,1,0:T(8,128)(2,1)}), bf16[8,16,128]{2,1,0:T(8,128)(2,1)S(1)}, u32[]{:S(2)}, u32[]{:S(2)}) async-start(bf16[8,16,128]{2,1,0:T(8,128)(2,1)} %broadcast_in_dim.145), calls=%async_computation.2 | async-start | bytes 65536 | tf_op jit(solution)/shard_map/all_to_all | solution.py:36
  120.8 20.6 %collective-permute-start.14 = (bf16[16,4224]{1,0:T(8,128)(2,1)S(1)}, bf16[16,4224]{1,0:T(8,128)(2,1)S(1)}, u32[]{:S(2)}, u32[]{:S(2)}) collective-permute-start(bf16[16,4224]{1,0:T(8,128)(2,1)S(1)} %concatenate.85), channel_id=1, source_target_pairs={{0,8},{8,0},{1,9},{9,1},{2,10},{10,2},{3,11},{11,3},{4,12},{12,4},... | collective-permute-start | bytes 405512 | tf_op jit(solution)/shard_map/ppermute | solution.py:45
  137.8 19.5 %all-to-all-start.3 = ((bf16[8,16,1408]{2,1,0:T(8,128)(2,1)}), bf16[8,16,1408]{2,1,0:T(8,128)(2,1)S(1)}, u32[]{:S(2)}, u32[]{:S(2)}) async-start(bf16[8,16,1408]{2,1,0:T(8,128)(2,1)} %bitcast.31), calls=%async_computation.3 | async-start | bytes 720896 | tf_op jit(solution)/shard_map/all_to_all | solution.py:36
  142.1 14.3 %collective-permute-start.15 = (bf16[32,4224]{1,0:T(8,128)(2,1)}, bf16[32,4224]{1,0:T(8,128)(2,1)S(1)}, u32[]{:S(2)}, u32[]{:S(2)}) collective-permute-start(bf16[32,4224]{1,0:T(8,128)(2,1)} %pad_maximum_fusion.11), channel_id=1, source_target_pairs={{2,0},{4,2},{6,4},{0,6},{3,1},{5,3},{7,5},{1,7},{10,8},{12,10},{14... | collective-permute-start | bytes 811016 | tf_op jit(solution)/shard_map/ppermute | solution.py:52
  145.2 24.3 %collective-permute-start.16 = (bf16[32,4224]{1,0:T(8,128)(2,1)}, bf16[32,4224]{1,0:T(8,128)(2,1)}, u32[]{:S(2)}, u32[]{:S(2)}) collective-permute-start(bf16[32,4224]{1,0:T(8,128)(2,1)} %pad_maximum_fusion.11), channel_id=1, source_target_pairs={{4,0},{6,2},{0,4},{2,6},{5,1},{7,3},{1,5},{3,7},{12,8},{14,10},{8,... | collective-permute-start | bytes 811016 | tf_op jit(solution)/shard_map/ppermute | solution.py:52
  146.1 25.3 %collective-permute-start.17 = (bf16[32,4224]{1,0:T(8,128)(2,1)}, bf16[32,4224]{1,0:T(8,128)(2,1)}, u32[]{:S(2)}, u32[]{:S(2)}) collective-permute-start(bf16[32,4224]{1,0:T(8,128)(2,1)} %pad_maximum_fusion.11), channel_id=1, source_target_pairs={{6,0},{0,2},{2,4},{4,6},{7,1},{1,3},{3,5},{5,7},{14,8},{8,10},{10,... | collective-permute-start | bytes 811016 | tf_op jit(solution)/shard_map/ppermute | solution.py:52
  160.9 20.2 %all-to-all-start.4 = ((bf16[8,16,1408]{2,1,0:T(8,128)(2,1)}), bf16[8,16,1408]{2,1,0:T(8,128)(2,1)S(1)}, u32[]{:S(2)}, u32[]{:S(2)}) async-start(bf16[8,16,1408]{2,1,0:T(8,128)(2,1)} %broadcast_in_dim.146), calls=%async_computation.4 | async-start | bytes 720896 | tf_op jit(solution)/shard_map/all_to_all | solution.py:36
  173.2 19.7 %collective-permute-start.18 = (bf16[128,4224]{1,0:T(8,128)(2,1)}, bf16[128,4224]{1,0:T(8,128)(2,1)}, u32[]{:S(2)}, u32[]{:S(2)}) collective-permute-start(bf16[128,4224]{1,0:T(8,128)(2,1)} %get-tuple-element.21), channel_id=1, source_target_pairs={{0,1},{1,0},{2,3},{3,2},{4,5},{5,4},{6,7},{7,6},{8,9},{9,8},{10,11... | collective-permute-start | bytes 3244040 | tf_op jit(solution)/shard_map/ppermute | solution.py:45
  188.7 16.7 %all-to-all-start.5 = ((bf16[8,176,128]{2,1,0:T(8,128)(2,1)}), bf16[8,176,128]{2,1,0:T(8,128)(2,1)}, u32[]{:S(2)}, u32[]{:S(2)}) async-start(bf16[8,176,128]{2,1,0:T(8,128)(2,1)} %broadcast_in_dim.150), calls=%async_computation.5 | async-start | bytes 720896 | tf_op jit(solution)/shard_map/all_to_all | solution.py:36
  225.9 21.4 %all-to-all-start.6 = ((bf16[8,128,256]{2,1,0:T(8,128)(2,1)}), bf16[8,128,256]{2,1,0:T(8,128)(2,1)S(1)}, u32[]{:S(2)}, u32[]{:S(2)}) async-start(bf16[8,128,256]{2,1,0:T(8,128)(2,1)} %bitcast.39), calls=%async_computation.6 | async-start | bytes 1048576 | tf_op jit(solution)/shard_map/all_to_all | solution.py:36
  (59 other events, 543.4 us)

commit v2 on v1

v2 whole, which is shorter than its diff:
```python
import functools
import math

import jax
import jax.numpy as jnp
from jax import lax
from jax.experimental import pallas as pl
from jax.experimental.pallas import tpu as pltpu
from jax.sharding import Mesh, PartitionSpec as P


HEADS = 16
HEAD = 128
PATCH = 128
CHIPS = 8

MASKED = -1e30
LOSS_SCALE = 16.0
EPSILON = 1e-06

F32 = jnp.float32
BF16 = jnp.bfloat16
CHIP = ("zh", "y")
ROWS = ("y", "zh")
MIB = 1024 * 1024


def dot(a, b, dims):
    return lax.dot_general(a, b, (dims, ((), ())), preferred_element_type=F32)


def mm(a, b):
    return dot(a, b, ((1,), (0,)))


def mt(a, b):
    return dot(a, b, ((1,), (1,)))


def exchange(pieces, axis):
    return lax.all_to_all(pieces, axis, split_axis=0, concat_axis=0, tiled=True)


def swap(value, axis="core"):
    return lax.ppermute(value, axis, [(0, 1), (1, 0)])


def ring_blocks(value, axis):
    size = lax.axis_size(axis)
    blocks = [value]
    for step in range(1, size):
        blocks.append(lax.ppermute(value, axis, [((i + step) % size, i) for i in range(size)]))
    return blocks


def whole(shape):
    return pl.BlockSpec(shape, lambda _: (0,) * len(shape))


def kernel_call(body, outs, flops, moved, operands, scalars=None):
    specs = [whole(operand.shape) for operand in operands]
    if scalars is not None:
        specs = [pl.BlockSpec(memory_space=pltpu.SMEM)] + specs
        operands = [scalars] + operands
    return pl.pallas_call(
        body,
        grid=(1,),
        out_shape=[jax.ShapeDtypeStruct(shape, kind) for shape, kind in outs],
        in_specs=specs,
        out_specs=[whole(shape) for shape, _ in outs],
        cost_estimate=pl.CostEstimate(flops=flops, bytes_accessed=moved, transcendentals=0),
    )(*operands)


def pack_body(spots_ref, query_ref, key_ref, value_ref, out_ref):
    core = spots_ref[0]
    for chip in range(CHIPS):
        group = slice((chip // 2) * HEAD, (chip // 2 + 1) * HEAD)
        near = pl.multiple_of((2 * chip + core) * HEAD, HEAD)
        far = pl.multiple_of((2 * chip + 1 - core) * HEAD, HEAD)
        out_ref[chip, :, 0:HEAD] = query_ref[:, pl.ds(near, HEAD)]
        out_ref[chip, :, HEAD : 2 * HEAD] = query_ref[:, pl.ds(far, HEAD)]
        out_ref[chip, :, 2 * HEAD : 3 * HEAD] = key_ref[:, group]
        out_ref[chip, :, 3 * HEAD :] = value_ref[:, group]


def pick_rows(wanted, first, count):
    lanes = lax.broadcasted_iota(jnp.int32, (wanted.shape[0], count), 1) + first
    return (lanes == wanted).astype(F32).astype(BF16)


def attend_body(mine_ref, other_ref, at_ref, live_ref, att_ref, weights_ref, denominator_ref):
    span = mine_ref.shape[0]
    block = 128
    for start in range(0, at_ref.shape[0], block):
        here = slice(start, start + block)
        wanted = at_ref[here, :]
        query = mm(pick_rows(wanted, 0, span), mine_ref[:, 0:HEAD])
        query = query + mm(pick_rows(wanted, span, span), other_ref[:, HEAD : 2 * HEAD])
        query = query.astype(BF16)
        scale = 1.0 / math.sqrt(HEAD)
        first = mt(query, mine_ref[:, 2 * HEAD : 3 * HEAD]) * scale
        first = jnp.where(live_ref[:, 0:span] > 0, first, MASKED)
        second = mt(query, other_ref[:, 2 * HEAD : 3 * HEAD]) * scale
        second = jnp.where(live_ref[:, span:] > 0, second, MASKED)
        highest = jnp.maximum(
            jnp.max(first, axis=-1, keepdims=True), jnp.max(second, axis=-1, keepdims=True)
        )
        first = jnp.exp(first - highest)
        second = jnp.exp(second - highest)
        denominator = jnp.sum(first, axis=-1, keepdims=True) + jnp.sum(
            second, axis=-1, keepdims=True
        )
        first = first.astype(BF16)
        second = second.astype(BF16)
        blended = mm(first, mine_ref[:, 3 * HEAD :]) + mm(second, other_ref[:, 3 * HEAD :])
        att_ref[here, :] = (blended / denominator).astype(BF16)
        weights_ref[here, 0:span] = first
        weights_ref[here, span:] = second
        denominator_ref[here, :] = denominator


def project_body(near, across, index_ref, att_ref, att_other_ref, crop_ref, *refs):
    count = across
    own_refs, pair_refs, refs = refs[:count], refs[count : 2 * count], refs[2 * count :]
    stream_ref, stream_other_ref, noisy_ref, noisy_other_ref, out_ref, weight_ref = refs
    core, chip, x, zl = index_ref[0], index_ref[1], index_ref[2], index_ref[3]
    half = out_ref.shape[0]
    tokens = stream_ref.shape[0]
    width = stream_ref.shape[1]
    rows = pl.ds(pl.multiple_of(core * half, half), half)
    kept = att_ref[rows, :]
    other = att_other_ref[rows, :]
    wanted = crop_ref[rows, :] - chip * (2 * tokens)
    pick = pick_rows(wanted, core * tokens, tokens)
    pick_other = pick_rows(wanted, (1 - core) * tokens, tokens)
    for shift in range(across):
        for step in range(near):
            place = lax.rem(x + shift, across) * near + lax.rem(zl + step, near)
            size = own_refs[shift].shape[2]
            columns = pl.ds(pl.multiple_of(place * size, size), size)
            weight = own_refs[shift][step]
            weight_ref[:, columns] = weight
            total = mm(kept, weight) + mm(other, pair_refs[shift][step])
            total = total + mm(pick, stream_ref[:, columns])
            total = total + mm(pick_other, stream_other_ref[:, columns])
            out_ref[:, columns] = total.astype(BF16)
    noisy = mm(pick, noisy_ref[...]) + mm(pick_other, noisy_other_ref[...])
    out_ref[:, width:] = noisy.astype(BF16)


def slope_body(
    core_ref,
    factor_ref,
    token_ref,
    back_ref,
    crop_ref,
    crop_row_ref,
    weight_latent_ref,
    mean_ref,
    sum_ref,
    unit_weight_ref,
    unit_latent_ref,
    inverse_ref,
    att_ref,
    weights_ref,
    denominator_ref,
    mine_ref,
    other_ref,
    out_ref,
    noise_ref,
):
    span = mine_ref.shape[0]
    block = 128
    core = core_ref[0]
    half = out_ref.shape[0] // 2
    near, far = token_ref[0:half, :], back_ref[0:half, :]
    low = jnp.where(core == 0, near, far).astype(BF16)
    high = jnp.where(core == 0, far, near).astype(BF16)
    for start in range(0, out_ref.shape[0], block):
        here = slice(start, start + block)
        same = (crop_ref[here, :] == crop_row_ref[...]).astype(F32).astype(BF16)
        latent = mm(same[:, 0:half], low) + mm(same[:, half:], high)
        noise = (factor_ref[...] * latent).astype(BF16)
        noise_ref[here, :] = noise
        noise32 = noise.astype(F32)
        row_mean = jnp.sum(noise32 * mean_ref[...], axis=-1, keepdims=True)
        row_along = jnp.sum(noise32 * unit_latent_ref[here, :], axis=-1, keepdims=True)
        slope = mt(noise, weight_latent_ref[...]) - row_mean * sum_ref[...]
        slope = (slope - row_along * unit_weight_ref[here, :]) * inverse_ref[here, :]
        slope = slope.astype(BF16)
        delta = jnp.sum(slope.astype(F32) * att_ref[here, :].astype(F32), axis=-1, keepdims=True)
        recip = 1.0 / denominator_ref[here, :]
        first = mt(slope, mine_ref[:, 3 * HEAD :]) - delta
        first = (weights_ref[here, 0:span].astype(F32) * (first * recip)).astype(BF16)
        second = mt(slope, other_ref[:, 3 * HEAD :]) - delta
        second = (weights_ref[here, span:].astype(F32) * (second * recip)).astype(BF16)
        total = mm(first, mine_ref[:, 2 * HEAD : 3 * HEAD])
        total = total + mm(second, other_ref[:, 2 * HEAD : 3 * HEAD])
        out_ref[here, :] = (total * (1.0 / math.sqrt(HEAD))).astype(BF16)


def spread_body(core_ref, slope_ref, slope_other_ref, label_ref, out_ref):
    core = core_ref[0]
    tokens = out_ref.shape[1]
    own = slope_ref[...]
    other = slope_other_ref[...]
    left = jnp.where(core == 0, own, other)
    right = jnp.where(core == 0, other, own)
    for chip in range(CHIPS):
        token = lax.broadcasted_iota(jnp.int32, (tokens, 1), 0) + (2 * chip + core) * tokens
        pick = (token == label_ref[...]).astype(F32).astype(BF16)
        out_ref[chip, :, 0:HEAD] = mm(pick, left).astype(BF16)
        out_ref[chip, :, HEAD:] = mm(pick, right).astype(BF16)


def home_body(home_ref, out_ref):
    for chip in range(CHIPS):
        out_ref[:, chip * 2 * HEAD : (chip + 1) * 2 * HEAD] = home_ref[chip]


def partial_body(index_ref, arrived_ref, keep_ref, give_ref):
    zh = index_ref[1]
    share = keep_ref.shape[0]
    own = pl.ds(pl.multiple_of(zh * share, share), share)
    away = pl.ds(pl.multiple_of((1 - zh) * share, share), share)
    keep = arrived_ref[0, own, :].astype(F32)
    give = arrived_ref[0, away, :].astype(F32)
    for y in range(1, 4):
        keep = keep + arrived_ref[y, own, :].astype(F32)
        give = give + arrived_ref[y, away, :].astype(F32)
    keep_ref[...] = keep
    give_ref[...] = give.astype(BF16)


def split3(value):
    first = value.astype(BF16)
    rest = value - first.astype(F32)
    second = rest.astype(BF16)
    third = (rest - second.astype(F32)).astype(BF16)
    return first, second, third


def layer_body(
    keep_ref, got_ref, gain_ref, shift_ref, weight_ref, signal_ref, noise_ref, out_ref, unit_ref
):
    width = gain_ref.shape[1]
    residual = keep_ref[:, 0:width] + got_ref[:, 0:width].astype(F32)
    noisy = keep_ref[:, width:] + got_ref[:, width:].astype(F32)
    centred = residual - jnp.mean(residual, axis=-1, keepdims=True)
    inverse = lax.rsqrt(jnp.mean(centred * centred, axis=-1, keepdims=True) + EPSILON)
    unit = centred * inverse
    modulated = (unit * gain_ref[...] + shift_ref[...]).astype(BF16)
    predicted = mm(modulated, weight_ref[...])
    denoised = ((noisy - noise_ref[...] * predicted) / signal_ref[...]).astype(BF16)
    for chip in range(CHIPS):
        out_ref[chip] = denoised
    unit_ref[:, 0:width] = unit.astype(BF16)
    lane = lax.broadcasted_iota(jnp.int32, noisy.shape, 1)
    tail = jnp.zeros(noisy.shape, F32)
    for place, piece in enumerate(split3(inverse)):
        tail = jnp.where(lane == place, piece.astype(F32), tail)
    unit_ref[:, width:] = tail.astype(BF16)


def pair_body(index_ref, own_ref, got_ref, out_ref):
    zh = index_ref[1]
    share = own_ref.shape[0]
    out_ref[pl.ds(pl.multiple_of(zh * share, share), share), :] = own_ref[...]
    out_ref[pl.ds(pl.multiple_of((1 - zh) * share, share), share), :] = got_ref[...]


def half_body(index_ref, *refs):
    y = index_ref[2]
    out_ref = refs[-1]
    size = refs[0].shape[0]
    for shift, ref in enumerate(refs[:-1]):
        place = lax.rem(y + shift, 4)
        out_ref[pl.ds(pl.multiple_of(place * size, size), size), :] = ref[...]


def unit_body(index_ref, half_ref, other_ref, head_ref, latent_ref, weight_ref, along_ref, inverse_ref):
    core = index_ref[0]
    count = half_ref.shape[0]
    width = head_ref.shape[1]
    for ref, place in ((half_ref, core), (other_ref, 1 - core)):
        here = pl.ds(pl.multiple_of(place * count, count), count)
        weight_ref[here, :] = mt(ref[:, 0:width], head_ref[...])
        along_ref[here, :] = mm(ref[:, 0:width], latent_ref[...]) * (1.0 / width)
        inverse_ref[here, :] = jnp.sum(ref[:, width:].astype(F32), axis=-1, keepdims=True)


def norm_body(index_ref, embedded_ref, added_ref, gain_ref, head_ref, out_ref, reward_ref):
    share = added_ref.shape[1]
    rows = 2 * embedded_ref.shape[0]
    own = pl.ds(pl.multiple_of(index_ref[3] * share, share), share)
    summed = added_ref[0].astype(F32)
    for chip in range(1, CHIPS):
        summed = summed + added_ref[chip].astype(F32)
    summed = embedded_ref[own, :] + summed
    root = jnp.sqrt(jnp.mean(summed * summed, axis=-1, keepdims=True) + EPSILON)
    unit = summed / root
    gain, head = gain_ref[...], head_ref[...]
    head_slope = -(LOSS_SCALE / rows) * head * gain
    slope = (head_slope - unit * jnp.mean(head_slope * unit, axis=-1, keepdims=True)) / root
    slope = slope.astype(BF16)
    for chip in range(CHIPS):
        out_ref[chip] = slope
    reward = jnp.sum(unit * gain * head, axis=-1, keepdims=True)
    reward = jnp.sum(reward, axis=0, keepdims=True) / rows
    for place, piece in enumerate(split3(reward)):
        here = slice(place * 16, (place + 1) * 16)
        reward_ref[here, :] = jnp.broadcast_to(piece.astype(F32), (16, PATCH)).astype(BF16)


def back_body(
    slope_ref, down_ref, hidden_ref, latent_ref, embed_ref, root_ref, reward_ref, width, out_ref
):
    hidden = hidden_ref[...]
    upstream = mt(slope_ref[...], down_ref[...])
    scale = math.sqrt(2.0 / math.pi)
    curve = jnp.tanh(scale * (hidden + 0.044715 * (hidden * hidden * hidden)))
    steep = scale * (1.0 + (3.0 * 0.044715) * (hidden * hidden))
    hidden_slope = upstream * (
        0.5 * (1.0 + curve) + 0.5 * hidden * (1.0 - curve * curve) * steep
    )
    along = jnp.sum(hidden_slope * hidden, axis=-1, keepdims=True) * (1.0 / width)
    part = mt(hidden_slope.astype(BF16), latent_ref[...]) - along * embed_ref[...]
    part = (part / root_ref[...]).astype(BF16)
    half = part.shape[0]
    for chip in range(CHIPS):
        out_ref[chip, 0:half, :] = part
        out_ref[chip, half:, :] = reward_ref[...]


def stream_body(
    index_ref, half_ref, other_ref, label_ref, noise_ref, weight_ref, gain_ref, out_ref
):
    core = index_ref[0]
    first = index_ref[4]
    tokens = out_ref.shape[0]
    count = half_ref.shape[0]
    width = gain_ref.shape[1]
    token = lax.broadcasted_iota(jnp.int32, (tokens, 1), 0) + first
    own = label_ref[:, pl.ds(pl.multiple_of(core * count, count), count)]
    away = label_ref[:, pl.ds(pl.multiple_of((1 - core) * count, count), count)]
    own = (token == own).astype(F32).astype(BF16)
    away = (token == away).astype(F32).astype(BF16)
    every = (token == label_ref[...]).astype(F32).astype(BF16)
    noise = mm(every, noise_ref[...]).astype(BF16)
    inverse = mm(own, half_ref[:, width:]) + mm(away, other_ref[:, width:])
    inverse = jnp.sum(inverse, axis=-1, keepdims=True)
    unit = mm(own, half_ref[:, 0:width]) + mm(away, other_ref[:, 0:width])
    slope = mt(noise, weight_ref[...]) * gain_ref[...]
    mean = jnp.mean(slope, axis=-1, keepdims=True)
    along = jnp.mean(slope * unit, axis=-1, keepdims=True)
    out_ref[...] = ((slope - mean - unit * along) * inverse).astype(BF16)


def plan(noise_step):
    phase = (noise_step.astype(F32) / 1000.0 + 0.008) / 1.008 * (math.pi / 2.0)
    signal_root = jnp.cos(phase)
    return (signal_root, jnp.sqrt(1.0 - signal_root * signal_root))


def step(
    stream,
    queries,
    keys,
    values,
    clip_lengths,
    mod_shift,
    mod_scale,
    out_weight,
    final_weight,
    noisy_latents,
    timestep,
    crop_map,
    embed_weight,
    pre_gain,
    up_weight,
    down_weight,
    post_gain,
    head_weight,
):
    tokens = queries.shape[1]
    width = stream.shape[2]
    crop = crop_map[0]
    rows = crop.shape[0]
    half = rows // 2
    share = half // CHIPS
    core = lax.axis_index("core")
    zh = lax.axis_index("zh")
    y = lax.axis_index("y")
    chip = zh * 4 + y
    place = y * 2 + zh
    core_scalar = jnp.reshape(core, (1,)).astype(jnp.int32)
    own_first = (chip * 2 + core) * tokens
    spots = jnp.stack([core, zh, y, place, own_first]).astype(jnp.int32)

    near, across = lax.axis_size("zl"), lax.axis_size("x")
    by_zl = jnp.stack(ring_blocks(out_weight, "zl"))
    weight_blocks = ring_blocks(by_zl, "x")
    pair_blocks = [swap(block) for block in weight_blocks]
    up_pair = jnp.concatenate([up_weight, swap(up_weight)], axis=1)
    down_pair = jnp.concatenate([down_weight, swap(down_weight)], axis=0)

    (sent,) = kernel_call(
        pack_body,
        [((CHIPS, tokens, 4 * HEAD), BF16)],
        10**6,
        2 * MIB,
        [queries[0], keys[0], values[0]],
        spots,
    )
    mine = exchange(sent, CHIP).reshape(CHIPS * tokens, 4 * HEAD)
    other = swap(mine)
    spot_at = jnp.arange(2 * CHIPS * tokens, dtype=jnp.int32)
    spot_core = jnp.where(spot_at < CHIPS * tokens, core, 1 - core)
    spot_rest = spot_at % (CHIPS * tokens)
    token_at = (spot_rest // tokens) * (2 * tokens) + spot_core * tokens + spot_rest % tokens
    live = (token_at < clip_lengths[0]).astype(jnp.int32)[None]
    crop_core = (crop // tokens) % 2
    crop_at = (
        jnp.where(crop_core == core, 0, CHIPS * tokens)
        + (crop // (2 * tokens)) * tokens
        + crop % tokens
    )

    attended, weights, denominator = kernel_call(
        attend_body,
        [((rows, HEAD), BF16), ((rows, 2 * CHIPS * tokens), BF16), ((rows, 1), F32)],
        6 * 10**8,
        4 * MIB,
        [mine, other, crop_at[:, None], live],
    )

    indices = jnp.stack([core, chip, lax.axis_index("x"), lax.axis_index("zl")]).astype(jnp.int32)
    partial, own_weight = kernel_call(
        functools.partial(project_body, near, across),
        [((half, width + PATCH), BF16), ((out_weight.shape[0], width), BF16)],
        6 * 10**8,
        7 * MIB,
        [attended, swap(attended), crop[:, None]]
        + weight_blocks
        + pair_blocks
        + [stream[0], swap(stream[0]), noisy_latents[0], swap(noisy_latents[0])],
        indices,
    )
    arrived = exchange(partial.reshape(4, 2 * share, width + PATCH), "y")
    keep, give = kernel_call(
        partial_body,
        [((share, width + PATCH), F32), ((share, width + PATCH), BF16)],
        10**6,
        2 * MIB,
        [arrived],
        spots,
    )
    got = swap(give, "zh")
    signal_root, noise_root = plan(timestep[0])
    gain_rows = 1.0 + mod_scale[0]
    crop_copies, unit_own = kernel_call(
        layer_body,
        [((CHIPS, share, PATCH), BF16), ((share, width + PATCH), BF16)],
        2 * 10**7,
        2 * MIB,
        [
            keep,
            got,
            gain_rows[None],
            mod_shift,
            final_weight,
            jnp.broadcast_to(signal_root, (1, PATCH)),
            jnp.broadcast_to(noise_root, (1, PATCH)),
        ],
    )
    crop_tokens = exchange(crop_copies, ROWS).reshape(half, PATCH)

    unit_got = swap(unit_own, "zh")
    (unit_pair,) = kernel_call(
        pair_body,
        [((2 * share, width + PATCH), BF16)],
        10**6,
        MIB // 2,
        [unit_own, unit_got],
        spots,
    )
    unit_blocks = ring_blocks(unit_pair, "y")
    (unit_half,) = kernel_call(
        half_body, [((half, width + PATCH), BF16)], 10**6, 2 * MIB, unit_blocks, spots
    )
    unit_other = swap(unit_half)

    embedded = mm(crop_tokens, embed_weight)
    first_root = jnp.sqrt(jnp.mean(embedded * embedded, axis=-1, keepdims=True) + EPSILON)
    first_unit = embedded / first_root
    normed = (first_unit * pre_gain).astype(BF16)
    hidden = mm(normed, up_pair)
    active = jax.nn.gelu(hidden, approximate=True).astype(BF16)
    lowered = mm(active, down_pair).astype(BF16).reshape(CHIPS, share, -1)
    added = exchange(lowered, ROWS)
    reward_width = embedded.shape[1]
    slope_copies, reward_lanes = kernel_call(
        norm_body,
        [((CHIPS, share, reward_width), BF16), ((48, PATCH), BF16)],
        10**6,
        MIB,
        [embedded, added, post_gain[None], head_weight[None]],
        spots,
    )
    slope_half = exchange(slope_copies, ROWS).reshape(half, reward_width)
    gained_embed = (embed_weight.astype(F32) * pre_gain).astype(BF16)
    hidden_embed = mm(gained_embed, up_pair).astype(BF16)
    unit_embed = mt(first_unit.astype(BF16), embed_weight)
    (part_copies,) = kernel_call(
        lambda *refs: back_body(*refs[:-1], reward_width, refs[-1]),
        [((CHIPS, half + 48, PATCH), BF16)],
        3 * 10**8,
        4 * MIB,
        [slope_half, down_pair, hidden, hidden_embed, unit_embed, first_root, reward_lanes],
    )
    parts = exchange(part_copies, ROWS).astype(F32).sum(axis=0)
    direct = lax.optimization_barrier(mt(slope_half, embed_weight))
    direct = jnp.concatenate([direct, jnp.zeros((48, PATCH), F32)], axis=0)
    both = parts + direct
    back = swap(both)
    reward = both + back
    reward = reward[half, 0] + reward[half + 16, 0] + reward[half + 32, 0]
    same = crop[:, None] == crop[None, :]
    gained = final_weight.astype(F32) * gain_rows[:, None]
    gained16 = gained.astype(BF16)
    weight_latent = mm(own_weight, gained16)
    weight_sum = jnp.sum(own_weight.astype(F32), axis=1)
    unit_weight, unit_latent, row_inverse = kernel_call(
        unit_body,
        [((rows, HEAD), F32), ((rows, PATCH), F32), ((rows, 1), F32)],
        6 * 10**8,
        4 * MIB,
        [unit_half, unit_other, own_weight, gained16],
        spots,
    )
    query_slope, noise_slope = kernel_call(
        slope_body,
        [((rows, HEAD), BF16), ((rows, PATCH), BF16)],
        6 * 10**8,
        5 * MIB,
        [
            jnp.broadcast_to(-(noise_root / signal_root), (1, PATCH)),
            both,
            back,
            crop[:, None],
            crop[None, :],
            weight_latent.astype(BF16),
            jnp.mean(gained, axis=0)[None],
            weight_sum[None],
            unit_weight,
            unit_latent,
            row_inverse,
            attended,
            weights,
            denominator,
            mine,
            other,
        ],
        core_scalar,
    )

    earlier = same & (jnp.arange(rows)[None, :] < jnp.arange(rows)[:, None])
    first_seen = jnp.logical_not(jnp.any(earlier, axis=1))
    label = jnp.where(first_seen, crop, -1)
    (spread,) = kernel_call(
        spread_body,
        [((CHIPS, tokens, 2 * HEAD), BF16)],
        10**8,
        MIB,
        [query_slope, swap(query_slope), label[None]],
        core_scalar,
    )
    home = exchange(spread, CHIP)
    (grad_queries,) = kernel_call(home_body, [((tokens, HEADS * HEAD), BF16)], 10**6, MIB, [home])
    (grad_stream,) = kernel_call(
        stream_body,
        [((tokens, width), BF16)],
        6 * 10**8,
        5 * MIB,
        [unit_half, unit_other, label[None], noise_slope, final_weight, gain_rows[None]],
        spots,
    )
    return (jnp.reshape(reward, (1,)), grad_stream[None], grad_queries[None])


DP = ("x", "zl")
CTX = ("zh", "y", "core")


def solution(mesh):
    across = mesh.shape["dp"]
    near = min(4, across)
    fine = Mesh(
        mesh.devices.reshape(across // near, near, 2, 4, 2), ("x", "zl", "zh", "y", "core")
    )
    return jax.shard_map(
        step,
        mesh=fine,
        in_specs=(
            P(DP, CTX, None),
            P(DP, CTX, None),
            P(DP, CTX, None),
            P(DP, CTX, None),
            P(DP),
            P(DP, None),
            P(DP, None),
            P(CTX, DP),
            P(),
            P(DP, CTX, None),
            P(DP),
            P(DP, None),
            P(),
            P(),
            P(None, CTX),
            P(CTX, None),
            P(),
            P(),
        ),
        out_specs=(P(DP), P(DP, CTX, None), P(DP, CTX, None)),
        check_vma=False,
    )
```

time: 252 us -> 253 us (level)
  the two profiles are of different devices: /device:TPU:32 before, /device:TPU:69 now
where the time goes in v2:
time: 253 us; the launch traced here: 248 us
  waiting for transfers between devices  91 us (36%)
  starting transfers between devices  72.6 us (29%)
  Pallas kernels  42.7 us (17%)
  local copies, waits for them, and re-layouts  17.4 us (7%)
  matrix products  10.6 us (4%)
  other arithmetic  8.26 us (3%)
  between operations  5.56 us (2%)
    all_to_all x7, waiting for transfers between devices, exchange(): return lax.all_to_all(pieces, axis, split_axis=0, concat_axis=0, tiled=True)  51.1 us
    pallas_call x14, Pallas kernels, kernel_call(): pl.pallas_call(body, grid=(1,), out_shape=[jax.ShapeDtypeStruct(shape, ki...  42.7 us
    all_to_all x7, starting transfers between devices, exchange(): return lax.all_to_all(pieces, axis, split_axis=0, concat_axis=0, tiled=True)  34.7 us
    ppermute x9, waiting for transfers between devices, ring_blocks(): lax.ppermute(value, axis, [((i + step) % size, i) for i in range(size)])  32 us
    ppermute x15, starting transfers between devices, swap(): return lax.ppermute(value, axis, [(0, 1), (1, 0)])  27.8 us
    dot_general x7, matrix products, dot(): return lax.dot_general(a, b, (dims, ((), ())), preferred_element_type=F32)  10.6 us
    ppermute x9, starting transfers between devices, ring_blocks(): lax.ppermute(value, axis, [((i + step) % size, i) for i in range(size)])  10.1 us
    unnamed x70, local copies, waits for them, and re-layouts  8.6 us
  transfers between devices with their start and end apart: 31, of which 16 were waited for; matrix products, arithmetic and copies ran while one was open for 11% of the time, Pallas kernels for 13%

profile of v2, /device:TPU:69, one launch (start us, length us, event | category | flops | bytes accessed | tf_op | source)
XLA Modules:
  0.0 248.1 jit_solution(13969412034488484470)
XLA Ops:
  3.6 9.1 %all-to-all-start = ((bf16[8,128,512]{2,1,0:T(8,128)(2,1)}), bf16[8,128,512]{2,1,0:T(8,128)(2,1)S(1)}, u32[]{:S(2)}, u32[]{:S(2)}) async-start(bf16[8,128,512]{2,1,0:T(8,128)(2,1)} %shard_map.193), calls=%async_computation | async-start | bytes 2097152 | tf_op jit(solution)/shard_map/all_to_all | solution.py:41
  18.2 19.0 %collective-permute-done.4 = bf16[128,256]{1,0:T(8,128)(2,1)S(1)} collective-permute-done((bf16[128,256]{1,0:T(8,128)(2,1)S(1)}, bf16[128,256]{1,0:T(8,128)(2,1)S(1)}, u32[]{:S(2)}, u32[]{:S(2)}) %collective-permute-start.4) | collective-permute-done | bytes 65568 | tf_op jit(solution)/shard_map/ppermute | solution.py:52
  58.5 4.3 %collective-permute-done.7.refs_3_ = bf16[4,128,256]{2,1,0:T(8,128)(2,1)} collective-permute-done((bf16[4,128,256]{2,1,0:T(8,128)(2,1)}, bf16[4,128,256]{2,1,0:T(8,128)(2,1)}, u32[]{:S(2)}, u32[]{:S(2)}) %collective-permute-start.7) | collective-permute-done | bytes 262176 | tf_op jit(solution)/shard_map/ppermute | solution.py:52
  65.3 4.2 %shard_map.194 = (bf16[256,128]{1,0:T(8,128)(2,1)}, bf16[256,2048]{1,0:T(8,128)(2,1)}, f32[256,1]{1,0:T(8,128)}) custom-call(bf16[1024,512]{1,0:T(8,128)(2,1)} %bitcast.47, bf16[1024,512]{1,0:T(8,128)(2,1)} %collective-permute-done.other_ref, s32[256,1]{1,0:T(8,128)} %fusion.27.at_ref, s32[1,2048]{1,0:T(1,128)} %compare_convert_fusion.live_ref), custom_call_target="tpu_custom_call" | custom-call | flops 600000000 | bytes 4194304 | tf_op jit(solution)/shard_map/pallas_call | solution.py:65
  71.7 4.7 %shard_map.195 = (bf16[128,4224]{1,0:T(8,128)(2,1)}, bf16[128,4096]{1,0:T(8,128)(2,1)}) custom-call(s32[4]{0:T(128)} %pad_add_fusion.1.index_ref, bf16[256,128]{1,0:T(8,128)(2,1)} %get-tuple-element.19.att_ref, bf16[256,128]{1,0:T(8,128)(2,1)} %copy-done.22, s32[256,1]{1,0:T(8,128)} %copy-done.11, bf16[4,128,256]{2,1,0:T(8,128)(2,1)} %pad_maximum_fusion.refs_0_, ...), custom_call_target="tpu_custom_call" | custom-call | flops 600000000 | bytes 7340032 | tf_op jit(solution)/shard_map/pallas_call | solution.py:65
  76.4 4.0 %all-to-all-start.1 = ((bf16[4,32,4224]{2,1,0:T(8,128)(2,1)}), bf16[4,32,4224]{2,1,0:T(8,128)(2,1)S(1)}, u32[]{:S(2)}, u32[]{:S(2)}) async-start(bf16[4,32,4224]{2,1,0:T(8,128)(2,1)} %bitcast.50), calls=%async_computation.1 | async-start | bytes 2162688 | tf_op jit(solution)/shard_map/all_to_all | solution.py:41
  81.0 14.5 %all-to-all-done.1.arrived_ref = bf16[4,32,4224]{2,1,0:T(8,128)(2,1)S(1)} async-done(((bf16[4,32,4224]{2,1,0:T(8,128)(2,1)}), bf16[4,32,4224]{2,1,0:T(8,128)(2,1)S(1)}, u32[]{:S(2)}, u32[]{:S(2)}) %all-to-all-start.1) | async-done | bytes 1081376 | tf_op jit(solution)/shard_map/all_to_all | solution.py:41
  98.5 4.0 %collective-permute-start.14 = (bf16[16,4224]{1,0:T(8,128)(2,1)}, bf16[16,4224]{1,0:T(8,128)(2,1)S(1)}, u32[]{:S(2)}, u32[]{:S(2)}) collective-permute-start(bf16[16,4224]{1,0:T(8,128)(2,1)} %get-tuple-element.22), channel_id=1, source_target_pairs={{0,8},{8,0},{1,9},{9,1},{2,10},{10,2},{3,11},{11,3},{4,12},{12,4},... | collective-permute-start | bytes 405512 | tf_op jit(solution)/shard_map/ppermute | solution.py:45
  103.9 6.6 %collective-permute-done.14.got_ref = bf16[16,4224]{1,0:T(8,128)(2,1)S(1)} collective-permute-done((bf16[16,4224]{1,0:T(8,128)(2,1)}, bf16[16,4224]{1,0:T(8,128)(2,1)S(1)}, u32[]{:S(2)}, u32[]{:S(2)}) %collective-permute-start.14) | collective-permute-done | bytes 135200 | tf_op jit(solution)/shard_map/ppermute | solution.py:45
  114.3 4.0 %all-to-all-start.2 = ((bf16[8,16,128]{2,1,0:T(8,128)(2,1)}), bf16[8,16,128]{2,1,0:T(8,128)(2,1)S(1)}, u32[]{:S(2)}, u32[]{:S(2)}) async-start(bf16[8,16,128]{2,1,0:T(8,128)(2,1)} %get-tuple-element.23), calls=%async_computation.2 | async-start | bytes 65536 | tf_op jit(solution)/shard_map/all_to_all | solution.py:41
  120.7 6.6 %all-to-all-done.2 = bf16[8,16,128]{2,1,0:T(8,128)(2,1)S(1)} async-done(((bf16[8,16,128]{2,1,0:T(8,128)(2,1)}), bf16[8,16,128]{2,1,0:T(8,128)(2,1)S(1)}, u32[]{:S(2)}, u32[]{:S(2)}) %all-to-all-start.2) | async-done | bytes 32800 | tf_op jit(solution)/shard_map/all_to_all | solution.py:41
  131.5 4.2 %all-to-all-start.3 = ((bf16[8,16,1408]{2,1,0:T(8,128)(2,1)}), bf16[8,16,1408]{2,1,0:T(8,128)(2,1)}, u32[]{:S(2)}, u32[]{:S(2)}) async-start(bf16[8,16,1408]{2,1,0:T(8,128)(2,1)} %bitcast.49), calls=%async_computation.3 | async-start | bytes 720896 | tf_op jit(solution)/shard_map/all_to_all | solution.py:41
  137.6 5.3 %collective-permute-start.18 = (bf16[16,4224]{1,0:T(8,128)(2,1)S(1)}, bf16[16,4224]{1,0:T(8,128)(2,1)S(1)}, u32[]{:S(2)}, u32[]{:S(2)}) collective-permute-start(bf16[16,4224]{1,0:T(8,128)(2,1)S(1)} %copy-done.19), channel_id=1, source_target_pairs={{0,8},{8,0},{1,9},{9,1},{2,10},{10,2},{3,11},{11,3},{4,12},{12,4},... | collective-permute-start | bytes 405512 | tf_op jit(solution)/shard_map/ppermute | solution.py:45
  143.0 5.1 %all-to-all-done.3.added_ref = bf16[8,16,1408]{2,1,0:T(8,128)(2,1)} async-done(((bf16[8,16,1408]{2,1,0:T(8,128)(2,1)}), bf16[8,16,1408]{2,1,0:T(8,128)(2,1)}, u32[]{:S(2)}, u32[]{:S(2)}) %all-to-all-start.3) | async-done | bytes 360480 | tf_op jit(solution)/shard_map/all_to_all | solution.py:41
  150.3 4.1 %all-to-all-start.4 = ((bf16[8,16,1408]{2,1,0:T(8,128)(2,1)}), bf16[8,16,1408]{2,1,0:T(8,128)(2,1)}, u32[]{:S(2)}, u32[]{:S(2)}) async-start(bf16[8,16,1408]{2,1,0:T(8,128)(2,1)} %get-tuple-element.24), calls=%async_computation.4 | async-start | bytes 720896 | tf_op jit(solution)/shard_map/all_to_all | solution.py:41
  174.2 8.2 %collective-permute-start.22 = (bf16[128,4224]{1,0:T(8,128)(2,1)}, bf16[128,4224]{1,0:T(8,128)(2,1)S(1)}, u32[]{:S(2)}, u32[]{:S(2)}) collective-permute-start(bf16[128,4224]{1,0:T(8,128)(2,1)} %shard_map.201.half_ref), channel_id=1, source_target_pairs={{0,1},{1,0},{2,3},{3,2},{4,5},{5,4},{6,7},{7,6},{8,9},{9,8},{10,11... | collective-permute-start | bytes 3244040 | tf_op jit(solution)/shard_map/ppermute | solution.py:45
  182.4 3.6 %shard_map.199 = bf16[8,176,128]{2,1,0:T(8,128)(2,1)} custom-call(bf16[128,1408]{1,0:T(8,128)(2,1)} %bitcast.24.refs_0_, bf16[768,1408]{1,0:T(8,128)(2,1)} %copy-done, f32[128,768]{1,0:T(8,128)} %copy-done.13, bf16[128,768]{1,0:T(8,128)(2,1)} %convolution_convert_fusion.1.refs_3_, f32[128,128]{1,0:T(8,128)} %fusion.11.refs_4_, f32[128,1]{1,0:T(8,128)} %copy.34.refs_5_, ...), custom_call_target="tpu_custom_call" | custom-call | flops 300000000 | bytes 4194304 | tf_op jit(solution)/shard_map/pallas_call | solution.py:65
  186.0 5.8 %all-to-all-start.5 = ((bf16[8,176,128]{2,1,0:T(8,128)(2,1)}), bf16[8,176,128]{2,1,0:T(8,128)(2,1)}, u32[]{:S(2)}, u32[]{:S(2)}) async-start(bf16[8,176,128]{2,1,0:T(8,128)(2,1)} %shard_map.199), calls=%async_computation.5 | async-start | bytes 720896 | tf_op jit(solution)/shard_map/all_to_all | solution.py:41
  194.4 13.7 %all-to-all-done.5 = bf16[8,176,128]{2,1,0:T(8,128)(2,1)} async-done(((bf16[8,176,128]{2,1,0:T(8,128)(2,1)}), bf16[8,176,128]{2,1,0:T(8,128)(2,1)}, u32[]{:S(2)}, u32[]{:S(2)}) %all-to-all-start.5) | async-done | bytes 360480 | tf_op jit(solution)/shard_map/all_to_all | solution.py:41
  211.8 4.2 %shard_map.202 = (f32[256,128]{1,0:T(8,128)}, f32[256,128]{1,0:T(8,128)}, f32[256,1]{1,0:T(8,128)}) custom-call(s32[5]{0:T(128)} %stack.51.spots_ref.index_ref, bf16[128,4224]{1,0:T(8,128)(2,1)} %shard_map.201.half_ref, bf16[128,4224]{1,0:T(8,128)(2,1)} %copy-done.7, bf16[128,4096]{1,0:T(8,128)(2,1)} %get-tuple-element.27.head_ref, bf16[4096,128]{1,0:T(8,128)(2,1)} %copy-done.3), custom_call_target="tpu_custom_call" | custom-call | flops 600000000 | bytes 4194304 | tf_op jit(solution)/shard_map/pallas_call | solution.py:65
  216.6 4.4 %shard_map.203 = (bf16[256,128]{1,0:T(8,128)(2,1)}, bf16[256,128]{1,0:T(8,128)(2,1)}) custom-call(s32[1]{0:T(128)} %bitcast.core_ref, f32[1,128]{1,0:T(1,128)} %broadcast_in_dim.64.factor_ref, f32[176,128]{1,0:T(8,128)} %copy-done.14, f32[176,128]{1,0:T(8,128)} %copy-done.16, s32[256,1]{1,0:T(8,128)} %copy-done.11, s32[1,256]{1,0:T(1,128)} %crop_row_ref.1, ...), custom_call_target="tpu_custom_call" | custom-call | flops 600000000 | bytes 5242880 | tf_op jit(solution)/shard_map/pallas_call | solution.py:65
  225.2 3.5 %all-to-all-start.6 = ((bf16[8,128,256]{2,1,0:T(8,128)(2,1)}), bf16[8,128,256]{2,1,0:T(8,128)(2,1)S(1)}, u32[]{:S(2)}, u32[]{:S(2)}) async-start(bf16[8,128,256]{2,1,0:T(8,128)(2,1)} %shard_map.205), calls=%async_computation.6 | async-start | bytes 1048576 | tf_op jit(solution)/shard_map/all_to_all | solution.py:41
  232.2 4.5 %shard_map.204 = bf16[128,4096]{1,0:T(8,128)(2,1)} custom-call(s32[5]{0:T(128)} %stack.51.spots_ref.index_ref, bf16[128,4224]{1,0:T(8,128)(2,1)} %shard_map.201.half_ref, bf16[128,4224]{1,0:T(8,128)(2,1)} %copy-done.7, s32[1,256]{1,0:T(1,128)} %reshape_select_fusion.label_ref, bf16[256,128]{1,0:T(8,128)(2,1)} %get-tuple-element.33.noise_ref, ...), custom_call_target="tpu_custom_call" | custom-call | flops 600000000 | bytes 5242880 | tf_op jit(solution)/shard_map/pallas_call | solution.py:65
  236.6 7.7 %all-to-all-done.6.home_ref = bf16[8,128,256]{2,1,0:T(8,128)(2,1)S(1)} async-done(((bf16[8,128,256]{2,1,0:T(8,128)(2,1)}), bf16[8,128,256]{2,1,0:T(8,128)(2,1)S(1)}, u32[]{:S(2)}, u32[]{:S(2)}) %all-to-all-start.6) | async-done | bytes 524320 | tf_op jit(solution)/shard_map/all_to_all | solution.py:41
  (154 shorter events, 87.3 us)
Async XLA Ops:
  3.6 37.0 %all-to-all-start = ((bf16[8,128,512]{2,1,0:T(8,128)(2,1)}), bf16[8,128,512]{2,1,0:T(8,128)(2,1)S(1)}, u32[]{:S(2)}, u32[]{:S(2)}) async-start(bf16[8,128,512]{2,1,0:T(8,128)(2,1)} %shard_map.193), calls=%async_computation | async-start | bytes 2097152 | tf_op jit(solution)/shard_map/all_to_all | solution.py:41
  12.7 24.4 %collective-permute-start.4 = (bf16[128,256]{1,0:T(8,128)(2,1)S(1)}, bf16[128,256]{1,0:T(8,128)(2,1)S(1)}, u32[]{:S(2)}, u32[]{:S(2)}) collective-permute-start(bf16[128,256]{1,0:T(8,128)(2,1)S(1)} %copy-done.24), channel_id=1, source_target_pairs={{48,0},{0,16},{16,32},{32,48},{49,1},{1,17},{17,33},{33,49},{50,2}... | collective-permute-start | bytes 196616 | tf_op jit(solution)/shard_map/ppermute | solution.py:52
  13.6 29.5 %collective-permute-start.3 = (bf16[128,256]{1,0:T(8,128)(2,1)S(1)}, bf16[128,256]{1,0:T(8,128)(2,1)S(1)}, u32[]{:S(2)}, u32[]{:S(2)}) collective-permute-start(bf16[128,256]{1,0:T(8,128)(2,1)S(1)} %copy-done.24), channel_id=1, source_target_pairs={{32,0},{48,16},{0,32},{16,48},{33,1},{49,17},{1,33},{17,49},{34,2}... | collective-permute-start | bytes 196616 | tf_op jit(solution)/shard_map/ppermute | solution.py:52
  14.7 28.3 %collective-permute-start.2 = (bf16[128,256]{1,0:T(8,128)(2,1)S(1)}, bf16[128,256]{1,0:T(8,128)(2,1)S(1)}, u32[]{:S(2)}, u32[]{:S(2)}) collective-permute-start(bf16[128,256]{1,0:T(8,128)(2,1)S(1)} %copy-done.24), channel_id=1, source_target_pairs={{16,0},{32,16},{48,32},{0,48},{17,1},{33,17},{49,33},{1,49},{18,2}... | collective-permute-start | bytes 196616 | tf_op jit(solution)/shard_map/ppermute | solution.py:52
  16.4 54.3 %collective-permute-start.12 = (bf16[128,4096]{1,0:T(8,128)(2,1)}, bf16[128,4096]{1,0:T(8,128)(2,1)}, u32[]{:S(2)}, u32[]{:S(2)}) collective-permute-start(bf16[128,4096]{1,0:T(8,128)(2,1)} %bitcast.18.refs_8_), channel_id=1, source_target_pairs={{0,1},{1,0},{2,3},{3,2},{4,5},{5,4},{6,7},{7,6},{8,9},{9,8},{10,11... | collective-permute-start | bytes 3145736 | tf_op jit(solution)/shard_map/ppermute | solution.py:45
  18.1 31.4 %collective-permute-start.13 = (bf16[128,128]{1,0:T(8,128)(2,1)S(1)}, bf16[128,128]{1,0:T(8,128)(2,1)S(1)}, u32[]{:S(2)}, u32[]{:S(2)}) collective-permute-start(bf16[128,128]{1,0:T(8,128)(2,1)S(1)} %bitcast.63), channel_id=1, source_target_pairs={{0,1},{1,0},{2,3},{3,2},{4,5},{5,4},{6,7},{7,6},{8,9},{9,8},{10,11... | collective-permute-start | bytes 98312 | tf_op jit(solution)/shard_map/ppermute | solution.py:45
  40.6 24.1 %collective-permute-start = (bf16[1024,512]{1,0:T(8,128)(2,1)S(1)}, bf16[1024,512]{1,0:T(8,128)(2,1)}, u32[]{:S(2)}, u32[]{:S(2)}) collective-permute-start(bf16[1024,512]{1,0:T(8,128)(2,1)S(1)} %bitcast.46), channel_id=1, source_target_pairs={{0,1},{1,0},{2,3},{3,2},{4,5},{5,4},{6,7},{7,6},{8,9},{9,8},{10,11... | collective-permute-start | bytes 3145736 | tf_op jit(solution)/shard_map/ppermute | solution.py:45
  47.0 9.4 %collective-permute-start.6 = (bf16[4,128,256]{2,1,0:T(8,128)(2,1)}, bf16[4,128,256]{2,1,0:T(8,128)(2,1)}, u32[]{:S(2)}, u32[]{:S(2)}) collective-permute-start(bf16[4,128,256]{2,1,0:T(8,128)(2,1)} %pad_maximum_fusion.refs_0_), channel_id=1, source_target_pairs={{128,0},{192,64},{0,128},{64,192},{129,1},{193,65},{1,129},{65,193... | collective-permute-start | bytes 786440 | tf_op jit(solution)/shard_map/ppermute | solution.py:52
  49.6 13.2 %collective-permute-start.7 = (bf16[4,128,256]{2,1,0:T(8,128)(2,1)}, bf16[4,128,256]{2,1,0:T(8,128)(2,1)}, u32[]{:S(2)}, u32[]{:S(2)}) collective-permute-start(bf16[4,128,256]{2,1,0:T(8,128)(2,1)} %pad_maximum_fusion.refs_0_), channel_id=1, source_target_pairs={{192,0},{0,64},{64,128},{128,192},{193,1},{1,65},{65,129},{129,193... | collective-permute-start | bytes 786440 | tf_op jit(solution)/shard_map/ppermute | solution.py:52
  51.8 11.4 %collective-permute-start.8 = (bf16[4,128,256]{2,1,0:T(8,128)(2,1)}, bf16[4,128,256]{2,1,0:T(8,128)(2,1)}, u32[]{:S(2)}, u32[]{:S(2)}) collective-permute-start(bf16[4,128,256]{2,1,0:T(8,128)(2,1)} %pad_maximum_fusion.refs_0_), channel_id=1, source_target_pairs={{0,1},{1,0},{2,3},{3,2},{4,5},{5,4},{6,7},{7,6},{8,9},{9,8},{10,11... | collective-permute-start | bytes 786440 | tf_op jit(solution)/shard_map/ppermute | solution.py:45
  56.5 13.0 %collective-permute-start.9 = (bf16[4,128,256]{2,1,0:T(8,128)(2,1)}, bf16[4,128,256]{2,1,0:T(8,128)(2,1)}, u32[]{:S(2)}, u32[]{:S(2)}) collective-permute-start(bf16[4,128,256]{2,1,0:T(8,128)(2,1)} %collective-permute-done.5.refs_1_), channel_id=1, source_target_pairs={{0,1},{1,0},{2,3},{3,2},{4,5},{5,4},{6,7},{7,6},{8,9},{9,8},{10,11... | collective-permute-start | bytes 786440 | tf_op jit(solution)/shard_map/ppermute | solution.py:45
  64.7 37.8 %collective-permute-start.16 = (bf16[384,1408]{1,0:T(8,128)(2,1)}, bf16[384,1408]{1,0:T(8,128)(2,1)}, u32[]{:S(2)}, u32[]{:S(2)}) collective-permute-start(bf16[384,1408]{1,0:T(8,128)(2,1)} %param.33), channel_id=1, source_target_pairs={{0,1},{1,0},{2,3},{3,2},{4,5},{5,4},{6,7},{7,6},{8,9},{9,8},{10,11... | collective-permute-start | bytes 3244040 | tf_op jit(solution)/shard_map/ppermute | solution.py:45
  70.2 48.1 %collective-permute-start.15 = (bf16[1408,384]{1,0:T(8,128)(2,1)}, bf16[1408,384]{1,0:T(8,128)(2,1)}, u32[]{:S(2)}, u32[]{:S(2)}) collective-permute-start(bf16[1408,384]{1,0:T(8,128)(2,1)} %param.32), channel_id=1, source_target_pairs={{0,1},{1,0},{2,3},{3,2},{4,5},{5,4},{6,7},{7,6},{8,9},{9,8},{10,11... | collective-permute-start | bytes 3244040 | tf_op jit(solution)/shard_map/ppermute | solution.py:45
  76.4 19.1 %all-to-all-start.1 = ((bf16[4,32,4224]{2,1,0:T(8,128)(2,1)}), bf16[4,32,4224]{2,1,0:T(8,128)(2,1)S(1)}, u32[]{:S(2)}, u32[]{:S(2)}) async-start(bf16[4,32,4224]{2,1,0:T(8,128)(2,1)} %bitcast.50), calls=%async_computation.1 | async-start | bytes 2162688 | tf_op jit(solution)/shard_map/all_to_all | solution.py:41
  98.5 12.1 %collective-permute-start.14 = (bf16[16,4224]{1,0:T(8,128)(2,1)}, bf16[16,4224]{1,0:T(8,128)(2,1)S(1)}, u32[]{:S(2)}, u32[]{:S(2)}) collective-permute-start(bf16[16,4224]{1,0:T(8,128)(2,1)} %get-tuple-element.22), channel_id=1, source_target_pairs={{0,8},{8,0},{1,9},{9,1},{2,10},{10,2},{3,11},{11,3},{4,12},{12,4},... | collective-permute-start | bytes 405512 | tf_op jit(solution)/shard_map/ppermute | solution.py:45
  114.3 13.0 %all-to-all-start.2 = ((bf16[8,16,128]{2,1,0:T(8,128)(2,1)}), bf16[8,16,128]{2,1,0:T(8,128)(2,1)S(1)}, u32[]{:S(2)}, u32[]{:S(2)}) async-start(bf16[8,16,128]{2,1,0:T(8,128)(2,1)} %get-tuple-element.23), calls=%async_computation.2 | async-start | bytes 65536 | tf_op jit(solution)/shard_map/all_to_all | solution.py:41
  131.5 16.6 %all-to-all-start.3 = ((bf16[8,16,1408]{2,1,0:T(8,128)(2,1)}), bf16[8,16,1408]{2,1,0:T(8,128)(2,1)}, u32[]{:S(2)}, u32[]{:S(2)}) async-start(bf16[8,16,1408]{2,1,0:T(8,128)(2,1)} %bitcast.49), calls=%async_computation.3 | async-start | bytes 720896 | tf_op jit(solution)/shard_map/all_to_all | solution.py:41
  137.6 17.4 %collective-permute-start.18 = (bf16[16,4224]{1,0:T(8,128)(2,1)S(1)}, bf16[16,4224]{1,0:T(8,128)(2,1)S(1)}, u32[]{:S(2)}, u32[]{:S(2)}) collective-permute-start(bf16[16,4224]{1,0:T(8,128)(2,1)S(1)} %copy-done.19), channel_id=1, source_target_pairs={{0,8},{8,0},{1,9},{9,1},{2,10},{10,2},{3,11},{11,3},{4,12},{12,4},... | collective-permute-start | bytes 405512 | tf_op jit(solution)/shard_map/ppermute | solution.py:45
  150.3 32.1 %all-to-all-start.4 = ((bf16[8,16,1408]{2,1,0:T(8,128)(2,1)}), bf16[8,16,1408]{2,1,0:T(8,128)(2,1)}, u32[]{:S(2)}, u32[]{:S(2)}) async-start(bf16[8,16,1408]{2,1,0:T(8,128)(2,1)} %get-tuple-element.24), calls=%async_computation.4 | async-start | bytes 720896 | tf_op jit(solution)/shard_map/all_to_all | solution.py:41
  157.4 11.1 %collective-permute-start.19 = (bf16[32,4224]{1,0:T(8,128)(2,1)}, bf16[32,4224]{1,0:T(8,128)(2,1)S(1)}, u32[]{:S(2)}, u32[]{:S(2)}) collective-permute-start(bf16[32,4224]{1,0:T(8,128)(2,1)} %shard_map.200.refs_0_), channel_id=1, source_target_pairs={{2,0},{4,2},{6,4},{0,6},{3,1},{5,3},{7,5},{1,7},{10,8},{12,10},{14... | collective-permute-start | bytes 811016 | tf_op jit(solution)/shard_map/ppermute | solution.py:52
  160.5 11.4 %collective-permute-start.21 = (bf16[32,4224]{1,0:T(8,128)(2,1)}, bf16[32,4224]{1,0:T(8,128)(2,1)}, u32[]{:S(2)}, u32[]{:S(2)}) collective-permute-start(bf16[32,4224]{1,0:T(8,128)(2,1)} %shard_map.200.refs_0_), channel_id=1, source_target_pairs={{6,0},{0,2},{2,4},{4,6},{7,1},{1,3},{3,5},{5,7},{14,8},{8,10},{10,... | collective-permute-start | bytes 811016 | tf_op jit(solution)/shard_map/ppermute | solution.py:52
  174.2 36.6 %collective-permute-start.22 = (bf16[128,4224]{1,0:T(8,128)(2,1)}, bf16[128,4224]{1,0:T(8,128)(2,1)S(1)}, u32[]{:S(2)}, u32[]{:S(2)}) collective-permute-start(bf16[128,4224]{1,0:T(8,128)(2,1)} %shard_map.201.half_ref), channel_id=1, source_target_pairs={{0,1},{1,0},{2,3},{3,2},{4,5},{5,4},{6,7},{7,6},{8,9},{9,8},{10,11... | collective-permute-start | bytes 3244040 | tf_op jit(solution)/shard_map/ppermute | solution.py:45
  186.0 22.1 %all-to-all-start.5 = ((bf16[8,176,128]{2,1,0:T(8,128)(2,1)}), bf16[8,176,128]{2,1,0:T(8,128)(2,1)}, u32[]{:S(2)}, u32[]{:S(2)}) async-start(bf16[8,176,128]{2,1,0:T(8,128)(2,1)} %shard_map.199), calls=%async_computation.5 | async-start | bytes 720896 | tf_op jit(solution)/shard_map/all_to_all | solution.py:41
  225.2 19.1 %all-to-all-start.6 = ((bf16[8,128,256]{2,1,0:T(8,128)(2,1)}), bf16[8,128,256]{2,1,0:T(8,128)(2,1)S(1)}, u32[]{:S(2)}, u32[]{:S(2)}) async-start(bf16[8,128,256]{2,1,0:T(8,128)(2,1)} %shard_map.205), calls=%async_computation.6 | async-start | bytes 1048576 | tf_op jit(solution)/shard_map/all_to_all | solution.py:41
  (41 other events, 414.5 us)

commit v3 on v2

--- a/solution.py
+++ b/solution.py
@@ -57,7 +57,7 @@
     return pl.BlockSpec(shape, lambda _: (0,) * len(shape))
 
 
-def kernel_call(body, outs, flops, moved, operands, scalars=None):
+def kernel_call(body, outs, flops, moved, operands, scalars=None, limit=None):
     specs = [whole(operand.shape) for operand in operands]
     if scalars is not None:
         specs = [pl.BlockSpec(memory_space=pltpu.SMEM)] + specs
@@ -68,6 +68,7 @@
         out_shape=[jax.ShapeDtypeStruct(shape, kind) for shape, kind in outs],
         in_specs=specs,
         out_specs=[whole(shape) for shape, _ in outs],
+        compiler_params=pltpu.CompilerParams(vmem_limit_bytes=limit),
         cost_estimate=pl.CostEstimate(flops=flops, bytes_accessed=moved, transcendentals=0),
     )(*operands)
 
@@ -150,8 +151,7 @@
 
 
 def slope_body(
-    core_ref,
-    factor_ref,
+    consts_ref,
     token_ref,
     back_ref,
     crop_ref,
@@ -172,16 +172,16 @@
 ):
     span = mine_ref.shape[0]
     block = 128
-    core = core_ref[0]
+    core = consts_ref[3]
     half = out_ref.shape[0] // 2
     near, far = token_ref[0:half, :], back_ref[0:half, :]
-    low = jnp.where(core == 0, near, far).astype(BF16)
-    high = jnp.where(core == 0, far, near).astype(BF16)
+    low = jnp.where(core == 0.0, near, far).astype(BF16)
+    high = jnp.where(core == 0.0, far, near).astype(BF16)
     for start in range(0, out_ref.shape[0], block):
         here = slice(start, start + block)
         same = (crop_ref[here, :] == crop_row_ref[...]).astype(F32).astype(BF16)
         latent = mm(same[:, 0:half], low) + mm(same[:, half:], high)
-        noise = (factor_ref[...] * latent).astype(BF16)
+        noise = (consts_ref[2] * latent).astype(BF16)
         noise_ref[here, :] = noise
         noise32 = noise.astype(F32)
         row_mean = jnp.sum(noise32 * mean_ref[...], axis=-1, keepdims=True)
@@ -241,9 +241,7 @@
     return first, second, third
 
 
-def layer_body(
-    keep_ref, got_ref, gain_ref, shift_ref, weight_ref, signal_ref, noise_ref, out_ref, unit_ref
-):
+def layer_body(consts_ref, keep_ref, got_ref, gain_ref, shift_ref, weight_ref, out_ref, unit_ref):
     width = gain_ref.shape[1]
     residual = keep_ref[:, 0:width] + got_ref[:, 0:width].astype(F32)
     noisy = keep_ref[:, width:] + got_ref[:, width:].astype(F32)
@@ -252,7 +250,7 @@
     unit = centred * inverse
     modulated = (unit * gain_ref[...] + shift_ref[...]).astype(BF16)
     predicted = mm(modulated, weight_ref[...])
-    denoised = ((noisy - noise_ref[...] * predicted) / signal_ref[...]).astype(BF16)
+    denoised = ((noisy - consts_ref[1] * predicted) / consts_ref[0]).astype(BF16)
     for chip in range(CHIPS):
         out_ref[chip] = denoised
     unit_ref[:, 0:width] = unit.astype(BF16)
@@ -308,9 +306,11 @@
         out_ref[chip] = slope
     reward = jnp.sum(unit * gain * head, axis=-1, keepdims=True)
     reward = jnp.sum(reward, axis=0, keepdims=True) / rows
+    lane = lax.broadcasted_iota(jnp.int32, reward_ref.shape, 1)
+    tail = jnp.zeros(reward_ref.shape, F32)
     for place, piece in enumerate(split3(reward)):
-        here = slice(place * 16, (place + 1) * 16)
-        reward_ref[here, :] = jnp.broadcast_to(piece.astype(F32), (16, PATCH)).astype(BF16)
+        tail = jnp.where(lane == place, piece.astype(F32), tail)
+    reward_ref[...] = tail.astype(BF16)
 
 
 def back_body(
@@ -405,6 +405,9 @@
     up_pair = jnp.concatenate([up_weight, swap(up_weight)], axis=1)
     down_pair = jnp.concatenate([down_weight, swap(down_weight)], axis=0)
 
+    stream_other = swap(stream[0])
+    noisy_other = swap(noisy_latents[0])
+
     (sent,) = kernel_call(
         pack_body,
         [((CHIPS, tokens, 4 * HEAD), BF16)],
@@ -426,16 +429,29 @@
         + (crop // (2 * tokens)) * tokens
         + crop % tokens
     )
+    same = crop[:, None] == crop[None, :]
+    earlier = same & (jnp.arange(rows)[None, :] < jnp.arange(rows)[:, None])
+    first_seen = jnp.logical_not(jnp.any(earlier, axis=1))
+    label = jnp.where(first_seen, crop, -1)
+    label = label[None]
+    indices = jnp.stack([core, chip, lax.axis_index("x"), lax.axis_index("zl")]).astype(jnp.int32)
+    signal_root, noise_root = plan(timestep[0])
+    consts = jnp.stack(
+        [signal_root, noise_root, -(noise_root / signal_root), core.astype(F32)]
+    )
+    gain_rows = 1.0 + mod_scale[0]
+    gain_line = gain_rows[None]
+    at_column = crop_at[:, None]
 
     attended, weights, denominator = kernel_call(
         attend_body,
         [((rows, HEAD), BF16), ((rows, 2 * CHIPS * tokens), BF16), ((rows, 1), F32)],
         6 * 10**8,
         4 * MIB,
-        [mine, other, crop_at[:, None], live],
-    )
-
-    indices = jnp.stack([core, chip, lax.axis_index("x"), lax.axis_index("zl")]).astype(jnp.int32)
+        [mine, other, at_column, live],
+        limit=24 * MIB,
+    )
+
     partial, own_weight = kernel_call(
         functools.partial(project_body, near, across),
         [((half, width + PATCH), BF16), ((out_weight.shape[0], width), BF16)],
@@ -444,7 +460,7 @@
         [attended, swap(attended), crop[:, None]]
         + weight_blocks
         + pair_blocks
-        + [stream[0], swap(stream[0]), noisy_latents[0], swap(noisy_latents[0])],
+        + [stream[0], stream_other, noisy_latents[0], noisy_other],
         indices,
     )
     arrived = exchange(partial.reshape(4, 2 * share, width + PATCH), "y")
@@ -455,24 +471,16 @@
         2 * MIB,
         [arrived],
         spots,
+        limit=16 * MIB,
     )
     got = swap(give, "zh")
-    signal_root, noise_root = plan(timestep[0])
-    gain_rows = 1.0 + mod_scale[0]
     crop_copies, unit_own = kernel_call(
         layer_body,
         [((CHIPS, share, PATCH), BF16), ((share, width + PATCH), BF16)],
         2 * 10**7,
         2 * MIB,
-        [
-            keep,
-            got,
-            gain_rows[None],
-            mod_shift,
-            final_weight,
-            jnp.broadcast_to(signal_root, (1, PATCH)),
-            jnp.broadcast_to(noise_root, (1, PATCH)),
-        ],
+        [keep, got, gain_line, mod_shift, final_weight],
+        consts,
     )
     crop_tokens = exchange(crop_copies, ROWS).reshape(half, PATCH)
 
@@ -487,7 +495,13 @@
     )
     unit_blocks = ring_blocks(unit_pair, "y")
     (unit_half,) = kernel_call(
-        half_body, [((half, width + PATCH), BF16)], 10**6, 2 * MIB, unit_blocks, spots
+        half_body,
+        [((half, width + PATCH), BF16)],
+        10**6,
+        2 * MIB,
+        unit_blocks,
+        spots,
+        limit=16 * MIB,
     )
     unit_other = swap(unit_half)
 
@@ -502,7 +516,7 @@
     reward_width = embedded.shape[1]
     slope_copies, reward_lanes = kernel_call(
         norm_body,
-        [((CHIPS, share, reward_width), BF16), ((48, PATCH), BF16)],
+        [((CHIPS, share, reward_width), BF16), ((16, PATCH), BF16)],
         10**6,
         MIB,
         [embedded, added, post_gain[None], head_weight[None]],
@@ -514,19 +528,18 @@
     unit_embed = mt(first_unit.astype(BF16), embed_weight)
     (part_copies,) = kernel_call(
         lambda *refs: back_body(*refs[:-1], reward_width, refs[-1]),
-        [((CHIPS, half + 48, PATCH), BF16)],
+        [((CHIPS, half + 16, PATCH), BF16)],
         3 * 10**8,
         4 * MIB,
         [slope_half, down_pair, hidden, hidden_embed, unit_embed, first_root, reward_lanes],
     )
     parts = exchange(part_copies, ROWS).astype(F32).sum(axis=0)
     direct = lax.optimization_barrier(mt(slope_half, embed_weight))
-    direct = jnp.concatenate([direct, jnp.zeros((48, PATCH), F32)], axis=0)
+    direct = jnp.concatenate([direct, jnp.zeros((16, PATCH), F32)], axis=0)
     both = parts + direct
     back = swap(both)
     reward = both + back
-    reward = reward[half, 0] + reward[half + 16, 0] + reward[half + 32, 0]
-    same = crop[:, None] == crop[None, :]
+    reward = reward[half, 0] + reward[half, 1] + reward[half, 2]
     gained = final_weight.astype(F32) * gain_rows[:, None]
     gained16 = gained.astype(BF16)
     weight_latent = mm(own_weight, gained16)
@@ -545,7 +558,6 @@
         6 * 10**8,
         5 * MIB,
         [
-            jnp.broadcast_to(-(noise_root / signal_root), (1, PATCH)),
             both,
             back,
             crop[:, None],
@@ -562,28 +574,28 @@
             mine,
             other,
         ],
-        core_scalar,
-    )
-
-    earlier = same & (jnp.arange(rows)[None, :] < jnp.arange(rows)[:, None])
-    first_seen = jnp.logical_not(jnp.any(earlier, axis=1))
-    label = jnp.where(first_seen, crop, -1)
+        consts,
+    )
+
     (spread,) = kernel_call(
         spread_body,
         [((CHIPS, tokens, 2 * HEAD), BF16)],
         10**8,
         MIB,
-        [query_slope, swap(query_slope), label[None]],
+        [query_slope, swap(query_slope), label],
         core_scalar,
+        limit=16 * MIB,
     )
     home = exchange(spread, CHIP)
-    (grad_queries,) = kernel_call(home_body, [((tokens, HEADS * HEAD), BF16)], 10**6, MIB, [home])
+    (grad_queries,) = kernel_call(
+        home_body, [((tokens, HEADS * HEAD), BF16)], 10**6, MIB, [home], limit=16 * MIB
+    )
     (grad_stream,) = kernel_call(
         stream_body,
         [((tokens, width), BF16)],
         6 * 10**8,
         5 * MIB,
-        [unit_half, unit_other, label[None], noise_slope, final_weight, gain_rows[None]],
+        [unit_half, unit_other, label, noise_slope, final_weight, gain_line],
         spots,
     )
     return (jnp.reshape(reward, (1,)), grad_stream[None], grad_queries[None])

time: 253 us -> 238 us (0.941)
  starting transfers between devices: 72.6 us -> 61.9 us
  Pallas kernels: 42.7 us -> 35.1 us
    all_to_all x7, waiting for transfers between devices: 51.1 us -> 64.2 us  [exchange(): return lax.all_to_all(pieces, axis, split_axis=0, concat_axis=0, tiled=True)]
    ppermute x9, waiting for transfers between devices: 32 us -> 19.9 us  [ring_blocks(): lax.ppermute(value, axis, [((i + step) % size, i) for i in range(size)])]
    ppermute x15, starting transfers between devices: 27.8 us -> 18.5 us  [swap(): return lax.ppermute(value, axis, [(0, 1), (1, 0)])]
    pallas_call x14, Pallas kernels: 42.7 us -> 35.1 us  [kernel_call(): pl.pallas_call(body, grid=(1,), out_shape=[jax.ShapeDtypeStruct(shape, ki...]
    unnamed x70 -> x84, local copies, waits for them, and re-layouts: 8.6 us -> 11.4 us
  transfers between devices with their start and end apart: 31 -> 31, of which waited for: 16 -> 12; matrix products, arithmetic and copies ran while one was open for 11% -> 11% of each run, Pallas kernels for 13% -> 11%
where the time goes in v3:
time: 238 us; the launch traced here: 234 us
  waiting for transfers between devices  93.3 us (39%)
  starting transfers between devices  61.9 us (26%)
  Pallas kernels  35.1 us (15%)
  local copies, waits for them, and re-layouts  19.5 us (8%)
  matrix products  11.3 us (5%)
  other arithmetic  6.89 us (3%)
  between operations  5.67 us (2%)
    all_to_all x7, waiting for transfers between devices, exchange(): return lax.all_to_all(pieces, axis, split_axis=0, concat_axis=0, tiled=True)  64.2 us
    pallas_call x14, Pallas kernels, kernel_call(): pl.pallas_call(body, grid=(1,), out_shape=[jax.ShapeDtypeStruct(shape, ki...  35.1 us
    all_to_all x7, starting transfers between devices, exchange(): return lax.all_to_all(pieces, axis, split_axis=0, concat_axis=0, tiled=True)  33.3 us
    ppermute x9, waiting for transfers between devices, ring_blocks(): lax.ppermute(value, axis, [((i + step) % size, i) for i in range(size)])  19.9 us
    ppermute x15, starting transfers between devices, swap(): return lax.ppermute(value, axis, [(0, 1), (1, 0)])  18.5 us
    unnamed x84, local copies, waits for them, and re-layouts  11.4 us
    dot_general x7, matrix products, dot(): return lax.dot_general(a, b, (dims, ((), ())), preferred_element_type=F32)  11.3 us
    ppermute x9, starting transfers between devices, ring_blocks(): lax.ppermute(value, axis, [((i + step) % size, i) for i in range(size)])  10.1 us
  transfers between devices with their start and end apart: 31, of which 12 were waited for; matrix products, arithmetic and copies ran while one was open for 11% of the time, Pallas kernels for 11%

profile of v3, /device:TPU:69, one launch (start us, length us, event | category | flops | bytes accessed | tf_op | source)
XLA Modules:
  0.0 233.7 jit_solution(4038734753696151019)
XLA Ops:
  3.6 9.1 %all-to-all-start = ((bf16[8,128,512]{2,1,0:T(8,128)(2,1)}), bf16[8,128,512]{2,1,0:T(8,128)(2,1)S(1)}, u32[]{:S(2)}, u32[]{:S(2)}) async-start(bf16[8,128,512]{2,1,0:T(8,128)(2,1)} %shard_map.193), calls=%async_computation | async-start | bytes 2097152 | tf_op jit(solution)/shard_map/all_to_all | solution.py:41
  18.2 22.5 %all-to-all-done = bf16[8,128,512]{2,1,0:T(8,128)(2,1)S(1)} async-done(((bf16[8,128,512]{2,1,0:T(8,128)(2,1)}), bf16[8,128,512]{2,1,0:T(8,128)(2,1)S(1)}, u32[]{:S(2)}, u32[]{:S(2)}) %all-to-all-start) | async-done | bytes 1048608 | tf_op jit(solution)/shard_map/all_to_all | solution.py:41
  59.0 3.4 %collective-permute-done.7.refs_3_ = bf16[4,128,256]{2,1,0:T(8,128)(2,1)} collective-permute-done((bf16[4,128,256]{2,1,0:T(8,128)(2,1)}, bf16[4,128,256]{2,1,0:T(8,128)(2,1)}, u32[]{:S(2)}, u32[]{:S(2)}) %collective-permute-start.7) | collective-permute-done | bytes 262176 | tf_op jit(solution)/shard_map/ppermute | solution.py:52
  70.0 4.7 %shard_map.195 = (bf16[128,4224]{1,0:T(8,128)(2,1)}, bf16[128,4096]{1,0:T(8,128)(2,1)}) custom-call(s32[4]{0:T(128)} %pad_add_fusion.1.index_ref, bf16[256,128]{1,0:T(8,128)(2,1)} %copy-done.6, bf16[256,128]{1,0:T(8,128)(2,1)} %copy-done.31, s32[256,1]{1,0:T(8,128)} %copy-done.18, bf16[4,128,256]{2,1,0:T(8,128)(2,1)} %pad_maximum_fusion.refs_0_, ...), custom_call_target="tpu_custom_call" | custom-call | flops 600000000 | bytes 7340032 | tf_op jit(solution)/shard_map/pallas_call | solution.py:65
  74.7 4.0 %all-to-all-start.1 = ((bf16[4,32,4224]{2,1,0:T(8,128)(2,1)}), bf16[4,32,4224]{2,1,0:T(8,128)(2,1)S(1)}, u32[]{:S(2)}, u32[]{:S(2)}) async-start(bf16[4,32,4224]{2,1,0:T(8,128)(2,1)} %bitcast.53), calls=%async_computation.1 | async-start | bytes 2162688 | tf_op jit(solution)/shard_map/all_to_all | solution.py:41
  79.3 14.6 %all-to-all-done.1.arrived_ref = bf16[4,32,4224]{2,1,0:T(8,128)(2,1)S(1)} async-done(((bf16[4,32,4224]{2,1,0:T(8,128)(2,1)}), bf16[4,32,4224]{2,1,0:T(8,128)(2,1)S(1)}, u32[]{:S(2)}, u32[]{:S(2)}) %all-to-all-start.1) | async-done | bytes 1081376 | tf_op jit(solution)/shard_map/all_to_all | solution.py:41
  98.2 7.8 %collective-permute-done.14.got_ref = bf16[16,4224]{1,0:T(8,128)(2,1)S(1)} collective-permute-done((bf16[16,4224]{1,0:T(8,128)(2,1)S(1)}, bf16[16,4224]{1,0:T(8,128)(2,1)S(1)}, u32[]{:S(2)}, u32[]{:S(2)}) %collective-permute-start.14) | collective-permute-done | bytes 135200 | tf_op jit(solution)/shard_map/ppermute | solution.py:45
  109.3 3.3 %all-to-all-start.2 = ((bf16[8,16,128]{2,1,0:T(8,128)(2,1)}), bf16[8,16,128]{2,1,0:T(8,128)(2,1)S(1)}, u32[]{:S(2)}, u32[]{:S(2)}) async-start(bf16[8,16,128]{2,1,0:T(8,128)(2,1)} %get-tuple-element.23), calls=%async_computation.2 | async-start | bytes 65536 | tf_op jit(solution)/shard_map/all_to_all | solution.py:41
  115.0 6.5 %all-to-all-done.2 = bf16[8,16,128]{2,1,0:T(8,128)(2,1)S(1)} async-done(((bf16[8,16,128]{2,1,0:T(8,128)(2,1)}), bf16[8,16,128]{2,1,0:T(8,128)(2,1)S(1)}, u32[]{:S(2)}, u32[]{:S(2)}) %all-to-all-start.2) | async-done | bytes 32800 | tf_op jit(solution)/shard_map/all_to_all | solution.py:41
  125.7 3.4 %all-to-all-start.3 = ((bf16[8,16,1408]{2,1,0:T(8,128)(2,1)}), bf16[8,16,1408]{2,1,0:T(8,128)(2,1)S(1)}, u32[]{:S(2)}, u32[]{:S(2)}) async-start(bf16[8,16,1408]{2,1,0:T(8,128)(2,1)} %bitcast.52), calls=%async_computation.3 | async-start | bytes 720896 | tf_op jit(solution)/shard_map/all_to_all | solution.py:41
  130.7 5.3 %collective-permute-start.18 = (bf16[16,4224]{1,0:T(8,128)(2,1)S(1)}, bf16[16,4224]{1,0:T(8,128)(2,1)S(1)}, u32[]{:S(2)}, u32[]{:S(2)}) collective-permute-start(bf16[16,4224]{1,0:T(8,128)(2,1)S(1)} %copy-done.28), channel_id=1, source_target_pairs={{0,8},{8,0},{1,9},{9,1},{2,10},{10,2},{3,11},{11,3},{4,12},{12,4},... | collective-permute-start | bytes 405512 | tf_op jit(solution)/shard_map/ppermute | solution.py:45
  137.8 5.4 %all-to-all-done.3.added_ref = bf16[8,16,1408]{2,1,0:T(8,128)(2,1)S(1)} async-done(((bf16[8,16,1408]{2,1,0:T(8,128)(2,1)}), bf16[8,16,1408]{2,1,0:T(8,128)(2,1)S(1)}, u32[]{:S(2)}, u32[]{:S(2)}) %all-to-all-start.3) | async-done | bytes 360480 | tf_op jit(solution)/shard_map/all_to_all | solution.py:41
  146.1 4.2 %all-to-all-start.4 = ((bf16[8,16,1408]{2,1,0:T(8,128)(2,1)}), bf16[8,16,1408]{2,1,0:T(8,128)(2,1)}, u32[]{:S(2)}, u32[]{:S(2)}) async-start(bf16[8,16,1408]{2,1,0:T(8,128)(2,1)} %get-tuple-element.24), calls=%async_computation.4 | async-start | bytes 720896 | tf_op jit(solution)/shard_map/all_to_all | solution.py:41
  156.6 2.8 %convolution_convert_fusion.1.refs_3_ = bf16[128,768]{1,0:T(8,128)(2,1)} fusion(bf16[1408,768]{1,0:T(8,128)(2,1)} %constant_dynamic-update-slice_fusion, bf16[128,1408]{1,0:T(8,128)(2,1)S(1)} %copy-done.15, f32[1408]{0:T(1024)S(1)} %copy-done.38), kind=kOutput, calls=%fused_computation.5 | convolution fusion | flops 277463040 | bytes 2725376 | tf_op jit(solution)/shard_map/dot_general | solution.py:29
  159.4 5.7 %collective-permute-done.19.refs_1_ = bf16[32,4224]{1,0:T(8,128)(2,1)S(1)} collective-permute-done((bf16[32,4224]{1,0:T(8,128)(2,1)}, bf16[32,4224]{1,0:T(8,128)(2,1)S(1)}, u32[]{:S(2)}, u32[]{:S(2)}) %collective-permute-start.19) | collective-permute-done | bytes 270368 | tf_op jit(solution)/shard_map/ppermute | solution.py:52
  165.1 8.1 %collective-permute-done.21.refs_3_ = bf16[32,4224]{1,0:T(8,128)(2,1)S(1)} collective-permute-done((bf16[32,4224]{1,0:T(8,128)(2,1)}, bf16[32,4224]{1,0:T(8,128)(2,1)S(1)}, u32[]{:S(2)}, u32[]{:S(2)}) %collective-permute-start.21) | collective-permute-done | bytes 270368 | tf_op jit(solution)/shard_map/ppermute | solution.py:52
  177.2 3.5 %shard_map.199 = bf16[8,144,128]{2,1,0:T(8,128)(2,1)} custom-call(bf16[128,1408]{1,0:T(8,128)(2,1)} %bitcast.27.refs_0_, bf16[768,1408]{1,0:T(8,128)(2,1)} %constant_dynamic-update-slice_fusion.2.refs_1_, f32[128,768]{1,0:T(8,128)} %copy-done.19, bf16[128,768]{1,0:T(8,128)(2,1)} %convolution_convert_fusion.1.refs_3_, f32[128,128]{1,0:T(8,128)} %fusion.11.refs_4_, ...), custom_call_target="tpu_custom_call" | custom-call | flops 300000000 | bytes 4194304 | tf_op jit(solution)/shard_map/pallas_call | solution.py:65
  180.7 5.7 %all-to-all-start.5 = ((bf16[8,144,128]{2,1,0:T(8,128)(2,1)}), bf16[8,144,128]{2,1,0:T(8,128)(2,1)S(1)}, u32[]{:S(2)}, u32[]{:S(2)}) async-start(bf16[8,144,128]{2,1,0:T(8,128)(2,1)} %shard_map.199), calls=%async_computation.5 | async-start | bytes 589824 | tf_op jit(solution)/shard_map/all_to_all | solution.py:41
  189.9 7.8 %all-to-all-done.5 = bf16[8,144,128]{2,1,0:T(8,128)(2,1)S(1)} async-done(((bf16[8,144,128]{2,1,0:T(8,128)(2,1)}), bf16[8,144,128]{2,1,0:T(8,128)(2,1)S(1)}, u32[]{:S(2)}, u32[]{:S(2)}) %all-to-all-start.5) | async-done | bytes 294944 | tf_op jit(solution)/shard_map/all_to_all | solution.py:41
  200.0 4.2 %shard_map.202 = (f32[256,128]{1,0:T(8,128)}, f32[256,128]{1,0:T(8,128)}, f32[256,1]{1,0:T(8,128)}) custom-call(s32[5]{0:T(128)} %stack.66.spots_ref.index_ref, bf16[128,4224]{1,0:T(8,128)(2,1)} %copy-done, bf16[128,4224]{1,0:T(8,128)(2,1)} %collective-permute-done.22.other_ref, bf16[128,4096]{1,0:T(8,128)(2,1)} %get-tuple-element.27.head_ref, ...), custom_call_target="tpu_custom_call" | custom-call | flops 600000000 | bytes 4194304 | tf_op jit(solution)/shard_map/pallas_call | solution.py:65
  204.8 4.4 %shard_map.203 = (bf16[256,128]{1,0:T(8,128)(2,1)}, bf16[256,128]{1,0:T(8,128)(2,1)}) custom-call(f32[4]{0:T(128)} %pad_maximum_fusion.1.consts_ref, f32[144,128]{1,0:T(8,128)} %copy-done.22, f32[144,128]{1,0:T(8,128)} %copy-done.24, s32[256,1]{1,0:T(8,128)} %copy-done.18, s32[1,256]{1,0:T(1,128)} %crop_row_ref.1, ...), custom_call_target="tpu_custom_call" | custom-call | flops 600000000 | bytes 5242880 | tf_op jit(solution)/shard_map/pallas_call | solution.py:65
  212.7 3.5 %all-to-all-start.6 = ((bf16[8,128,256]{2,1,0:T(8,128)(2,1)}), bf16[8,128,256]{2,1,0:T(8,128)(2,1)S(1)}, u32[]{:S(2)}, u32[]{:S(2)}) async-start(bf16[8,128,256]{2,1,0:T(8,128)(2,1)} %shard_map.205), calls=%async_computation.6 | async-start | bytes 1048576 | tf_op jit(solution)/shard_map/all_to_all | solution.py:41
  219.8 4.5 %shard_map.204 = bf16[128,4096]{1,0:T(8,128)(2,1)} custom-call(s32[5]{0:T(128)} %stack.66.spots_ref.index_ref, bf16[128,4224]{1,0:T(8,128)(2,1)} %copy-done, bf16[128,4224]{1,0:T(8,128)(2,1)} %collective-permute-done.22.other_ref, s32[1,256]{1,0:T(1,128)} %copy-done.11, bf16[256,128]{1,0:T(8,128)(2,1)} %get-tuple-element.33.noise_ref, ...), custom_call_target="tpu_custom_call" | custom-call | flops 600000000 | bytes 5242880 | tf_op jit(solution)/shard_map/pallas_call | solution.py:65
  224.3 7.5 %all-to-all-done.6.home_ref = bf16[8,128,256]{2,1,0:T(8,128)(2,1)S(1)} async-done(((bf16[8,128,256]{2,1,0:T(8,128)(2,1)}), bf16[8,128,256]{2,1,0:T(8,128)(2,1)S(1)}, u32[]{:S(2)}, u32[]{:S(2)}) %all-to-all-start.6) | async-done | bytes 524320 | tf_op jit(solution)/shard_map/all_to_all | solution.py:41
  (166 shorter events, 76.3 us)
Async XLA Ops:
  3.6 37.0 %all-to-all-start = ((bf16[8,128,512]{2,1,0:T(8,128)(2,1)}), bf16[8,128,512]{2,1,0:T(8,128)(2,1)S(1)}, u32[]{:S(2)}, u32[]{:S(2)}) async-start(bf16[8,128,512]{2,1,0:T(8,128)(2,1)} %shard_map.193), calls=%async_computation | async-start | bytes 2097152 | tf_op jit(solution)/shard_map/all_to_all | solution.py:41
  12.8 32.6 %collective-permute-start.4 = (bf16[128,256]{1,0:T(8,128)(2,1)S(1)}, bf16[128,256]{1,0:T(8,128)(2,1)S(1)}, u32[]{:S(2)}, u32[]{:S(2)}) collective-permute-start(bf16[128,256]{1,0:T(8,128)(2,1)S(1)} %copy-done.32), channel_id=1, source_target_pairs={{48,0},{0,16},{16,32},{32,48},{49,1},{1,17},{17,33},{33,49},{50,2}... | collective-permute-start | bytes 196616 | tf_op jit(solution)/shard_map/ppermute | solution.py:52
  13.6 32.2 %collective-permute-start.3 = (bf16[128,256]{1,0:T(8,128)(2,1)S(1)}, bf16[128,256]{1,0:T(8,128)(2,1)S(1)}, u32[]{:S(2)}, u32[]{:S(2)}) collective-permute-start(bf16[128,256]{1,0:T(8,128)(2,1)S(1)} %copy-done.32), channel_id=1, source_target_pairs={{32,0},{48,16},{0,32},{16,48},{33,1},{49,17},{1,33},{17,49},{34,2}... | collective-permute-start | bytes 196616 | tf_op jit(solution)/shard_map/ppermute | solution.py:52
  14.8 31.0 %collective-permute-start.2 = (bf16[128,256]{1,0:T(8,128)(2,1)S(1)}, bf16[128,256]{1,0:T(8,128)(2,1)S(1)}, u32[]{:S(2)}, u32[]{:S(2)}) collective-permute-start(bf16[128,256]{1,0:T(8,128)(2,1)S(1)} %copy-done.32), channel_id=1, source_target_pairs={{16,0},{32,16},{48,32},{0,48},{17,1},{33,17},{49,33},{1,49},{18,2}... | collective-permute-start | bytes 196616 | tf_op jit(solution)/shard_map/ppermute | solution.py:52
  16.4 52.3 %collective-permute-start.12 = (bf16[128,4096]{1,0:T(8,128)(2,1)S(1)}, bf16[128,4096]{1,0:T(8,128)(2,1)}, u32[]{:S(2)}, u32[]{:S(2)}) collective-permute-start(bf16[128,4096]{1,0:T(8,128)(2,1)S(1)} %bitcast.55), channel_id=1, source_target_pairs={{0,1},{1,0},{2,3},{3,2},{4,5},{5,4},{6,7},{7,6},{8,9},{9,8},{10,11... | collective-permute-start | bytes 3145736 | tf_op jit(solution)/shard_map/ppermute | solution.py:45
  40.6 22.9 %collective-permute-start = (bf16[1024,512]{1,0:T(8,128)(2,1)S(1)}, bf16[1024,512]{1,0:T(8,128)(2,1)S(1)}, u32[]{:S(2)}, u32[]{:S(2)}) collective-permute-start(bf16[1024,512]{1,0:T(8,128)(2,1)S(1)} %bitcast.49), channel_id=1, source_target_pairs={{0,1},{1,0},{2,3},{3,2},{4,5},{5,4},{6,7},{7,6},{8,9},{9,8},{10,11... | collective-permute-start | bytes 3145736 | tf_op jit(solution)/shard_map/ppermute | solution.py:45
  46.8 10.3 %collective-permute-start.6 = (bf16[4,128,256]{2,1,0:T(8,128)(2,1)}, bf16[4,128,256]{2,1,0:T(8,128)(2,1)}, u32[]{:S(2)}, u32[]{:S(2)}) collective-permute-start(bf16[4,128,256]{2,1,0:T(8,128)(2,1)} %pad_maximum_fusion.refs_0_), channel_id=1, source_target_pairs={{128,0},{192,64},{0,128},{64,192},{129,1},{193,65},{1,129},{65,193... | collective-permute-start | bytes 786440 | tf_op jit(solution)/shard_map/ppermute | solution.py:52
  51.9 10.6 %collective-permute-start.7 = (bf16[4,128,256]{2,1,0:T(8,128)(2,1)}, bf16[4,128,256]{2,1,0:T(8,128)(2,1)}, u32[]{:S(2)}, u32[]{:S(2)}) collective-permute-start(bf16[4,128,256]{2,1,0:T(8,128)(2,1)} %pad_maximum_fusion.refs_0_), channel_id=1, source_target_pairs={{192,0},{0,64},{64,128},{128,192},{193,1},{1,65},{65,129},{129,193... | collective-permute-start | bytes 786440 | tf_op jit(solution)/shard_map/ppermute | solution.py:52
  54.6 8.4 %collective-permute-start.8 = (bf16[4,128,256]{2,1,0:T(8,128)(2,1)}, bf16[4,128,256]{2,1,0:T(8,128)(2,1)}, u32[]{:S(2)}, u32[]{:S(2)}) collective-permute-start(bf16[4,128,256]{2,1,0:T(8,128)(2,1)} %pad_maximum_fusion.refs_0_), channel_id=1, source_target_pairs={{0,1},{1,0},{2,3},{3,2},{4,5},{5,4},{6,7},{7,6},{8,9},{9,8},{10,11... | collective-permute-start | bytes 786440 | tf_op jit(solution)/shard_map/ppermute | solution.py:45
  57.0 10.5 %collective-permute-start.9 = (bf16[4,128,256]{2,1,0:T(8,128)(2,1)}, bf16[4,128,256]{2,1,0:T(8,128)(2,1)}, u32[]{:S(2)}, u32[]{:S(2)}) collective-permute-start(bf16[4,128,256]{2,1,0:T(8,128)(2,1)} %collective-permute-done.5.refs_1_), channel_id=1, source_target_pairs={{0,1},{1,0},{2,3},{3,2},{4,5},{5,4},{6,7},{7,6},{8,9},{9,8},{10,11... | collective-permute-start | bytes 786440 | tf_op jit(solution)/shard_map/ppermute | solution.py:45
  63.6 32.3 %collective-permute-start.16 = (bf16[384,1408]{1,0:T(8,128)(2,1)}, bf16[384,1408]{1,0:T(8,128)(2,1)}, u32[]{:S(2)}, u32[]{:S(2)}) collective-permute-start(bf16[384,1408]{1,0:T(8,128)(2,1)} %param.33), channel_id=1, source_target_pairs={{0,1},{1,0},{2,3},{3,2},{4,5},{5,4},{6,7},{7,6},{8,9},{9,8},{10,11... | collective-permute-start | bytes 3244040 | tf_op jit(solution)/shard_map/ppermute | solution.py:45
  68.2 44.5 %collective-permute-start.15 = (bf16[1408,384]{1,0:T(8,128)(2,1)}, bf16[1408,384]{1,0:T(8,128)(2,1)}, u32[]{:S(2)}, u32[]{:S(2)}) collective-permute-start(bf16[1408,384]{1,0:T(8,128)(2,1)} %param.32), channel_id=1, source_target_pairs={{0,1},{1,0},{2,3},{3,2},{4,5},{5,4},{6,7},{7,6},{8,9},{9,8},{10,11... | collective-permute-start | bytes 3244040 | tf_op jit(solution)/shard_map/ppermute | solution.py:45
  74.7 19.2 %all-to-all-start.1 = ((bf16[4,32,4224]{2,1,0:T(8,128)(2,1)}), bf16[4,32,4224]{2,1,0:T(8,128)(2,1)S(1)}, u32[]{:S(2)}, u32[]{:S(2)}) async-start(bf16[4,32,4224]{2,1,0:T(8,128)(2,1)} %bitcast.53), calls=%async_computation.1 | async-start | bytes 2162688 | tf_op jit(solution)/shard_map/all_to_all | solution.py:41
  94.6 11.5 %collective-permute-start.14 = (bf16[16,4224]{1,0:T(8,128)(2,1)S(1)}, bf16[16,4224]{1,0:T(8,128)(2,1)S(1)}, u32[]{:S(2)}, u32[]{:S(2)}) collective-permute-start(bf16[16,4224]{1,0:T(8,128)(2,1)S(1)} %get-tuple-element.22), channel_id=1, source_target_pairs={{0,8},{8,0},{1,9},{9,1},{2,10},{10,2},{3,11},{11,3},{4,12},{12,4},... | collective-permute-start | bytes 405512 | tf_op jit(solution)/shard_map/ppermute | solution.py:45
  109.3 12.3 %all-to-all-start.2 = ((bf16[8,16,128]{2,1,0:T(8,128)(2,1)}), bf16[8,16,128]{2,1,0:T(8,128)(2,1)S(1)}, u32[]{:S(2)}, u32[]{:S(2)}) async-start(bf16[8,16,128]{2,1,0:T(8,128)(2,1)} %get-tuple-element.23), calls=%async_computation.2 | async-start | bytes 65536 | tf_op jit(solution)/shard_map/all_to_all | solution.py:41
  125.7 17.4 %all-to-all-start.3 = ((bf16[8,16,1408]{2,1,0:T(8,128)(2,1)}), bf16[8,16,1408]{2,1,0:T(8,128)(2,1)S(1)}, u32[]{:S(2)}, u32[]{:S(2)}) async-start(bf16[8,16,1408]{2,1,0:T(8,128)(2,1)} %bitcast.52), calls=%async_computation.3 | async-start | bytes 720896 | tf_op jit(solution)/shard_map/all_to_all | solution.py:41
  130.7 19.8 %collective-permute-start.18 = (bf16[16,4224]{1,0:T(8,128)(2,1)S(1)}, bf16[16,4224]{1,0:T(8,128)(2,1)S(1)}, u32[]{:S(2)}, u32[]{:S(2)}) collective-permute-start(bf16[16,4224]{1,0:T(8,128)(2,1)S(1)} %copy-done.28), channel_id=1, source_target_pairs={{0,8},{8,0},{1,9},{9,1},{2,10},{10,2},{3,11},{11,3},{4,12},{12,4},... | collective-permute-start | bytes 405512 | tf_op jit(solution)/shard_map/ppermute | solution.py:45
  146.1 31.1 %all-to-all-start.4 = ((bf16[8,16,1408]{2,1,0:T(8,128)(2,1)}), bf16[8,16,1408]{2,1,0:T(8,128)(2,1)}, u32[]{:S(2)}, u32[]{:S(2)}) async-start(bf16[8,16,1408]{2,1,0:T(8,128)(2,1)} %get-tuple-element.24), calls=%async_computation.4 | async-start | bytes 720896 | tf_op jit(solution)/shard_map/all_to_all | solution.py:41
  152.9 12.2 %collective-permute-start.19 = (bf16[32,4224]{1,0:T(8,128)(2,1)}, bf16[32,4224]{1,0:T(8,128)(2,1)S(1)}, u32[]{:S(2)}, u32[]{:S(2)}) collective-permute-start(bf16[32,4224]{1,0:T(8,128)(2,1)} %shard_map.200.refs_0_), channel_id=1, source_target_pairs={{2,0},{4,2},{6,4},{0,6},{3,1},{5,3},{7,5},{1,7},{10,8},{12,10},{14... | collective-permute-start | bytes 811016 | tf_op jit(solution)/shard_map/ppermute | solution.py:52
  155.5 9.6 %collective-permute-start.20 = (bf16[32,4224]{1,0:T(8,128)(2,1)}, bf16[32,4224]{1,0:T(8,128)(2,1)S(1)}, u32[]{:S(2)}, u32[]{:S(2)}) collective-permute-start(bf16[32,4224]{1,0:T(8,128)(2,1)} %shard_map.200.refs_0_), channel_id=1, source_target_pairs={{4,0},{6,2},{0,4},{2,6},{5,1},{7,3},{1,5},{3,7},{12,8},{14,10},{8,... | collective-permute-start | bytes 811016 | tf_op jit(solution)/shard_map/ppermute | solution.py:52
  156.0 17.2 %collective-permute-start.21 = (bf16[32,4224]{1,0:T(8,128)(2,1)}, bf16[32,4224]{1,0:T(8,128)(2,1)S(1)}, u32[]{:S(2)}, u32[]{:S(2)}) collective-permute-start(bf16[32,4224]{1,0:T(8,128)(2,1)} %shard_map.200.refs_0_), channel_id=1, source_target_pairs={{6,0},{0,2},{2,4},{4,6},{7,1},{1,3},{3,5},{5,7},{14,8},{8,10},{10,... | collective-permute-start | bytes 811016 | tf_op jit(solution)/shard_map/ppermute | solution.py:52
  173.9 26.2 %collective-permute-start.22 = (bf16[128,4224]{1,0:T(8,128)(2,1)S(1)}, bf16[128,4224]{1,0:T(8,128)(2,1)}, u32[]{:S(2)}, u32[]{:S(2)}) collective-permute-start(bf16[128,4224]{1,0:T(8,128)(2,1)S(1)} %shard_map.201.half_ref), channel_id=1, source_target_pairs={{0,1},{1,0},{2,3},{3,2},{4,5},{5,4},{6,7},{7,6},{8,9},{9,8},{10,11... | collective-permute-start | bytes 3244040 | tf_op jit(solution)/shard_map/ppermute | solution.py:45
  180.7 17.0 %all-to-all-start.5 = ((bf16[8,144,128]{2,1,0:T(8,128)(2,1)}), bf16[8,144,128]{2,1,0:T(8,128)(2,1)S(1)}, u32[]{:S(2)}, u32[]{:S(2)}) async-start(bf16[8,144,128]{2,1,0:T(8,128)(2,1)} %shard_map.199), calls=%async_computation.5 | async-start | bytes 589824 | tf_op jit(solution)/shard_map/all_to_all | solution.py:41
  212.7 19.0 %all-to-all-start.6 = ((bf16[8,128,256]{2,1,0:T(8,128)(2,1)}), bf16[8,128,256]{2,1,0:T(8,128)(2,1)S(1)}, u32[]{:S(2)}, u32[]{:S(2)}) async-start(bf16[8,128,256]{2,1,0:T(8,128)(2,1)} %shard_map.205), calls=%async_computation.6 | async-start | bytes 1048576 | tf_op jit(solution)/shard_map/all_to_all | solution.py:41
  (48 other events, 440.3 us)

commit v4 on v3

--- a/solution.py
+++ b/solution.py
@@ -414,7 +414,7 @@
         10**6,
         2 * MIB,
         [queries[0], keys[0], values[0]],
-        spots,
+        core_scalar,
     )
     mine = exchange(sent, CHIP).reshape(CHIPS * tokens, 4 * HEAD)
     other = swap(mine)
@@ -504,6 +504,16 @@
         limit=16 * MIB,
     )
     unit_other = swap(unit_half)
+
+    gained = final_weight.astype(F32) * gain_rows[:, None]
+    gained16 = gained.astype(BF16)
+    weight_latent = mm(own_weight, gained16)
+    weight_sum = jnp.sum(own_weight.astype(F32), axis=1)
+    weight_latent = weight_latent.astype(BF16)
+    mean_line = jnp.mean(gained, axis=0)[None]
+    sum_line = weight_sum[None]
+    post_line = post_gain[None]
+    head_line = head_weight[None]
 
     embedded = mm(crop_tokens, embed_weight)
     first_root = jnp.sqrt(jnp.mean(embedded * embedded, axis=-1, keepdims=True) + EPSILON)
@@ -519,7 +529,7 @@
         [((CHIPS, share, reward_width), BF16), ((16, PATCH), BF16)],
         10**6,
         MIB,
-        [embedded, added, post_gain[None], head_weight[None]],
+        [embedded, added, post_line, head_line],
         spots,
     )
     slope_half = exchange(slope_copies, ROWS).reshape(half, reward_width)
@@ -540,10 +550,6 @@
     back = swap(both)
     reward = both + back
     reward = reward[half, 0] + reward[half, 1] + reward[half, 2]
-    gained = final_weight.astype(F32) * gain_rows[:, None]
-    gained16 = gained.astype(BF16)
-    weight_latent = mm(own_weight, gained16)
-    weight_sum = jnp.sum(own_weight.astype(F32), axis=1)
     unit_weight, unit_latent, row_inverse = kernel_call(
         unit_body,
         [((rows, HEAD), F32), ((rows, PATCH), F32), ((rows, 1), F32)],
@@ -562,9 +568,9 @@
             back,
             crop[:, None],
             crop[None, :],
-            weight_latent.astype(BF16),
-            jnp.mean(gained, axis=0)[None],
-            weight_sum[None],
+            weight_latent,
+            mean_line,
+            sum_line,
             unit_weight,
             unit_latent,
             row_inverse,

time: 238 us -> 239 us (level)
  the two profiles are of different devices: /device:TPU:69 before, /device:TPU:34 now
where the time goes in v4:
time: 239 us; the launch traced here: 238 us
  waiting for transfers between devices  103 us (43%)
  starting transfers between devices  60.9 us (25%)
  Pallas kernels  35.1 us (15%)
  local copies, waits for them, and re-layouts  16.5 us (7%)
  matrix products  9.88 us (4%)
  other arithmetic  7.59 us (3%)
  between operations  5.63 us (2%)
    all_to_all x7, waiting for transfers between devices, exchange(): return lax.all_to_all(pieces, axis, split_axis=0, concat_axis=0, tiled=True)  81.5 us
    all_to_all x7, starting transfers between devices, exchange(): return lax.all_to_all(pieces, axis, split_axis=0, concat_axis=0, tiled=True)  37.1 us
    pallas_call x14, Pallas kernels, kernel_call(): pl.pallas_call(body, grid=(1,), out_shape=[jax.ShapeDtypeStruct(shape, ki...  35.1 us
    ppermute x9, waiting for transfers between devices, ring_blocks(): lax.ppermute(value, axis, [((i + step) % size, i) for i in range(size)])  13.9 us
    ppermute x9, starting transfers between devices, ring_blocks(): lax.ppermute(value, axis, [((i + step) % size, i) for i in range(size)])  13.2 us
    ppermute x15, starting transfers between devices, swap(): return lax.ppermute(value, axis, [(0, 1), (1, 0)])  10.6 us
    unnamed x84, local copies, waits for them, and re-layouts  10.3 us
    dot_general x7, matrix products, dot(): return lax.dot_general(a, b, (dims, ((), ())), preferred_element_type=F32)  9.88 us
  transfers between devices with their start and end apart: 31, of which 14 were waited for; matrix products, arithmetic and copies ran while one was open for 10% of the time, Pallas kernels for 11%

profile of v4, /device:TPU:34, one launch (start us, length us, event | category | flops | bytes accessed | tf_op | source)
XLA Modules:
  0.0 238.1 jit_solution(4712430037841482247)
XLA Ops:
  3.0 10.3 %all-to-all-start = ((bf16[8,128,512]{2,1,0:T(8,128)(2,1)}), bf16[8,128,512]{2,1,0:T(8,128)(2,1)S(1)}, u32[]{:S(2)}, u32[]{:S(2)}) async-start(bf16[8,128,512]{2,1,0:T(8,128)(2,1)} %shard_map.193), calls=%async_computation | async-start | bytes 2097152 | tf_op jit(solution)/shard_map/all_to_all | solution.py:41
  16.9 28.0 %all-to-all-done = bf16[8,128,512]{2,1,0:T(8,128)(2,1)S(1)} async-done(((bf16[8,128,512]{2,1,0:T(8,128)(2,1)}), bf16[8,128,512]{2,1,0:T(8,128)(2,1)S(1)}, u32[]{:S(2)}, u32[]{:S(2)}) %all-to-all-start) | async-done | bytes 1048608 | tf_op jit(solution)/shard_map/all_to_all | solution.py:41
  56.8 5.6 %collective-permute-done.6.refs_2_ = bf16[4,128,256]{2,1,0:T(8,128)(2,1)} collective-permute-done((bf16[4,128,256]{2,1,0:T(8,128)(2,1)}, bf16[4,128,256]{2,1,0:T(8,128)(2,1)}, u32[]{:S(2)}, u32[]{:S(2)}) %collective-permute-start.6) | collective-permute-done | bytes 262176 | tf_op jit(solution)/shard_map/ppermute | solution.py:52
  70.5 4.6 %shard_map.195 = (bf16[128,4224]{1,0:T(8,128)(2,1)}, bf16[128,4096]{1,0:T(8,128)(2,1)}) custom-call(s32[4]{0:T(128)} %pad_add_fusion.1.index_ref, bf16[256,128]{1,0:T(8,128)(2,1)} %copy-done.6, bf16[256,128]{1,0:T(8,128)(2,1)} %copy-done.30, s32[256,1]{1,0:T(8,128)} %copy-done.19, bf16[4,128,256]{2,1,0:T(8,128)(2,1)} %pad_maximum_fusion.refs_0_, ...), custom_call_target="tpu_custom_call" | custom-call | flops 600000000 | bytes 7340032 | tf_op jit(solution)/shard_map/pallas_call | solution.py:65
  75.1 4.3 %all-to-all-start.1 = ((bf16[4,32,4224]{2,1,0:T(8,128)(2,1)}), bf16[4,32,4224]{2,1,0:T(8,128)(2,1)S(1)}, u32[]{:S(2)}, u32[]{:S(2)}) async-start(bf16[4,32,4224]{2,1,0:T(8,128)(2,1)} %bitcast.52), calls=%async_computation.1 | async-start | bytes 2162688 | tf_op jit(solution)/shard_map/all_to_all | solution.py:41
  80.0 15.2 %all-to-all-done.1.arrived_ref = bf16[4,32,4224]{2,1,0:T(8,128)(2,1)S(1)} async-done(((bf16[4,32,4224]{2,1,0:T(8,128)(2,1)}), bf16[4,32,4224]{2,1,0:T(8,128)(2,1)S(1)}, u32[]{:S(2)}, u32[]{:S(2)}) %all-to-all-start.1) | async-done | bytes 1081376 | tf_op jit(solution)/shard_map/all_to_all | solution.py:41
  100.6 5.9 %collective-permute-done.14.got_ref = bf16[16,4224]{1,0:T(8,128)(2,1)S(1)} collective-permute-done((bf16[16,4224]{1,0:T(8,128)(2,1)S(1)}, bf16[16,4224]{1,0:T(8,128)(2,1)S(1)}, u32[]{:S(2)}, u32[]{:S(2)}) %collective-permute-start.14) | collective-permute-done | bytes 135200 | tf_op jit(solution)/shard_map/ppermute | solution.py:45
  109.6 4.9 %all-to-all-start.2 = ((bf16[8,16,128]{2,1,0:T(8,128)(2,1)}), bf16[8,16,128]{2,1,0:T(8,128)(2,1)S(1)}, u32[]{:S(2)}, u32[]{:S(2)}) async-start(bf16[8,16,128]{2,1,0:T(8,128)(2,1)} %get-tuple-element.23), calls=%async_computation.2 | async-start | bytes 65536 | tf_op jit(solution)/shard_map/all_to_all | solution.py:41
  115.7 9.0 %all-to-all-done.2 = bf16[8,16,128]{2,1,0:T(8,128)(2,1)S(1)} async-done(((bf16[8,16,128]{2,1,0:T(8,128)(2,1)}), bf16[8,16,128]{2,1,0:T(8,128)(2,1)S(1)}, u32[]{:S(2)}, u32[]{:S(2)}) %all-to-all-start.2) | async-done | bytes 32800 | tf_op jit(solution)/shard_map/all_to_all | solution.py:41
  129.3 3.4 %all-to-all-start.3 = ((bf16[8,16,1408]{2,1,0:T(8,128)(2,1)}), bf16[8,16,1408]{2,1,0:T(8,128)(2,1)S(1)}, u32[]{:S(2)}, u32[]{:S(2)}) async-start(bf16[8,16,1408]{2,1,0:T(8,128)(2,1)} %bitcast.26), calls=%async_computation.3 | async-start | bytes 720896 | tf_op jit(solution)/shard_map/all_to_all | solution.py:41
  133.6 5.9 %collective-permute-start.18 = (bf16[16,4224]{1,0:T(8,128)(2,1)S(1)}, bf16[16,4224]{1,0:T(8,128)(2,1)S(1)}, u32[]{:S(2)}, u32[]{:S(2)}) collective-permute-start(bf16[16,4224]{1,0:T(8,128)(2,1)S(1)} %copy-done.27), channel_id=1, source_target_pairs={{0,8},{8,0},{1,9},{9,1},{2,10},{10,2},{3,11},{11,3},{4,12},{12,4},... | collective-permute-start | bytes 405512 | tf_op jit(solution)/shard_map/ppermute | solution.py:45
  141.2 6.7 %all-to-all-done.3.added_ref = bf16[8,16,1408]{2,1,0:T(8,128)(2,1)S(1)} async-done(((bf16[8,16,1408]{2,1,0:T(8,128)(2,1)}), bf16[8,16,1408]{2,1,0:T(8,128)(2,1)S(1)}, u32[]{:S(2)}, u32[]{:S(2)}) %all-to-all-start.3) | async-done | bytes 360480 | tf_op jit(solution)/shard_map/all_to_all | solution.py:41
  150.9 4.2 %all-to-all-start.4 = ((bf16[8,16,1408]{2,1,0:T(8,128)(2,1)}), bf16[8,16,1408]{2,1,0:T(8,128)(2,1)}, u32[]{:S(2)}, u32[]{:S(2)}) async-start(bf16[8,16,1408]{2,1,0:T(8,128)(2,1)} %get-tuple-element.24), calls=%async_computation.4 | async-start | bytes 720896 | tf_op jit(solution)/shard_map/all_to_all | solution.py:41
  157.7 3.1 %collective-permute-start.19 = (bf16[32,4224]{1,0:T(8,128)(2,1)}, bf16[32,4224]{1,0:T(8,128)(2,1)S(1)}, u32[]{:S(2)}, u32[]{:S(2)}) collective-permute-start(bf16[32,4224]{1,0:T(8,128)(2,1)} %shard_map.200.refs_0_), channel_id=1, source_target_pairs={{2,0},{4,2},{6,4},{0,6},{3,1},{5,3},{7,5},{1,7},{10,8},{12,10},{14... | collective-permute-start | bytes 811016 | tf_op jit(solution)/shard_map/ppermute | solution.py:52
  165.3 3.7 %collective-permute-done.19.refs_1_ = bf16[32,4224]{1,0:T(8,128)(2,1)S(1)} collective-permute-done((bf16[32,4224]{1,0:T(8,128)(2,1)}, bf16[32,4224]{1,0:T(8,128)(2,1)S(1)}, u32[]{:S(2)}, u32[]{:S(2)}) %collective-permute-start.19) | collective-permute-done | bytes 270368 | tf_op jit(solution)/shard_map/ppermute | solution.py:52
  169.6 2.8 %collective-permute-done.21.refs_3_ = bf16[32,4224]{1,0:T(8,128)(2,1)S(1)} collective-permute-done((bf16[32,4224]{1,0:T(8,128)(2,1)}, bf16[32,4224]{1,0:T(8,128)(2,1)S(1)}, u32[]{:S(2)}, u32[]{:S(2)}) %collective-permute-start.21) | collective-permute-done | bytes 270368 | tf_op jit(solution)/shard_map/ppermute | solution.py:52
  174.8 3.5 %shard_map.199 = bf16[8,144,128]{2,1,0:T(8,128)(2,1)} custom-call(bf16[128,1408]{1,0:T(8,128)(2,1)} %bitcast.27.refs_0_, bf16[768,1408]{1,0:T(8,128)(2,1)} %constant_dynamic-update-slice_fusion.2.refs_1_, f32[128,768]{1,0:T(8,128)} %copy-done.20, bf16[128,768]{1,0:T(8,128)(2,1)} %convolution_convert_fusion.1.refs_3_, f32[128,128]{1,0:T(8,128)} %fusion.11.refs_4_, ...), custom_call_target="tpu_custom_call" | custom-call | flops 300000000 | bytes 4194304 | tf_op jit(solution)/shard_map/pallas_call | solution.py:65
  178.3 6.4 %all-to-all-start.5 = ((bf16[8,144,128]{2,1,0:T(8,128)(2,1)}), bf16[8,144,128]{2,1,0:T(8,128)(2,1)}, u32[]{:S(2)}, u32[]{:S(2)}) async-start(bf16[8,144,128]{2,1,0:T(8,128)(2,1)} %shard_map.199), calls=%async_computation.5 | async-start | bytes 589824 | tf_op jit(solution)/shard_map/all_to_all | solution.py:41
  187.0 13.2 %all-to-all-done.5 = bf16[8,144,128]{2,1,0:T(8,128)(2,1)} async-done(((bf16[8,144,128]{2,1,0:T(8,128)(2,1)}), bf16[8,144,128]{2,1,0:T(8,128)(2,1)}, u32[]{:S(2)}, u32[]{:S(2)}) %all-to-all-start.5) | async-done | bytes 294944 | tf_op jit(solution)/shard_map/all_to_all | solution.py:41
  202.3 4.2 %shard_map.202 = (f32[256,128]{1,0:T(8,128)}, f32[256,128]{1,0:T(8,128)}, f32[256,1]{1,0:T(8,128)}) custom-call(s32[5]{0:T(128)} %copy-done.9, bf16[128,4224]{1,0:T(8,128)(2,1)} %copy-done, bf16[128,4224]{1,0:T(8,128)(2,1)} %collective-permute-done.22.other_ref, bf16[128,4096]{1,0:T(8,128)(2,1)} %get-tuple-element.27.head_ref, bf16[4096,128]{1,0:T(8,128)(2,1)} %copy-done.15), custom_call_target="tpu_custom_call" | custom-call | flops 600000000 | bytes 4194304 | tf_op jit(solution)/shard_map/pallas_call | solution.py:65
  207.1 4.4 %shard_map.203 = (bf16[256,128]{1,0:T(8,128)(2,1)}, bf16[256,128]{1,0:T(8,128)(2,1)}) custom-call(f32[4]{0:T(128)} %pad_maximum_fusion.1.consts_ref, f32[144,128]{1,0:T(8,128)} %copy-done.23, f32[144,128]{1,0:T(8,128)} %copy-done.25, s32[256,1]{1,0:T(8,128)} %copy-done.19, s32[1,256]{1,0:T(1,128)} %crop_row_ref.1, ...), custom_call_target="tpu_custom_call" | custom-call | flops 600000000 | bytes 5242880 | tf_op jit(solution)/shard_map/pallas_call | solution.py:65
  215.1 3.5 %all-to-all-start.6 = ((bf16[8,128,256]{2,1,0:T(8,128)(2,1)}), bf16[8,128,256]{2,1,0:T(8,128)(2,1)S(1)}, u32[]{:S(2)}, u32[]{:S(2)}) async-start(bf16[8,128,256]{2,1,0:T(8,128)(2,1)} %shard_map.205), calls=%async_computation.6 | async-start | bytes 1048576 | tf_op jit(solution)/shard_map/all_to_all | solution.py:41
  222.1 4.5 %shard_map.204 = bf16[128,4096]{1,0:T(8,128)(2,1)} custom-call(s32[5]{0:T(128)} %copy-done.9, bf16[128,4224]{1,0:T(8,128)(2,1)} %copy-done, bf16[128,4224]{1,0:T(8,128)(2,1)} %collective-permute-done.22.other_ref, s32[1,256]{1,0:T(1,128)} %copy-done.11, bf16[256,128]{1,0:T(8,128)(2,1)} %get-tuple-element.33.noise_ref, bf16[4096,128]{1,0:T(8,128)(2,1)} %weight_ref.3, ...), custom_call_target="tpu_custom_call" | custom-call | flops 600000000 | bytes 5242880 | tf_op jit(solution)/shard_map/pallas_call | solution.py:65
  226.6 9.5 %all-to-all-done.6.home_ref = bf16[8,128,256]{2,1,0:T(8,128)(2,1)S(1)} async-done(((bf16[8,128,256]{2,1,0:T(8,128)(2,1)}), bf16[8,128,256]{2,1,0:T(8,128)(2,1)S(1)}, u32[]{:S(2)}, u32[]{:S(2)}) %all-to-all-start.6) | async-done | bytes 524320 | tf_op jit(solution)/shard_map/all_to_all | solution.py:41
  (166 shorter events, 65.7 us)
Async XLA Ops:
  3.0 41.9 %all-to-all-start = ((bf16[8,128,512]{2,1,0:T(8,128)(2,1)}), bf16[8,128,512]{2,1,0:T(8,128)(2,1)S(1)}, u32[]{:S(2)}, u32[]{:S(2)}) async-start(bf16[8,128,512]{2,1,0:T(8,128)(2,1)} %shard_map.193), calls=%async_computation | async-start | bytes 2097152 | tf_op jit(solution)/shard_map/all_to_all | solution.py:41
  13.4 32.8 %collective-permute-start.4 = (bf16[128,256]{1,0:T(8,128)(2,1)S(1)}, bf16[128,256]{1,0:T(8,128)(2,1)S(1)}, u32[]{:S(2)}, u32[]{:S(2)}) collective-permute-start(bf16[128,256]{1,0:T(8,128)(2,1)S(1)} %copy-done.31), channel_id=1, source_target_pairs={{48,0},{0,16},{16,32},{32,48},{49,1},{1,17},{17,33},{33,49},{50,2}... | collective-permute-start | bytes 196616 | tf_op jit(solution)/shard_map/ppermute | solution.py:52
  14.4 32.1 %collective-permute-start.3 = (bf16[128,256]{1,0:T(8,128)(2,1)S(1)}, bf16[128,256]{1,0:T(8,128)(2,1)S(1)}, u32[]{:S(2)}, u32[]{:S(2)}) collective-permute-start(bf16[128,256]{1,0:T(8,128)(2,1)S(1)} %copy-done.31), channel_id=1, source_target_pairs={{32,0},{48,16},{0,32},{16,48},{33,1},{49,17},{1,33},{17,49},{34,2}... | collective-permute-start | bytes 196616 | tf_op jit(solution)/shard_map/ppermute | solution.py:52
  16.8 29.8 %collective-permute-start.2 = (bf16[128,256]{1,0:T(8,128)(2,1)S(1)}, bf16[128,256]{1,0:T(8,128)(2,1)S(1)}, u32[]{:S(2)}, u32[]{:S(2)}) collective-permute-start(bf16[128,256]{1,0:T(8,128)(2,1)S(1)} %copy-done.31), channel_id=1, source_target_pairs={{16,0},{32,16},{48,32},{0,48},{17,1},{33,17},{49,33},{1,49},{18,2}... | collective-permute-start | bytes 196616 | tf_op jit(solution)/shard_map/ppermute | solution.py:52
  16.9 52.8 %collective-permute-start.12 = (bf16[128,4096]{1,0:T(8,128)(2,1)}, bf16[128,4096]{1,0:T(8,128)(2,1)}, u32[]{:S(2)}, u32[]{:S(2)}) collective-permute-start(bf16[128,4096]{1,0:T(8,128)(2,1)} %bitcast.22.refs_8_), channel_id=1, source_target_pairs={{0,1},{1,0},{2,3},{3,2},{4,5},{5,4},{6,7},{7,6},{8,9},{9,8},{10,11... | collective-permute-start | bytes 3145736 | tf_op jit(solution)/shard_map/ppermute | solution.py:45
  44.9 19.8 %collective-permute-start = (bf16[1024,512]{1,0:T(8,128)(2,1)S(1)}, bf16[1024,512]{1,0:T(8,128)(2,1)S(1)}, u32[]{:S(2)}, u32[]{:S(2)}) collective-permute-start(bf16[1024,512]{1,0:T(8,128)(2,1)S(1)} %bitcast.49), channel_id=1, source_target_pairs={{0,1},{1,0},{2,3},{3,2},{4,5},{5,4},{6,7},{7,6},{8,9},{9,8},{10,11... | collective-permute-start | bytes 3145736 | tf_op jit(solution)/shard_map/ppermute | solution.py:45
  47.3 8.6 %collective-permute-start.5 = (bf16[4,128,256]{2,1,0:T(8,128)(2,1)}, bf16[4,128,256]{2,1,0:T(8,128)(2,1)}, u32[]{:S(2)}, u32[]{:S(2)}) collective-permute-start(bf16[4,128,256]{2,1,0:T(8,128)(2,1)} %pad_maximum_fusion.refs_0_), channel_id=1, source_target_pairs={{64,0},{128,64},{192,128},{0,192},{65,1},{129,65},{193,129},{1,193... | collective-permute-start | bytes 786440 | tf_op jit(solution)/shard_map/ppermute | solution.py:52
  47.8 14.6 %collective-permute-start.6 = (bf16[4,128,256]{2,1,0:T(8,128)(2,1)}, bf16[4,128,256]{2,1,0:T(8,128)(2,1)}, u32[]{:S(2)}, u32[]{:S(2)}) collective-permute-start(bf16[4,128,256]{2,1,0:T(8,128)(2,1)} %pad_maximum_fusion.refs_0_), channel_id=1, source_target_pairs={{128,0},{192,64},{0,128},{64,192},{129,1},{193,65},{1,129},{65,193... | collective-permute-start | bytes 786440 | tf_op jit(solution)/shard_map/ppermute | solution.py:52
  52.9 10.5 %collective-permute-start.7 = (bf16[4,128,256]{2,1,0:T(8,128)(2,1)}, bf16[4,128,256]{2,1,0:T(8,128)(2,1)}, u32[]{:S(2)}, u32[]{:S(2)}) collective-permute-start(bf16[4,128,256]{2,1,0:T(8,128)(2,1)} %pad_maximum_fusion.refs_0_), channel_id=1, source_target_pairs={{192,0},{0,64},{64,128},{128,192},{193,1},{1,65},{65,129},{129,193... | collective-permute-start | bytes 786440 | tf_op jit(solution)/shard_map/ppermute | solution.py:52
  55.9 8.1 %collective-permute-start.8 = (bf16[4,128,256]{2,1,0:T(8,128)(2,1)}, bf16[4,128,256]{2,1,0:T(8,128)(2,1)}, u32[]{:S(2)}, u32[]{:S(2)}) collective-permute-start(bf16[4,128,256]{2,1,0:T(8,128)(2,1)} %pad_maximum_fusion.refs_0_), channel_id=1, source_target_pairs={{0,1},{1,0},{2,3},{3,2},{4,5},{5,4},{6,7},{7,6},{8,9},{9,8},{10,11... | collective-permute-start | bytes 786440 | tf_op jit(solution)/shard_map/ppermute | solution.py:45
  64.8 33.5 %collective-permute-start.16 = (bf16[384,1408]{1,0:T(8,128)(2,1)S(1)}, bf16[384,1408]{1,0:T(8,128)(2,1)}, u32[]{:S(2)}, u32[]{:S(2)}) collective-permute-start(bf16[384,1408]{1,0:T(8,128)(2,1)S(1)} %copy-done.22), channel_id=1, source_target_pairs={{0,1},{1,0},{2,3},{3,2},{4,5},{5,4},{6,7},{7,6},{8,9},{9,8},{10,11... | collective-permute-start | bytes 3244040 | tf_op jit(solution)/shard_map/ppermute | solution.py:45
  69.3 45.2 %collective-permute-start.15 = (bf16[1408,384]{1,0:T(8,128)(2,1)}, bf16[1408,384]{1,0:T(8,128)(2,1)S(1)}, u32[]{:S(2)}, u32[]{:S(2)}) collective-permute-start(bf16[1408,384]{1,0:T(8,128)(2,1)} %param.32), channel_id=1, source_target_pairs={{0,1},{1,0},{2,3},{3,2},{4,5},{5,4},{6,7},{7,6},{8,9},{9,8},{10,11... | collective-permute-start | bytes 3244040 | tf_op jit(solution)/shard_map/ppermute | solution.py:45
  75.1 20.0 %all-to-all-start.1 = ((bf16[4,32,4224]{2,1,0:T(8,128)(2,1)}), bf16[4,32,4224]{2,1,0:T(8,128)(2,1)S(1)}, u32[]{:S(2)}, u32[]{:S(2)}) async-start(bf16[4,32,4224]{2,1,0:T(8,128)(2,1)} %bitcast.52), calls=%async_computation.1 | async-start | bytes 2162688 | tf_op jit(solution)/shard_map/all_to_all | solution.py:41
  96.5 9.9 %collective-permute-start.14 = (bf16[16,4224]{1,0:T(8,128)(2,1)S(1)}, bf16[16,4224]{1,0:T(8,128)(2,1)S(1)}, u32[]{:S(2)}, u32[]{:S(2)}) collective-permute-start(bf16[16,4224]{1,0:T(8,128)(2,1)S(1)} %get-tuple-element.22), channel_id=1, source_target_pairs={{0,8},{8,0},{1,9},{9,1},{2,10},{10,2},{3,11},{11,3},{4,12},{12,4},... | collective-permute-start | bytes 405512 | tf_op jit(solution)/shard_map/ppermute | solution.py:45
  109.6 15.1 %all-to-all-start.2 = ((bf16[8,16,128]{2,1,0:T(8,128)(2,1)}), bf16[8,16,128]{2,1,0:T(8,128)(2,1)S(1)}, u32[]{:S(2)}, u32[]{:S(2)}) async-start(bf16[8,16,128]{2,1,0:T(8,128)(2,1)} %get-tuple-element.23), calls=%async_computation.2 | async-start | bytes 65536 | tf_op jit(solution)/shard_map/all_to_all | solution.py:41
  129.3 18.6 %all-to-all-start.3 = ((bf16[8,16,1408]{2,1,0:T(8,128)(2,1)}), bf16[8,16,1408]{2,1,0:T(8,128)(2,1)S(1)}, u32[]{:S(2)}, u32[]{:S(2)}) async-start(bf16[8,16,1408]{2,1,0:T(8,128)(2,1)} %bitcast.26), calls=%async_computation.3 | async-start | bytes 720896 | tf_op jit(solution)/shard_map/all_to_all | solution.py:41
  133.6 21.7 %collective-permute-start.18 = (bf16[16,4224]{1,0:T(8,128)(2,1)S(1)}, bf16[16,4224]{1,0:T(8,128)(2,1)S(1)}, u32[]{:S(2)}, u32[]{:S(2)}) collective-permute-start(bf16[16,4224]{1,0:T(8,128)(2,1)S(1)} %copy-done.27), channel_id=1, source_target_pairs={{0,8},{8,0},{1,9},{9,1},{2,10},{10,2},{3,11},{11,3},{4,12},{12,4},... | collective-permute-start | bytes 405512 | tf_op jit(solution)/shard_map/ppermute | solution.py:45
  150.9 23.9 %all-to-all-start.4 = ((bf16[8,16,1408]{2,1,0:T(8,128)(2,1)}), bf16[8,16,1408]{2,1,0:T(8,128)(2,1)}, u32[]{:S(2)}, u32[]{:S(2)}) async-start(bf16[8,16,1408]{2,1,0:T(8,128)(2,1)} %get-tuple-element.24), calls=%async_computation.4 | async-start | bytes 720896 | tf_op jit(solution)/shard_map/all_to_all | solution.py:41
  157.7 11.3 %collective-permute-start.19 = (bf16[32,4224]{1,0:T(8,128)(2,1)}, bf16[32,4224]{1,0:T(8,128)(2,1)S(1)}, u32[]{:S(2)}, u32[]{:S(2)}) collective-permute-start(bf16[32,4224]{1,0:T(8,128)(2,1)} %shard_map.200.refs_0_), channel_id=1, source_target_pairs={{2,0},{4,2},{6,4},{0,6},{3,1},{5,3},{7,5},{1,7},{10,8},{12,10},{14... | collective-permute-start | bytes 811016 | tf_op jit(solution)/shard_map/ppermute | solution.py:52
  160.8 8.8 %collective-permute-start.20 = (bf16[32,4224]{1,0:T(8,128)(2,1)}, bf16[32,4224]{1,0:T(8,128)(2,1)S(1)}, u32[]{:S(2)}, u32[]{:S(2)}) collective-permute-start(bf16[32,4224]{1,0:T(8,128)(2,1)} %shard_map.200.refs_0_), channel_id=1, source_target_pairs={{4,0},{6,2},{0,4},{2,6},{5,1},{7,3},{1,5},{3,7},{12,8},{14,10},{8,... | collective-permute-start | bytes 811016 | tf_op jit(solution)/shard_map/ppermute | solution.py:52
  161.6 10.7 %collective-permute-start.21 = (bf16[32,4224]{1,0:T(8,128)(2,1)}, bf16[32,4224]{1,0:T(8,128)(2,1)S(1)}, u32[]{:S(2)}, u32[]{:S(2)}) collective-permute-start(bf16[32,4224]{1,0:T(8,128)(2,1)} %shard_map.200.refs_0_), channel_id=1, source_target_pairs={{6,0},{0,2},{2,4},{4,6},{7,1},{1,3},{3,5},{5,7},{14,8},{8,10},{10,... | collective-permute-start | bytes 811016 | tf_op jit(solution)/shard_map/ppermute | solution.py:52
  173.0 29.3 %collective-permute-start.22 = (bf16[128,4224]{1,0:T(8,128)(2,1)S(1)}, bf16[128,4224]{1,0:T(8,128)(2,1)}, u32[]{:S(2)}, u32[]{:S(2)}) collective-permute-start(bf16[128,4224]{1,0:T(8,128)(2,1)S(1)} %shard_map.201.half_ref), channel_id=1, source_target_pairs={{0,1},{1,0},{2,3},{3,2},{4,5},{5,4},{6,7},{7,6},{8,9},{9,8},{10,11... | collective-permute-start | bytes 3244040 | tf_op jit(solution)/shard_map/ppermute | solution.py:45
  178.3 21.9 %all-to-all-start.5 = ((bf16[8,144,128]{2,1,0:T(8,128)(2,1)}), bf16[8,144,128]{2,1,0:T(8,128)(2,1)}, u32[]{:S(2)}, u32[]{:S(2)}) async-start(bf16[8,144,128]{2,1,0:T(8,128)(2,1)} %shard_map.199), calls=%async_computation.5 | async-start | bytes 589824 | tf_op jit(solution)/shard_map/all_to_all | solution.py:41
  215.1 21.0 %all-to-all-start.6 = ((bf16[8,128,256]{2,1,0:T(8,128)(2,1)}), bf16[8,128,256]{2,1,0:T(8,128)(2,1)S(1)}, u32[]{:S(2)}, u32[]{:S(2)}) async-start(bf16[8,128,256]{2,1,0:T(8,128)(2,1)} %shard_map.205), calls=%async_computation.6 | async-start | bytes 1048576 | tf_op jit(solution)/shard_map/all_to_all | solution.py:41
  (48 other events, 503.3 us)
